TPU v7x, 256 devices: a whole 4x4x8 slice. The times are simulated.
256 devices in a mesh: row: 32 (over y, x, core), col: 8 (over z).
Axes of the slice: x: 4, y: 4, z: 8, core: 2. Of those that a mesh axis runs over, the one named last changes fastest.
Arguments:
- sources: float32 [3, 4096, 8192], P(None, 'row', 'col'), may hold values from -32 to 32
- labels: int32 [4096, 8192], P('row', 'col'), may hold values from 0 to 2
Outputs:
- blended: float32 [4096, 8192], P('row', 'col')
- overview_fine: float32 [2048, 4096], P('row', 'col')
- overview_mid: float32 [1024, 2048], P(None, 'col')
- overview_coarse: float32 [512, 1024], P(None, 'col')
All inputs are finite; a program needn't handle non-finite values.
Results may differ from a plain program's by a relative error of at most 0.0001.
Values sent between devices are 32-bit elements; how exact they have to be, the bound alone decides.
No kernel may reach another device: no remote copies, remote signals or barrier semaphores. Data moves between devices by JAX's collectives and lax.ppermute only.
A program may use at most 64 MiB of HBM per device.

v0:
```python
import jax
import jax.numpy as jnp
from jax import lax
from jax.sharding import Mesh
from jax.sharding import PartitionSpec as P

ITERS = 3
ROW_COL = ("row_0", "row_1", "row_2", "col")
ROW = ("row_0", "row_1", "row_2")


def padded_2(value, sides, width):
    edges = {}
    for axis, dim in sides:
        devices, length = (lax.axis_size(axis), value.shape[dim])
        up = [(i, (i + 1) % devices) for i in range(devices - 1)]
        last = lax.slice_in_dim(value, length - width, length, axis=dim)
        leading = lax.slice_in_dim(value, 0, width, axis=dim)
        edges[dim] = (
            lax.ppermute(last, axis, up),
            lax.ppermute(leading, axis, [(b, a) for a, b in up]),
        )
    done = []
    for _, dim in sides:
        low, high = edges[dim]
        around = [(width, width) if d in done else (0, 0) for d in range(value.ndim)]
        value = jnp.concatenate([jnp.pad(low, around), value, jnp.pad(high, around)], axis=dim)
        done.append(dim)
    return value


def by_axis(value, axes):
    for axis in axes:
        value = lax.psum(value, axis)
    return value


def from_everyone(value, axis):
    copies = jnp.broadcast_to(value, (lax.axis_size(axis), *value.shape))
    return lax.all_to_all(copies, axis, split_axis=0, concat_axis=0, tiled=True)


def laid_out(tiles, dim):
    tiles = jnp.moveaxis(tiles, 0, dim)
    dims = tiles.shape
    return tiles.reshape(*dims[:dim], dims[dim] * dims[dim + 1], *dims[dim + 2 :])


def gathered_copies(value, axis, dim):
    tiles = from_everyone(value, axis)
    return laid_out(tiles, dim)


def stencil_padded(padded, values):
    beside = padded[2:, 1:-1] + padded[:-2, 1:-1]
    beside = beside + padded[1:-1, 2:] + padded[1:-1, :-2]
    return 4.0 * values - beside


def apply_stencil(values):
    padded = padded_2(values, ((ROW, 0), ("col", 1)), 1)
    return stencil_padded(padded, values)


def average_pool(values):
    return 0.25 * (
        values[0::2, 0::2] + values[1::2, 0::2] + values[0::2, 1::2] + values[1::2, 1::2]
    )


def two_products(residual, applied):
    return (
        by_axis(jnp.sum(residual * residual), ROW_COL),
        by_axis(jnp.sum(residual * applied), ROW_COL),
    )


def per_device(sources, labels):
    source_pad = padded_2(sources, ((ROW, 1), ("col", 2)), 1)
    right_side = jnp.zeros(labels.shape, jnp.float32)
    for channel in range(sources.shape[0]):
        stencil_term = stencil_padded(source_pad[channel], sources[channel])
        right_side = right_side + jnp.where(labels == channel, stencil_term, jnp.float32(0.0))
    blended = jnp.zeros(labels.shape, jnp.float32)
    residual = right_side
    applied = apply_stencil(residual)
    norm_now, product = two_products(residual, applied)
    step_size = norm_now / product
    direction = residual
    along = applied
    for iteration in range(ITERS):
        blended = blended + step_size * direction
        residual = residual - step_size * along
        if iteration + 1 < ITERS:
            applied = apply_stencil(residual)
            norm_next, product = two_products(residual, applied)
            beta_ratio = norm_next / norm_now
            step_size = norm_next / (product - beta_ratio * norm_next / step_size)
            direction = residual + beta_ratio * direction
            along = applied + beta_ratio * along
            norm_now = norm_next
    overview_fine = average_pool(blended)
    overview_mid = gathered_copies(average_pool(overview_fine), ROW, 0)
    overview_coarse = average_pool(overview_mid)
    return (blended, overview_fine, overview_mid, overview_coarse)


def solution(mesh):
    finer = Mesh(
        mesh.devices.reshape(4, 4, 2, mesh.shape["col"]), ("row_0", "row_1", "row_2", "col")
    )
    return jax.shard_map(
        per_device,
        mesh=finer,
        in_specs=(P(None, ROW, "col"), P(ROW, "col")),
        out_specs=(P(ROW, "col"), P(ROW, "col"), P(None, "col"), P(None, "col")),
        check_vma=False,
    )
```

profile of v0, /device:TPU:1, one launch (start us, length us, event | category | flops | bytes accessed | tf_op | source)
XLA Modules:
  0.0 306.4 jit_solution(11265011908296794969)
XLA Ops:
  1.7 4.5 %collective-permute-start.1 = (f32[3,1,1024]{2,1,0:T(1,128)S(1)}, f32[3,1,1024]{2,1,0:T(1,128)S(1)}, u32[]{:S(2)}, u32[]{:S(2)}) collective-permute-start(f32[3,1,1024]{2,1,0:T(1,128)S(1)} %get-tuple-element.39), channel_id=1, source_target_pairs={{0,8},{8,16},{16,24},{24,32},{32,40},{40,48},{48,56},{56,64},{64,7... | collective-permute-start | bytes 36872 | tf_op jit(solution)/shard_map/ppermute | solution.py:20
  6.2 1.9 collective-permute-start.2
  9.3 1.3 collective-permute-start.3
  10.6 4.2 %collective-permute-start = (f32[3,128,1]{2,1,0:T(8,128)S(1)}, f32[3,128,1]{2,1,0:T(8,128)S(1)}, u32[]{:S(2)}, u32[]{:S(2)}) collective-permute-start(f32[3,128,1]{2,1,0:T(8,128)S(1)} %get-tuple-element.38), channel_id=1, source_target_pairs={{0,1},{1,2},{2,3},{3,4},{4,5},{5,6},{6,7},{8,9},{9,10},{10,11},{11... | collective-permute-start | bytes 4616 | tf_op jit(solution)/shard_map/ppermute | solution.py:20
  14.8 2.9 collective-permute-done.3
  17.7 1.8 collective-permute-done
  19.5 1.4 pad_maximum_fusion
  20.9 2.8 concatenate.55
  23.7 1.6 slice_bitcast_fusion.2
  25.4 1.4 fusion.22
  26.8 3.4 %collective-permute-start.5 = (f32[1,1024]{1,0:T(1,128)S(1)}, f32[1,1024]{1,0:T(1,128)S(1)}, u32[]{:S(2)}, u32[]{:S(2)}) collective-permute-start(f32[1,1024]{1,0:T(1,128)S(1)} %get-tuple-element.51), channel_id=1, source_target_pairs={{0,8},{8,16},{16,24},{24,32},{32,40},{40,48},{48,56},{56,64},{64,7... | collective-permute-start | bytes 12296 | tf_op jit(solution)/shard_map/ppermute | solution.py:20
  30.2 1.9 collective-permute-start.4
  32.2 1.3 collective-permute-start.6
  33.5 4.7 %collective-permute-start.7 = (f32[128,1]{1,0:T(8,128)S(1)}, f32[128,1]{1,0:T(8,128)S(1)}, u32[]{:S(2)}, u32[]{:S(2)}) collective-permute-start(f32[128,1]{1,0:T(8,128)S(1)} %get-tuple-element.50), channel_id=1, source_target_pairs={{0,1},{1,2},{2,3},{3,4},{4,5},{5,6},{6,7},{8,9},{9,10},{10,11},{11... | collective-permute-start | bytes 1544 | tf_op jit(solution)/shard_map/ppermute | solution.py:20
  38.3 1.3 collective-permute-done.7
  40.6 9.4 %all-reduce.16 = (f32[]{:T(128)}, f32[]{:T(128)}) all-reduce(f32[]{:T(128)} %get-tuple-element.9, f32[]{:T(128)} %get-tuple-element.8), channel_id=1, replica_groups=mesh['row_0'=4,'row_1'=4,'row_2'=2,'col'=8] {'row_0'}, use_global_device_ids=true, to_apply=%region_1.2 | all-reduce | flops 2 | bytes 16 | tf_op jit(solution)/shard_map/psum | solution.py:34
  50.0 9.3 %all-reduce.13 = (f32[]{:T(128)}, f32[]{:T(128)}) all-reduce(f32[]{:T(128)} %get-tuple-element.26, f32[]{:T(128)} %get-tuple-element.27), channel_id=1, replica_groups=mesh['row_0'=4,'row_1'=4,'row_2'=2,'col'=8] {'row_1'}, use_global_device_ids=true, to_apply=%region_2.3 | all-reduce | flops 2 | bytes 16 | tf_op jit(solution)/shard_map/psum | solution.py:34
  59.3 8.5 %all-reduce.19 = (f32[]{:T(128)}, f32[]{:T(128)}) all-reduce(f32[]{:T(128)} %get-tuple-element.20, f32[]{:T(128)} %get-tuple-element.21), channel_id=1, replica_groups=mesh['row_0'=4,'row_1'=4,'row_2'=2,'col'=8] {'row_2'}, use_global_device_ids=true, to_apply=%region_3.4 | all-reduce | flops 2 | bytes 16 | tf_op jit(solution)/shard_map/psum | solution.py:34
  67.8 19.2 %all-reduce.10 = (f32[]{:T(128)}, f32[]{:T(128)}) all-reduce(f32[]{:T(128)} %get-tuple-element.32, f32[]{:T(128)} %get-tuple-element.33), channel_id=1, replica_groups=mesh['row_0'=4,'row_1'=4,'row_2'=2,'col'=8] {'col'}, use_global_device_ids=true, to_apply=%region_4.5 | all-reduce | flops 2 | bytes 16 | tf_op jit(solution)/shard_map/psum | solution.py:34
  88.7 7.6 %collective-permute-start.9 = (f32[1,1024]{1,0:T(1,128)S(1)}, f32[1,1024]{1,0:T(1,128)S(1)}, u32[]{:S(2)}, u32[]{:S(2)}) collective-permute-start(f32[1,1024]{1,0:T(1,128)S(1)} %get-tuple-element.47), channel_id=1, source_target_pairs={{0,8},{8,16},{16,24},{24,32},{32,40},{40,48},{48,56},{56,64},{64,7... | collective-permute-start | bytes 12296 | tf_op jit(solution)/shard_map/ppermute | solution.py:20
  96.4 1.9 collective-permute-start.8
  98.4 1.3 collective-permute-start.10
  99.7 4.0 %collective-permute-start.11 = (f32[128,1]{1,0:T(8,128)S(1)}, f32[128,1]{1,0:T(8,128)S(1)}, u32[]{:S(2)}, u32[]{:S(2)}) collective-permute-start(f32[128,1]{1,0:T(8,128)S(1)} %get-tuple-element.46), channel_id=1, source_target_pairs={{0,1},{1,2},{2,3},{3,4},{4,5},{5,6},{6,7},{8,9},{9,10},{10,11},{11... | collective-permute-start | bytes 1544 | tf_op jit(solution)/shard_map/ppermute | solution.py:20
  103.7 1.3 collective-permute-done.11
  106.0 6.6 %all-reduce.15 = (f32[]{:T(128)}, f32[]{:T(128)}) all-reduce(f32[]{:T(128)} %get-tuple-element.7, f32[]{:T(128)} %get-tuple-element.6), channel_id=1, replica_groups=mesh['row_0'=4,'row_1'=4,'row_2'=2,'col'=8] {'row_0'}, use_global_device_ids=true, to_apply=%region_11.12 | all-reduce | flops 2 | bytes 16 | tf_op jit(solution)/shard_map/psum | solution.py:34
  112.6 7.5 %all-reduce.12 = (f32[]{:T(128)}, f32[]{:T(128)}) all-reduce(f32[]{:T(128)} %get-tuple-element.24, f32[]{:T(128)} %get-tuple-element.25), channel_id=1, replica_groups=mesh['row_0'=4,'row_1'=4,'row_2'=2,'col'=8] {'row_1'}, use_global_device_ids=true, to_apply=%region_12.13 | all-reduce | flops 2 | bytes 16 | tf_op jit(solution)/shard_map/psum | solution.py:34
  120.1 8.6 %all-reduce.18 = (f32[]{:T(128)}, f32[]{:T(128)}) all-reduce(f32[]{:T(128)} %get-tuple-element.18, f32[]{:T(128)} %get-tuple-element.19), channel_id=1, replica_groups=mesh['row_0'=4,'row_1'=4,'row_2'=2,'col'=8] {'row_2'}, use_global_device_ids=true, to_apply=%region_13.14 | all-reduce | flops 2 | bytes 16 | tf_op jit(solution)/shard_map/psum | solution.py:34
  128.7 13.4 %all-reduce.9 = (f32[]{:T(128)}, f32[]{:T(128)}) all-reduce(f32[]{:T(128)} %get-tuple-element.30, f32[]{:T(128)} %get-tuple-element.31), channel_id=1, replica_groups=mesh['row_0'=4,'row_1'=4,'row_2'=2,'col'=8] {'col'}, use_global_device_ids=true, to_apply=%region_14.15 | all-reduce | flops 2 | bytes 16 | tf_op jit(solution)/shard_map/psum | solution.py:34
  147.4 7.5 %collective-permute-start.13 = (f32[1,1024]{1,0:T(1,128)S(1)}, f32[1,1024]{1,0:T(1,128)S(1)}, u32[]{:S(2)}, u32[]{:S(2)}) collective-permute-start(f32[1,1024]{1,0:T(1,128)S(1)} %get-tuple-element.43), channel_id=1, source_target_pairs={{0,8},{8,16},{16,24},{24,32},{32,40},{40,48},{48,56},{56,64},{64,7... | collective-permute-start | bytes 12296 | tf_op jit(solution)/shard_map/ppermute | solution.py:20
  154.8 1.9 collective-permute-start.12
  156.8 1.3 collective-permute-start.14
  158.1 4.0 %collective-permute-start.15 = (f32[128,1]{1,0:T(8,128)S(1)}, f32[128,1]{1,0:T(8,128)S(1)}, u32[]{:S(2)}, u32[]{:S(2)}) collective-permute-start(f32[128,1]{1,0:T(8,128)S(1)} %get-tuple-element.42), channel_id=1, source_target_pairs={{0,1},{1,2},{2,3},{3,4},{4,5},{5,6},{6,7},{8,9},{9,10},{10,11},{11... | collective-permute-start | bytes 1544 | tf_op jit(solution)/shard_map/ppermute | solution.py:20
  162.2 1.3 collective-permute-done.15
  164.4 6.9 %all-reduce.14 = (f32[]{:T(128)}, f32[]{:T(128)}) all-reduce(f32[]{:T(128)} %get-tuple-element.5, f32[]{:T(128)} %get-tuple-element.4), channel_id=1, replica_groups=mesh['row_0'=4,'row_1'=4,'row_2'=2,'col'=8] {'row_0'}, use_global_device_ids=true, to_apply=%region_21.22 | all-reduce | flops 2 | bytes 16 | tf_op jit(solution)/shard_map/psum | solution.py:34
  171.3 9.6 %all-reduce.11 = (f32[]{:T(128)}, f32[]{:T(128)}) all-reduce(f32[]{:T(128)} %get-tuple-element.22, f32[]{:T(128)} %get-tuple-element.23), channel_id=1, replica_groups=mesh['row_0'=4,'row_1'=4,'row_2'=2,'col'=8] {'row_1'}, use_global_device_ids=true, to_apply=%region_22.23 | all-reduce | flops 2 | bytes 16 | tf_op jit(solution)/shard_map/psum | solution.py:34
  180.9 8.5 %all-reduce.17 = (f32[]{:T(128)}, f32[]{:T(128)}) all-reduce(f32[]{:T(128)} %get-tuple-element.16, f32[]{:T(128)} %get-tuple-element.17), channel_id=1, replica_groups=mesh['row_0'=4,'row_1'=4,'row_2'=2,'col'=8] {'row_2'}, use_global_device_ids=true, to_apply=%region_23.24 | all-reduce | flops 2 | bytes 16 | tf_op jit(solution)/shard_map/psum | solution.py:34
  189.4 14.3 %all-reduce.8 = (f32[]{:T(128)}, f32[]{:T(128)}) all-reduce(f32[]{:T(128)} %get-tuple-element.28, f32[]{:T(128)} %get-tuple-element.29), channel_id=1, replica_groups=mesh['row_0'=4,'row_1'=4,'row_2'=2,'col'=8] {'col'}, use_global_device_ids=true, to_apply=%region_24.25 | all-reduce | flops 2 | bytes 16 | tf_op jit(solution)/shard_map/psum | solution.py:34
  208.6 4.5 %slice.235 = f32[64,512]{1,0:T(8,128)S(1)} slice(f32[128,1024]{1,0:T(8,128)S(1)} %multiply_add_fusion), slice={[1:128:2], [1:1024:2]} | slice | bytes 262144 | tf_op jit(solution)/shard_map/slice | solution.py:67
  213.1 4.5 %slice.234 = f32[64,512]{1,0:T(8,128)S(1)} slice(f32[128,1024]{1,0:T(8,128)S(1)} %multiply_add_fusion), slice={[0:128:2], [1:1024:2]} | slice | bytes 262144 | tf_op jit(solution)/shard_map/slice | solution.py:67
  217.6 4.5 %slice.233 = f32[64,512]{1,0:T(8,128)S(1)} slice(f32[128,1024]{1,0:T(8,128)S(1)} %multiply_add_fusion), slice={[1:128:2], [0:1024:2]} | slice | bytes 262144 | tf_op jit(solution)/shard_map/slice | solution.py:67
  222.1 4.7 %slice.232 = f32[64,512]{1,0:T(8,128)S(1)} slice(f32[128,1024]{1,0:T(8,128)S(1)} %multiply_add_fusion), slice={[0:128:2], [0:1024:2]} | slice | bytes 262144 | tf_op jit(solution)/shard_map/slice | solution.py:67
  226.9 1.2 slice.239
  230.4 1.2 slice.236
  231.7 24.6 %all_to_all.5 = f32[32,32,256]{2,1,0:T(8,128)S(1)} all-to-all(f32[32,32,256]{2,1,0:T(8,128)S(1)} %broadcast_in_dim.10), channel_id=1, replica_groups=mesh['row_0'=4,'row_1'=4,'row_2'=2,'col'=8] {'row_0','row_1','row_2'}, dimensions={0} | all-to-all | bytes 2097152 | tf_op jit(solution)/shard_map/all_to_all | solution.py:40
  256.3 12.0 %slice.243 = f32[512,128]{1,0:T(8,128)S(1)} slice(f32[1024,256]{1,0:T(8,128)S(1)} %bitcast.13), slice={[1:1024:2], [1:256:2]} | slice | bytes 524288 | tf_op jit(solution)/shard_map/slice | solution.py:67
  268.3 12.0 %slice.242 = f32[512,128]{1,0:T(8,128)S(1)} slice(f32[1024,256]{1,0:T(8,128)S(1)} %bitcast.14), slice={[0:1024:2], [1:256:2]} | slice | bytes 524288 | tf_op jit(solution)/shard_map/slice | solution.py:67
  280.3 12.0 %slice.241 = f32[512,128]{1,0:T(8,128)S(1)} slice(f32[1024,256]{1,0:T(8,128)S(1)} %bitcast.15), slice={[1:1024:2], [0:256:2]} | slice | bytes 524288 | tf_op jit(solution)/shard_map/slice | solution.py:67
  292.3 12.3 %slice.240 = f32[512,128]{1,0:T(8,128)S(1)} slice(f32[1024,256]{1,0:T(8,128)S(1)} %bitcast.16), slice={[0:1024:2], [0:256:2]} | slice | bytes 524288 | tf_op jit(solution)/shard_map/slice | solution.py:67
  (42 shorter events, 11.6 us)
Async XLA Ops:
  0.6 18.9 %copy-start = (f32[3,128,1024]{2,1,0:T(8,128)S(1)}, f32[3,128,1024]{2,1,0:T(8,128)}, u32[]{:S(2)}) copy-start(f32[3,128,1024]{2,1,0:T(8,128)} %param.2) | copy-start | bytes 4718596
  1.7 17.8 %collective-permute-start.1 = (f32[3,1,1024]{2,1,0:T(1,128)S(1)}, f32[3,1,1024]{2,1,0:T(1,128)S(1)}, u32[]{:S(2)}, u32[]{:S(2)}) collective-permute-start(f32[3,1,1024]{2,1,0:T(1,128)S(1)} %get-tuple-element.39), channel_id=1, source_target_pairs={{0,8},{8,16},{16,24},{24,32},{32,40},{40,48},{48,56},{56,64},{64,7... | collective-permute-start | bytes 36872 | tf_op jit(solution)/shard_map/ppermute | solution.py:20
  6.2 13.3 %collective-permute-start.2 = (f32[3,1,1024]{2,1,0:T(1,128)S(1)}, f32[3,1,1024]{2,1,0:T(1,128)S(1)}, u32[]{:S(2)}, u32[]{:S(2)}) collective-permute-start(f32[3,1,1024]{2,1,0:T(1,128)S(1)} %get-tuple-element.40), channel_id=1, source_target_pairs={{8,0},{16,8},{24,16},{32,24},{40,32},{48,40},{56,48},{64,56},{72,6... | collective-permute-start | bytes 36872 | tf_op jit(solution)/shard_map/ppermute | solution.py:21
  9.3 8.3 %collective-permute-start.3 = (f32[3,128,1]{2,1,0:T(8,128)S(1)}, f32[3,128,1]{2,1,0:T(8,128)S(1)}, u32[]{:S(2)}, u32[]{:S(2)}) collective-permute-start(f32[3,128,1]{2,1,0:T(8,128)S(1)} %get-tuple-element.37), channel_id=1, source_target_pairs={{1,0},{2,1},{3,2},{4,3},{5,4},{6,5},{7,6},{9,8},{10,9},{11,10},{12... | collective-permute-start | bytes 4616 | tf_op jit(solution)/shard_map/ppermute | solution.py:21
  10.6 8.9 %collective-permute-start = (f32[3,128,1]{2,1,0:T(8,128)S(1)}, f32[3,128,1]{2,1,0:T(8,128)S(1)}, u32[]{:S(2)}, u32[]{:S(2)}) collective-permute-start(f32[3,128,1]{2,1,0:T(8,128)S(1)} %get-tuple-element.38), channel_id=1, source_target_pairs={{0,1},{1,2},{2,3},{3,4},{4,5},{5,6},{6,7},{8,9},{9,10},{10,11},{11... | collective-permute-start | bytes 4616 | tf_op jit(solution)/shard_map/ppermute | solution.py:20
  23.7 1.6 copy-start.2
  26.8 12.8 %collective-permute-start.5 = (f32[1,1024]{1,0:T(1,128)S(1)}, f32[1,1024]{1,0:T(1,128)S(1)}, u32[]{:S(2)}, u32[]{:S(2)}) collective-permute-start(f32[1,1024]{1,0:T(1,128)S(1)} %get-tuple-element.51), channel_id=1, source_target_pairs={{0,8},{8,16},{16,24},{24,32},{32,40},{40,48},{48,56},{56,64},{64,7... | collective-permute-start | bytes 12296 | tf_op jit(solution)/shard_map/ppermute | solution.py:20
  30.2 9.4 %collective-permute-start.4 = (f32[1,1024]{1,0:T(1,128)S(1)}, f32[1,1024]{1,0:T(1,128)S(1)}, u32[]{:S(2)}, u32[]{:S(2)}) collective-permute-start(f32[1,1024]{1,0:T(1,128)S(1)} %get-tuple-element.52), channel_id=1, source_target_pairs={{8,0},{16,8},{24,16},{32,24},{40,32},{48,40},{56,48},{64,56},{72,6... | collective-permute-start | bytes 12296 | tf_op jit(solution)/shard_map/ppermute | solution.py:21
  32.2 6.0 %collective-permute-start.6 = (f32[128,1]{1,0:T(8,128)S(1)}, f32[128,1]{1,0:T(8,128)S(1)}, u32[]{:S(2)}, u32[]{:S(2)}) collective-permute-start(f32[128,1]{1,0:T(8,128)S(1)} %get-tuple-element.49), channel_id=1, source_target_pairs={{1,0},{2,1},{3,2},{4,3},{5,4},{6,5},{7,6},{9,8},{10,9},{11,10},{12... | collective-permute-start | bytes 1544 | tf_op jit(solution)/shard_map/ppermute | solution.py:21
  33.5 6.1 %collective-permute-start.7 = (f32[128,1]{1,0:T(8,128)S(1)}, f32[128,1]{1,0:T(8,128)S(1)}, u32[]{:S(2)}, u32[]{:S(2)}) collective-permute-start(f32[128,1]{1,0:T(8,128)S(1)} %get-tuple-element.50), channel_id=1, source_target_pairs={{0,1},{1,2},{2,3},{3,4},{4,5},{5,6},{6,7},{8,9},{9,10},{10,11},{11... | collective-permute-start | bytes 1544 | tf_op jit(solution)/shard_map/ppermute | solution.py:20
  88.7 16.2 %collective-permute-start.9 = (f32[1,1024]{1,0:T(1,128)S(1)}, f32[1,1024]{1,0:T(1,128)S(1)}, u32[]{:S(2)}, u32[]{:S(2)}) collective-permute-start(f32[1,1024]{1,0:T(1,128)S(1)} %get-tuple-element.47), channel_id=1, source_target_pairs={{0,8},{8,16},{16,24},{24,32},{32,40},{40,48},{48,56},{56,64},{64,7... | collective-permute-start | bytes 12296 | tf_op jit(solution)/shard_map/ppermute | solution.py:20
  96.4 8.6 %collective-permute-start.8 = (f32[1,1024]{1,0:T(1,128)S(1)}, f32[1,1024]{1,0:T(1,128)S(1)}, u32[]{:S(2)}, u32[]{:S(2)}) collective-permute-start(f32[1,1024]{1,0:T(1,128)S(1)} %get-tuple-element.48), channel_id=1, source_target_pairs={{8,0},{16,8},{24,16},{32,24},{40,32},{48,40},{56,48},{64,56},{72,6... | collective-permute-start | bytes 12296 | tf_op jit(solution)/shard_map/ppermute | solution.py:21
  98.4 5.3 %collective-permute-start.10 = (f32[128,1]{1,0:T(8,128)S(1)}, f32[128,1]{1,0:T(8,128)S(1)}, u32[]{:S(2)}, u32[]{:S(2)}) collective-permute-start(f32[128,1]{1,0:T(8,128)S(1)} %get-tuple-element.45), channel_id=1, source_target_pairs={{1,0},{2,1},{3,2},{4,3},{5,4},{6,5},{7,6},{9,8},{10,9},{11,10},{12... | collective-permute-start | bytes 1544 | tf_op jit(solution)/shard_map/ppermute | solution.py:21
  99.7 5.3 %collective-permute-start.11 = (f32[128,1]{1,0:T(8,128)S(1)}, f32[128,1]{1,0:T(8,128)S(1)}, u32[]{:S(2)}, u32[]{:S(2)}) collective-permute-start(f32[128,1]{1,0:T(8,128)S(1)} %get-tuple-element.46), channel_id=1, source_target_pairs={{0,1},{1,2},{2,3},{3,4},{4,5},{5,6},{6,7},{8,9},{9,10},{10,11},{11... | collective-permute-start | bytes 1544 | tf_op jit(solution)/shard_map/ppermute | solution.py:20
  147.4 16.1 %collective-permute-start.13 = (f32[1,1024]{1,0:T(1,128)S(1)}, f32[1,1024]{1,0:T(1,128)S(1)}, u32[]{:S(2)}, u32[]{:S(2)}) collective-permute-start(f32[1,1024]{1,0:T(1,128)S(1)} %get-tuple-element.43), channel_id=1, source_target_pairs={{0,8},{8,16},{16,24},{24,32},{32,40},{40,48},{48,56},{56,64},{64,7... | collective-permute-start | bytes 12296 | tf_op jit(solution)/shard_map/ppermute | solution.py:20
  154.8 8.6 %collective-permute-start.12 = (f32[1,1024]{1,0:T(1,128)S(1)}, f32[1,1024]{1,0:T(1,128)S(1)}, u32[]{:S(2)}, u32[]{:S(2)}) collective-permute-start(f32[1,1024]{1,0:T(1,128)S(1)} %get-tuple-element.44), channel_id=1, source_target_pairs={{8,0},{16,8},{24,16},{32,24},{40,32},{48,40},{56,48},{64,56},{72,6... | collective-permute-start | bytes 12296 | tf_op jit(solution)/shard_map/ppermute | solution.py:21
  156.8 5.3 %collective-permute-start.14 = (f32[128,1]{1,0:T(8,128)S(1)}, f32[128,1]{1,0:T(8,128)S(1)}, u32[]{:S(2)}, u32[]{:S(2)}) collective-permute-start(f32[128,1]{1,0:T(8,128)S(1)} %get-tuple-element.41), channel_id=1, source_target_pairs={{1,0},{2,1},{3,2},{4,3},{5,4},{6,5},{7,6},{9,8},{10,9},{11,10},{12... | collective-permute-start | bytes 1544 | tf_op jit(solution)/shard_map/ppermute | solution.py:21
  158.1 5.3 %collective-permute-start.15 = (f32[128,1]{1,0:T(8,128)S(1)}, f32[128,1]{1,0:T(8,128)S(1)}, u32[]{:S(2)}, u32[]{:S(2)}) collective-permute-start(f32[128,1]{1,0:T(8,128)S(1)} %get-tuple-element.42), channel_id=1, source_target_pairs={{0,1},{1,2},{2,3},{3,4},{4,5},{5,6},{6,7},{8,9},{9,10},{10,11},{11... | collective-permute-start | bytes 1544 | tf_op jit(solution)/shard_map/ppermute | solution.py:20
  208.5 47.8 %copy-start.1 = (f32[128,1024]{1,0:T(8,128)}, f32[128,1024]{1,0:T(8,128)S(1)}, u32[]{:S(2)}) copy-start(f32[128,1024]{1,0:T(8,128)S(1)} %multiply_add_fusion) | copy-start | bytes 1572868
  226.9 29.4 %copy-start.3 = (f32[64,512]{1,0:T(8,128)}, f32[64,512]{1,0:T(8,128)S(1)}, u32[]{:S(2)}) copy-start(f32[64,512]{1,0:T(8,128)S(1)} %add_multiply_fusion.1) | copy-start | bytes 393220
where the time goes:
time: 307 us; the launch traced here: 306 us
  blocking collectives  146 us (48%)
  local copies, waits for them, and re-layouts  79.2 us (26%)
  starting transfers between devices  52.7 us (17%)
  between operations  11 us (4%)
  waiting for transfers between devices  8.59 us (3%)
  other arithmetic  8.45 us (3%)
    psum x12, blocking collectives, by_axis(): value = lax.psum(value, axis)  122 us
    ppermute x8, starting transfers between devices, padded_2(): lax.ppermute(last, axis, up)  39.9 us
    all_to_all x1, blocking collectives, from_everyone(): return lax.all_to_all(copies, axis, split_axis=0, concat_axis=0, tiled=True)  24.6 us
    slice x3, local copies, waits for them, and re-layouts, average_pool(): values[0::2, 0::2] + values[1::2, 0::2] + values[0::2, 1::2]  18.2 us
    slice x3, local copies, waits for them, and re-layouts, average_pool(): values[1::2, 0::2]  17.7 us
    slice x3, local copies, waits for them, and re-layouts, average_pool(): values[0::2, 1::2]  17.7 us
    slice x3, local copies, waits for them, and re-layouts, average_pool(): values[1::2, 1::2]  17.7 us
    ppermute x8, starting transfers between devices, padded_2(): lax.ppermute(leading, axis, [(b, a) for a, b in up])  12.8 us
  transfers between devices with their start and end apart: 16, of which 5 were waited for; matrix products, arithmetic and copies ran while one was open for 0% of the time, Pallas kernels for 0%

commit v1 on v0

v1 whole, which is shorter than its diff:
```python
import jax
import jax.numpy as jnp
from jax import lax
from jax.experimental import pallas as pl
from jax.experimental.pallas import tpu as pltpu
from jax.sharding import Mesh
from jax.sharding import PartitionSpec as P

K = 3
H, W = 128, 1024
TOP = 16
ROWS = TOP + H + 16
LANES = 128
BLOCKS = W // LANES
HALO = 4
ROW = ("row_0", "row_1", "row_2")
CHIP = ("row_0", "row_1")
ALL = ("row_0", "row_1", "row_2", "col")
VMEM = pltpu.MemorySpace.VMEM
ANY = pl.ANY
f32 = jnp.float32


def iota(shape, dim):
    return lax.broadcasted_iota(jnp.int32, shape, dim)


def place():
    row = (lax.axis_index("row_0") * 4 + lax.axis_index("row_1")) * 2 + lax.axis_index("row_2")
    return row, lax.axis_index("col")


def pack_kernel(src, lab, even_out, odd_out, left_out, right_out, rows, cols, lrows, lcols, sem):
    copies = []

    def fetch(a, b):
        c = pltpu.make_async_copy(a, b, sem.at[len(copies)])
        c.start()
        copies.append(c)

    for side, start in ((0, 0), (1, H - 8)):
        fetch(src.at[:, pl.ds(start, 8), :], rows.at[side])
        fetch(lab.at[pl.ds(start, 8), :], lrows.at[side])
    for side, start in ((0, 0), (1, W - LANES)):
        fetch(src.at[:, :, pl.ds(start, LANES)], cols.at[side])
        fetch(lab.at[:, pl.ds(start, LANES)], lcols.at[side])
    for c in copies[:4]:
        c.wait()
    row, _ = place()
    even = (row % 2) == 0
    upper = iota((8, W), 0) < HALO

    def sides(side):
        a = [rows[side, k] for k in range(K)] + [lrows[side].astype(f32)]
        pairs = []
        for x, y in ((a[0], a[1]), (a[2], a[3])):
            if side == 0:
                pairs.append(jnp.where(upper, x, pltpu.roll(y, HALO, 0)))
            else:
                pairs.append(jnp.where(upper, pltpu.roll(x, HALO, 0), y))
        return pairs

    top, bottom = sides(0), sides(1)
    for i in range(2):
        even_out[pl.ds(8 * i, 8), :] = jnp.where(even, bottom[i], top[i])
        odd_out[pl.ds(8 * i, 8), :] = jnp.where(even, top[i], bottom[i])
    for c in copies[4:]:
        c.wait()
    lane = iota((H, LANES), 1)
    for side, out in ((0, left_out), (1, right_out)):
        a = [cols[side, k] for k in range(K)] + [lcols[side].astype(f32)]
        total = jnp.zeros((H, LANES), f32)
        for k in range(K + 1):
            shift = HALO * k + (HALO if side else 0)
            moved = pltpu.roll(a[k], shift, 1) if shift else a[k]
            total = jnp.where((lane >= HALO * k) & (lane < HALO * (k + 1)), moved, total)
        out[...] = total


def pack(sources, labels):
    return pl.pallas_call(
        pack_kernel,
        out_shape=(
            jax.ShapeDtypeStruct((16, W), f32),
            jax.ShapeDtypeStruct((16, W), f32),
            jax.ShapeDtypeStruct((H, LANES), f32),
            jax.ShapeDtypeStruct((H, LANES), f32),
        ),
        in_specs=[pl.BlockSpec(memory_space=ANY)] * 2,
        out_specs=(pl.BlockSpec(memory_space=VMEM),) * 4,
        scratch_shapes=[
            pltpu.VMEM((2, K, 8, W), f32),
            pltpu.VMEM((2, K, H, LANES), f32),
            pltpu.VMEM((2, 8, W), jnp.int32),
            pltpu.VMEM((2, H, LANES), jnp.int32),
            pltpu.SemaphoreType.DMA((8,)),
        ],
        name="pack_rows",
    )(sources, labels)


def corner_kernel(got_even, got_odd, left, right, even_out, odd_out):
    row, col = place()
    row_even = (row % 2) == 0
    col_even = (col % 2) == 0
    upper = iota((8, LANES), 0) < HALO
    lane = iota((8, LANES), 1)
    strips = []
    for side, start in ((0, 0), (1, W - LANES)):
        total = jnp.zeros((8, LANES), f32)
        for k in range(K + 1):
            tile, half = divmod(k, 2)
            at = (pl.ds(8 * tile, 8), pl.ds(start, LANES))
            e, o = got_even[at], got_odd[at]
            above = jnp.where(row_even, o, e)
            below = jnp.where(row_even, e, o)
            if half:
                both = jnp.where(upper, pltpu.roll(above, HALO, 0), below)
            else:
                both = jnp.where(upper, above, pltpu.roll(below, HALO, 0))
            shift = HALO * k + (HALO if side else 0)
            moved = pltpu.roll(both, shift, 1) if shift else both
            total = jnp.where((lane >= HALO * k) & (lane < HALO * (k + 1)), moved, total)
        strips.append(total)
    even_out[pl.ds(0, H), :] = jnp.where(col_even, right[...], left[...])
    odd_out[pl.ds(0, H), :] = jnp.where(col_even, left[...], right[...])
    even_out[pl.ds(H, 8), :] = jnp.where(col_even, strips[1], strips[0])
    odd_out[pl.ds(H, 8), :] = jnp.where(col_even, strips[0], strips[1])


def pack_columns(got_even, got_odd, left, right):
    return pl.pallas_call(
        corner_kernel,
        out_shape=(jax.ShapeDtypeStruct((H + 8, LANES), f32),) * 2,
        in_specs=[pl.BlockSpec(memory_space=VMEM)] * 4,
        out_specs=(pl.BlockSpec(memory_space=VMEM),) * 2,
        name="pack_columns",
    )(got_even, got_odd, left, right)


def two_sum(a, b):
    s = a + b
    t = s - a
    return s, (a - (s - t)) + (b - t)


def exact_total(x):
    s, e = x, jnp.zeros_like(x)
    for shift in (4, 2, 1):
        s, more = two_sum(s, pltpu.roll(s, shift, 0))
        e = e + pltpu.roll(e, shift, 0) + more
    for shift in (64, 32, 16, 8, 4, 2, 1):
        s, more = two_sum(s, pltpu.roll(s, shift, 1))
        e = e + pltpu.roll(e, shift, 1) + more
    return s, e


def beside(ref, j, base):
    vertical = ref[j, pl.ds(base + 1, 8), :] + ref[j, pl.ds(base - 1, 8), :]
    return vertical


def shifted(tiles):
    lane = iota((8, LANES), 1)
    to_left = [pltpu.roll(t, LANES - 1, 1) for t in tiles]
    to_right = [pltpu.roll(t, 1, 1) for t in tiles]
    last, first = lane == LANES - 1, lane == 0
    after, before = [], []
    for j in range(len(tiles)):
        after.append(jnp.where(last, to_left[min(j + 1, len(tiles) - 1)], to_left[j]))
        before.append(jnp.where(first, to_right[max(j - 1, 0)], to_right[j]))
    return after, before


def main_kernel(
    src, lab, r_even, r_odd, c_even, c_odd, v0, v1, v2, sums_out, pooled_out, ext, lext, sem
):
    copies = []
    for k in range(K + 1):
        for j in range(BLOCKS):
            lanes = pl.ds(j * LANES, LANES)
            a = src.at[k, :, lanes] if k < K else lab.at[:, lanes]
            b = ext.at[k, j + 1, pl.ds(TOP, H), :] if k < K else lext.at[j + 1, pl.ds(TOP, H), :]
            c = pltpu.make_async_copy(a, b, sem.at[k, j])
            c.start()
            copies.append(c)
    row, col = place()
    row_even = (row % 2) == 0
    col_even = (col % 2) == 0

    def put(k, j, start, size, value):
        if k < K:
            ext[k, j, pl.ds(start, size), :] = value
        else:
            lext[j, pl.ds(start, size), :] = value.astype(jnp.int32)

    for k in range(K + 1):
        at = pl.ds(HALO * k, HALO)
        for j in range(BLOCKS):
            lanes = pl.ds(j * LANES, LANES)
            e, o = r_even[at, lanes], r_odd[at, lanes]
            put(k, j + 1, TOP - HALO, HALO, jnp.where(row_even, o, e))
            put(k, j + 1, TOP + H, HALO, jnp.where(row_even, e, o))
    for side, j in ((0, 0), (1, BLOCKS + 1)):
        e, o = c_even[...], c_odd[...]
        got = jnp.where(col_even, o, e) if side == 0 else jnp.where(col_even, e, o)
        for k in range(K + 1):
            shift = (LANES - HALO - HALO * k) if side == 0 else (LANES - HALO * k) % LANES
            moved = pltpu.roll(got, shift, 1) if shift else got
            put(k, j, TOP, H, moved[:H])
            put(k, j, TOP - HALO, HALO, moved[H : H + HALO])
            put(k, j, TOP + H, HALO, moved[H + HALO :])

    def outside(ref):
        @pl.when(row == 0)
        def _():
            ref[:, pl.ds(TOP - 8, 8), :] = jnp.zeros((BLOCKS + 2, 8, LANES), f32)

        @pl.when(row == 31)
        def _():
            ref[:, pl.ds(TOP + H, 8), :] = jnp.zeros((BLOCKS + 2, 8, LANES), f32)

        @pl.when(col == 0)
        def _():
            ref[0, :, :] = jnp.zeros((ROWS, LANES), f32)

        @pl.when(col == 7)
        def _():
            ref[BLOCKS + 1, :, :] = jnp.zeros((ROWS, LANES), f32)

    for c in copies:
        c.wait()

    def right_side(t, carry):
        base = pl.multiple_of(TOP - 8 + 8 * t, 8)
        out = [jnp.zeros((8, LANES), f32)] * (BLOCKS + 2)
        picked = [lext[j, pl.ds(base, 8), :] for j in range(BLOCKS + 2)]
        for k in range(K):
            plane = ext.at[k]
            tiles = [plane[j, pl.ds(base, 8), :] for j in range(BLOCKS + 2)]
            after, before = shifted(tiles)
            for j in range(BLOCKS + 2):
                term = 4.0 * tiles[j] - (beside(plane, j, base) + after[j] + before[j])
                out[j] = jnp.where(picked[j] == k, term, out[j])
        for j in range(BLOCKS + 2):
            v0[j, pl.ds(base, 8), :] = out[j]
        return carry

    lax.fori_loop(0, H // 8 + 2, right_side, 0)
    outside(v0)

    def neighbours(source, target):
        def step(t, carry):
            base = pl.multiple_of(TOP - 8 + 8 * t, 8)
            tiles = [source[j, pl.ds(base, 8), :] for j in range(BLOCKS + 2)]
            after, before = shifted(tiles)
            for j in range(BLOCKS + 2):
                target[j, pl.ds(base, 8), :] = beside(source, j, base) + after[j] + before[j]
            return carry

        lax.fori_loop(0, H // 8 + 2, step, 0)
        outside(target)

    neighbours(v0, v1)
    neighbours(v1, v2)

    def products(t, carry):
        base = pl.multiple_of(TOP + 8 * t, 8)
        at = pl.ds(base, 8)
        last = iota((8, LANES), 1) == LANES - 1
        c = [v2[j, at, :] for j in range(1, BLOCKS + 2)]
        rolled = [pltpu.roll(x, LANES - 1, 1) for x in c]
        found = [[] for _ in range(6)]
        for j in range(BLOCKS):
            x0, x1, x2 = v0[j + 1, at, :], v1[j + 1, at, :], c[j]
            x3 = v2[j + 1, pl.ds(base + 1, 8), :] + jnp.where(last, rolled[j + 1], rolled[j])
            for i, (a, b) in enumerate(((x0, x0), (x0, x1), (x1, x1), (x1, x2), (x2, x2), (x2, x3))):
                found[i].append(a * b)
        out = []
        for i in range(6):
            x = found[i]
            while len(x) > 1:
                x = [a + b for a, b in zip(x[0::2], x[1::2])]
            out.append(carry[i] + x[0])
        return tuple(out)

    zero = jnp.zeros((8, LANES), f32)
    totals = lax.fori_loop(0, H // 8, products, (zero,) * 6)
    lane = iota((8, LANES), 1)
    line = zero
    for i in range(6):
        s, e = exact_total(totals[i])
        if i == 5:
            s, e = s + s, e + e
        line = jnp.where(lane == i, s, jnp.where(lane == i + 8, e, line))
    sums_out[...] = jnp.broadcast_to(line[:1], (256, LANES))

    groups = W // 2 // LANES // 2
    spread = jnp.where(iota((512, LANES), 0) // 4 == iota((512, LANES), 1), f32(0.0625), f32(0.0))
    for i, ref in enumerate((v0, v1, v2)):
        for g in range(groups):
            parts = []
            for j in range(4):
                block = 1 + 4 * g + j
                at = [ref[block, pl.ds(TOP + q, H // 4, stride=4), :] for q in range(4)]
                parts.append((at[0] + at[1]) + (at[2] + at[3]))
            pooled_out[i, :, pl.ds(g * LANES, LANES)] = jnp.dot(
                jnp.concatenate(parts, 1), spread, precision=lax.Precision.HIGHEST, preferred_element_type=f32
            )


def main_stage(sources, labels, r_even, r_odd, c_even, c_odd):
    field = jax.ShapeDtypeStruct((BLOCKS + 2, ROWS, LANES), f32)
    return pl.pallas_call(
        main_kernel,
        out_shape=(
            field,
            field,
            field,
            jax.ShapeDtypeStruct((256, LANES), f32),
            jax.ShapeDtypeStruct((3, H // 4, W // 4), f32),
        ),
        in_specs=[pl.BlockSpec(memory_space=ANY)] * 2 + [pl.BlockSpec(memory_space=VMEM)] * 4,
        out_specs=(pl.BlockSpec(memory_space=VMEM),) * 5,
        scratch_shapes=[
            pltpu.VMEM((K, BLOCKS + 2, ROWS, LANES), f32),
            pltpu.VMEM((BLOCKS + 2, ROWS, LANES), jnp.int32),
            pltpu.SemaphoreType.DMA((K + 1, BLOCKS)),
        ],
        name="fields_and_products",
    )(sources, labels, r_even, r_odd, c_even, c_odd)


def two_product(a, b):
    p = a * b
    big = f32(4097.0)
    t = big * a
    ah = t - (t - a)
    al = a - ah
    t = big * b
    bh = t - (t - b)
    bl = b - bh
    return p, ((ah * bh - p) + ah * bl + al * bh) + al * bl


def less_scaled(a, b, scale):
    p, low = two_product(b[0], scale)
    low = low + b[1] * scale
    s, e = two_sum(a[0], -p)
    e = e + (a[1] - low)
    return two_sum(s, e)


def coefficients(n):
    shift = n[1][0] / n[0][0]
    current = n
    m = [n[0][0]]
    for _ in range(5):
        current = [less_scaled(current[i + 1], current[i], shift) for i in range(len(current) - 1)]
        m.append(current[0][0] + current[0][1])
    m0, m1, m2, m3, m4, m5 = m
    t = m1 / m0
    theta0 = shift + t
    m5 = m5 - 5.0 * t * m4
    m4 = m4 - 4.0 * t * m3
    m3 = m3 - 3.0 * t * m2
    m2 = m2 - t * m1
    one = jnp.ones_like(m0)
    zero = jnp.zeros_like(m0)
    second = m2 > 0.0
    safe2 = jnp.where(second, m2, one)
    b1 = jnp.where(second, m2 / m0, zero)
    s = jnp.where(second, m3 / safe2, zero)
    h2 = m4 - s * m3 - b1 * m2
    third = second & (h2 > 0.0)
    safe3 = jnp.where(third, h2, one)
    theta1 = theta0 + s
    theta2 = theta0 - s + (m5 - s * m4 - b1 * m3) / safe3
    b2 = h2 / safe2
    d0, d1, d2 = 4.0 - theta0, 4.0 - theta1, 4.0 - theta2
    e = d1 * d2 - b2
    y2 = jnp.where(third, one / (d0 * e - b1 * d2), zero)
    y1 = jnp.where(third, d2 * y2, jnp.where(second, one / (d0 * d1 - b1), zero))
    y0 = jnp.where(third, e * y2, jnp.where(second, d1 * y1, one / d0))
    return (
        y0 - theta0 * y1 + (theta0 * theta1 - b1) * y2,
        y1 - (theta0 + theta1) * y2,
        y2,
    )


def solve_kernel(all_sums, pooled, coef_out, mid_out):
    tiles = [(all_sums[pl.ds(8 * i, 8), :], jnp.zeros((8, LANES), f32)) for i in range(32)]
    while len(tiles) > 1:
        merged = []
        for a, b in zip(tiles[0::2], tiles[1::2]):
            s, e = two_sum(a[0], b[0])
            merged.append((s, e + (a[1] + b[1])))
        tiles = merged
    s, e = tiles[0]
    for shift in (4, 2, 1):
        s, more = two_sum(s, pltpu.roll(s, shift, 0))
        e = e + pltpu.roll(e, shift, 0) + more
    lane = iota((8, LANES), 1)

    def lane_of(x, i):
        return jnp.broadcast_to(
            jnp.sum(jnp.where(lane == i, x, f32(0.0)), axis=1, keepdims=True), (8, LANES)
        )

    n = [two_sum(lane_of(s, i), lane_of(e, i) + lane_of(s, i + 8)) for i in range(6)]
    c = coefficients(n)
    for i in range(3):
        coef_out[i] = c[i]
    for q in range(H // 4 // 8):
        for g in range(2):
            at = (pl.ds(8 * q, 8), pl.ds(g * LANES, LANES))
            value = c[0] * pooled[(0, *at)] + c[1] * pooled[(1, *at)] + c[2] * pooled[(2, *at)]
            for d in range(16):
                mid_out[(d, *at)] = value


def solve(all_sums, pooled):
    return pl.pallas_call(
        solve_kernel,
        out_shape=(
            jax.ShapeDtypeStruct((3, 8, LANES), f32),
            jax.ShapeDtypeStruct((16, H // 4, W // 4), f32),
        ),
        in_specs=[pl.BlockSpec(memory_space=VMEM)] * 2,
        out_specs=(pl.BlockSpec(memory_space=VMEM),) * 2,
        name="coefficients",
    )(all_sums, pooled)


def half_matrix(rows):
    return jnp.where(iota((rows, rows // 2), 0) // 2 == iota((rows, rows // 2), 1), f32(0.25), f32(0.0))


def blend_kernel(coef, v0, v1, v2, blended_out, fine_out, scratch):
    c = [coef[i] for i in range(3)]

    def step(t, carry):
        base = pl.multiple_of(8 * t, 8)
        for j in range(BLOCKS):
            at = (j + 1, pl.ds(base + TOP, 8), slice(None))
            value = c[0] * v0[at] + c[1] * v1[at] + c[2] * v2[at]
            blended_out[pl.ds(base, 8), pl.ds(j * LANES, LANES)] = value
            scratch[j, pl.ds(base, 8), :] = value
        return carry

    lax.fori_loop(0, H // 8, step, 0)
    half = half_matrix(2 * LANES)
    for g in range(BLOCKS // 2):
        parts = [
            scratch[2 * g + i, pl.ds(0, H // 2, stride=2), :] + scratch[2 * g + i, pl.ds(1, H // 2, stride=2), :]
            for i in range(2)
        ]
        fine_out[:, pl.ds(g * LANES, LANES)] = jnp.dot(
            jnp.concatenate(parts, 1), half, precision=lax.Precision.HIGHEST, preferred_element_type=f32
        )


def blend(coef, v0, v1, v2):
    return pl.pallas_call(
        blend_kernel,
        out_shape=(
            jax.ShapeDtypeStruct((H, W), f32),
            jax.ShapeDtypeStruct((H // 2, W // 2), f32),
        ),
        in_specs=[pl.BlockSpec(memory_space=VMEM)] * 4,
        out_specs=(pl.BlockSpec(memory_space=VMEM),) * 2,
        scratch_shapes=[pltpu.VMEM((BLOCKS, H, LANES), f32)],
        name="blend",
    )(coef, v0, v1, v2)


def assemble_kernel(own, other, mid_out, coarse_out, scratch):
    core = lax.axis_index("row_2")
    n = H // 4
    half = half_matrix(2 * LANES)
    first = core == 0

    def step(d, carry):
        at = pl.multiple_of(d * 2 * n, 2 * n)
        a, b = own[d], other[d]
        low, high = jnp.where(first, a, b), jnp.where(first, b, a)
        mid_out[pl.ds(at, n), :] = low
        mid_out[pl.ds(at + n, n), :] = high
        for g in range(2):
            lanes = slice(g * LANES, (g + 1) * LANES)
            scratch[g, pl.ds(at, n), :] = low[:, lanes]
            scratch[g, pl.ds(at + n, n), :] = high[:, lanes]
        return carry

    lax.fori_loop(0, 16, step, 0)
    parts = [
        scratch[g, pl.ds(0, 16 * n, stride=2), :] + scratch[g, pl.ds(1, 16 * n, stride=2), :] for g in range(2)
    ]
    coarse_out[...] = jnp.dot(
        jnp.concatenate(parts, 1), half, precision=lax.Precision.HIGHEST, preferred_element_type=f32
    )


def assemble(own, other):
    n = H // 4
    return pl.pallas_call(
        assemble_kernel,
        out_shape=(
            jax.ShapeDtypeStruct((32 * n, W // 4), f32),
            jax.ShapeDtypeStruct((16 * n, W // 8), f32),
        ),
        in_specs=[pl.BlockSpec(memory_space=VMEM)] * 2,
        out_specs=(pl.BlockSpec(memory_space=VMEM),) * 2,
        scratch_shapes=[pltpu.VMEM((2, 32 * n, LANES), f32)],
        name="assemble",
    )(own, other)


def swaps(devices, first):
    pairs = [(i, i + 1) for i in range(first, devices - 1, 2)]
    return pairs + [(b, a) for a, b in pairs]


def exchange(even, odd, axis):
    devices = lax.axis_size(axis)
    return lax.ppermute(even, axis, swaps(devices, 0)), lax.ppermute(odd, axis, swaps(devices, 1))


def per_device(sources, labels):
    even, odd, left, right = pack(sources, labels)
    r_even, r_odd = exchange(even, odd, ROW)
    c_even, c_odd = exchange(*pack_columns(r_even, r_odd, left, right), "col")
    v0, v1, v2, sums, pooled = main_stage(sources, labels, r_even, r_odd, c_even, c_odd)
    sums = lax.all_to_all(sums.reshape(256, 1, LANES), ALL, split_axis=0, concat_axis=0, tiled=True)
    coef, mid = solve(sums.reshape(256, LANES), pooled)
    mid = lax.all_to_all(mid, CHIP, split_axis=0, concat_axis=0, tiled=True)
    other = lax.ppermute(mid, "row_2", [(0, 1), (1, 0)])
    blended, fine = blend(coef, v0, v1, v2)
    overview_mid, overview_coarse = assemble(mid, other)
    return (blended, fine, overview_mid, overview_coarse)


def solution(mesh):
    finer = Mesh(
        mesh.devices.reshape(4, 4, 2, mesh.shape["col"]), ("row_0", "row_1", "row_2", "col")
    )
    return jax.shard_map(
        per_device,
        mesh=finer,
        in_specs=(P(None, ROW, "col"), P(ROW, "col")),
        out_specs=(P(ROW, "col"), P(ROW, "col"), P(None, "col"), P(None, "col")),
        check_vma=False,
    )
```

time: 307 us -> 86.4 us (0.28)
  blocking collectives: 146 us -> 45.2 us
  local copies, waits for them, and re-layouts: 79.2 us -> 2.67 us
  starting transfers between devices: 52.7 us -> 7.66 us
  Pallas kernels: 0 us -> 23 us
  between operations: 11 us -> 0.69 us
  other arithmetic: 8.45 us -> 0 us
    psum x12 -> x0, blocking collectives: 122 us -> none  [by_axis(): value = lax.psum(value, axis)]
    slice x20 -> x0, local copies, waits for them, and re-layouts: 73.6 us -> none  [the longest x3 18.2 us: average_pool(): values[0::2, 0::2] + values[1::2, 0::2] + values[0::2, 1::2]]
    ppermute x16 -> x5, starting transfers between devices: 52.7 us -> 7.66 us  [the longest x2 3.29 us: exchange(): lax.ppermute(even, axis, swaps(devices, 0))]
    pallas_call x0 -> x6, Pallas kernels: none -> 23 us  [the longest x1 11.6 us: main_stage(): pl.pallas_call(main_kernel, out_shape=(field, field, field, jax.ShapeDtyp...]
    all_to_all x1 -> x2, blocking collectives: 24.6 us -> 45.2 us  [the longest x1 31 us: per_device(): lax.all_to_all(sums.reshape(256, 1, LANES), ALL, split_axis=0, concat_axi...]
    ppermute x16 -> x5, waiting for transfers between devices: 8.59 us -> 6.56 us  [the longest x2 3.85 us: exchange(): lax.ppermute(odd, axis, swaps(devices, 1))]
  transfers between devices with their start and end apart: 16 -> 5, of which waited for: 5 -> 2; matrix products, arithmetic and copies ran while one was open for 0% -> 0% of each run, Pallas kernels for 0% -> 3%
where the time goes in v1:
time: 86.4 us; the launch traced here: 85.8 us
  blocking collectives  45.2 us (52%)
  Pallas kernels  23 us (27%)
  starting transfers between devices  7.66 us (9%)
  waiting for transfers between devices  6.56 us (8%)
  local copies, waits for them, and re-layouts  2.67 us (3%)
    all_to_all x1, blocking collectives, per_device(): lax.all_to_all(sums.reshape(256, 1, LANES), ALL, split_axis=0, concat_axi...  31 us
    all_to_all x1, blocking collectives, per_device(): mid = lax.all_to_all(mid, CHIP, split_axis=0, concat_axis=0, tiled=True)  14.2 us
    pallas_call x1, Pallas kernels, main_stage(): pl.pallas_call(main_kernel, out_shape=(field, field, field, jax.ShapeDtyp...  11.6 us
    ppermute x2, waiting for transfers between devices, exchange(): lax.ppermute(odd, axis, swaps(devices, 1))  3.85 us
    ppermute x2, starting transfers between devices, exchange(): lax.ppermute(even, axis, swaps(devices, 0))  3.29 us
    pallas_call x1, Pallas kernels, blend(): pl.pallas_call(blend_kernel, out_shape=(jax.ShapeDtypeStruct((H, W), f32)...  2.97 us
    ppermute x2, waiting for transfers between devices, exchange(): lax.ppermute(even, axis, swaps(devices, 0))  2.71 us
    pallas_call x1, Pallas kernels, assemble(): pl.pallas_call(assemble_kernel, out_shape=(jax.ShapeDtypeStruct((32 * n,...  2.7 us
  transfers between devices with their start and end apart: 5, of which 2 were waited for; matrix products, arithmetic and copies ran while one was open for 0% of the time, Pallas kernels for 3%

profile of v1, /device:TPU:1, one launch (start us, length us, event | category | flops | bytes accessed | tf_op | source)
XLA Modules:
  0.0 85.8 jit_solution(7035697712159935313)
XLA Ops:
  0.6 2.1 %pack_rows.1 = (f32[16,1024]{1,0:T(8,128)}, f32[16,1024]{1,0:T(8,128)}, f32[128,128]{1,0:T(8,128)}, f32[128,128]{1,0:T(8,128)}) custom-call(f32[3,128,1024]{2,1,0:T(8,128)} %src.3, s32[128,1024]{1,0:T(8,128)} %lab.3), custom_call_target="tpu_custom_call" | custom-call | tf_op jit(solution)/shard_map/pack_rows/pallas_call | solution.py:81
  2.7 3.3 %collective-permute-start = (f32[16,1024]{1,0:T(8,128)}, f32[16,1024]{1,0:T(8,128)S(1)}, u32[]{:S(2)}, u32[]{:S(2)}) collective-permute-start(f32[16,1024]{1,0:T(8,128)} %get-tuple-element.21), channel_id=1, source_target_pairs={{0,8},{16,24},{32,40},{48,56},{64,72},{80,88},{96,104},{112,120},{... | collective-permute-start | bytes 196616 | tf_op jit(solution)/shard_map/ppermute | solution.py:527
  6.0 1.9 %collective-permute-start.1 = (f32[16,1024]{1,0:T(8,128)}, f32[16,1024]{1,0:T(8,128)S(1)}, u32[]{:S(2)}, u32[]{:S(2)}) collective-permute-start(f32[16,1024]{1,0:T(8,128)} %get-tuple-element.22), channel_id=1, source_target_pairs={{8,16},{24,32},{40,48},{56,64},{72,80},{88,96},{104,112},{120,128}... | collective-permute-start | bytes 196616 | tf_op jit(solution)/shard_map/ppermute | solution.py:527
  7.9 0.0 collective-permute-done.got_even.r_even
  7.9 0.0 copy-start.2
  7.9 3.8 %collective-permute-done.1.got_odd.r_odd = f32[16,1024]{1,0:T(8,128)S(1)} collective-permute-done((f32[16,1024]{1,0:T(8,128)}, f32[16,1024]{1,0:T(8,128)S(1)}, u32[]{:S(2)}, u32[]{:S(2)}) %collective-permute-start.1) | collective-permute-done | bytes 65568 | tf_op jit(solution)/shard_map/ppermute | solution.py:527
  11.8 0.0 copy-start.3
  11.8 0.0 copy-done.2
  11.8 0.6 copy-done.3
  12.4 1.7 %pack_columns.1 = (f32[136,128]{1,0:T(8,128)}, f32[136,128]{1,0:T(8,128)}) custom-call(f32[16,1024]{1,0:T(8,128)} %copy-done.2, f32[16,1024]{1,0:T(8,128)} %copy-done.3, f32[128,128]{1,0:T(8,128)} %get-tuple-element.23.left, f32[128,128]{1,0:T(8,128)} %get-tuple-element.24.right), custom_call_target="tpu_custom_call" | custom-call | tf_op jit(solution)/shard_map/pack_columns/pallas_call | solution.py:132
  14.1 0.0 collective-permute-start.2
  14.1 0.7 collective-permute-start.3
  14.7 2.7 %collective-permute-done.2.c_even = f32[136,128]{1,0:T(8,128)S(1)} collective-permute-done((f32[136,128]{1,0:T(8,128)}, f32[136,128]{1,0:T(8,128)S(1)}, u32[]{:S(2)}, u32[]{:S(2)}) %collective-permute-start.2) | collective-permute-done | bytes 69664 | tf_op jit(solution)/shard_map/ppermute | solution.py:527
  17.5 0.0 copy-start.4
  17.5 0.0 collective-permute-done.3.c_odd
  17.5 0.6 copy-done.4
  18.1 0.0 copy-start.5
  18.1 0.6 copy-done.5
  18.7 11.6 %fields_and_products.1 = (f32[10,160,128]{2,1,0:T(8,128)}, f32[10,160,128]{2,1,0:T(8,128)}, f32[10,160,128]{2,1,0:T(8,128)}, f32[256,128]{1,0:T(8,128)}, f32[3,32,256]{2,1,0:T(8,128)}) custom-call(f32[3,128,1024]{2,1,0:T(8,128)} %src.3, s32[128,1024]{1,0:T(8,128)} %lab.3, f32[16,1024]{1,0:T(8,128)} %copy-done.2, f32[16,1024]{1,0:T(8,128)} %copy-done.3, ...), custom_call_target="tpu_custom_call" | custom-call | tf_op jit(solution)/shard_map/fields_and_products/pallas_call | solution.py:314
  30.3 31.0 %all_to_all.10 = f32[256,1,128]{2,1,0:T(1,128)} all-to-all(f32[256,1,128]{2,1,0:T(1,128)} %bitcast.5), channel_id=1, replica_groups=mesh['row_0'=4,'row_1'=4,'row_2'=2,'col'=8] {'row_0','row_1','row_2','col'}, dimensions={0} | all-to-all | bytes 262144 | tf_op jit(solution)/shard_map/all_to_all | solution.py:535
  61.3 2.0 %coefficients.1 = (f32[3,8,128]{2,1,0:T(8,128)}, f32[16,32,256]{2,1,0:T(8,128)}) custom-call(f32[256,128]{1,0:T(8,128)} %bitcast.4, f32[3,32,256]{2,1,0:T(8,128)} %get-tuple-element.28.pooled), custom_call_target="tpu_custom_call" | custom-call | tf_op jit(solution)/shard_map/coefficients/pallas_call | solution.py:424
  63.3 14.2 %all_to_all.11.own = f32[16,32,256]{2,1,0:T(8,128)S(1)} all-to-all(f32[16,32,256]{2,1,0:T(8,128)} %get-tuple-element.35), channel_id=1, replica_groups=mesh['row_0'=4,'row_1'=4,'row_2'=2,'col'=8] {'row_0','row_1'}, dimensions={0} | all-to-all | bytes 1048576 | tf_op jit(solution)/shard_map/all_to_all | solution.py:537
  77.5 0.0 copy-start
  77.5 1.8 %collective-permute-start.4 = (f32[16,32,256]{2,1,0:T(8,128)S(1)}, f32[16,32,256]{2,1,0:T(8,128)S(1)}, u32[]{:S(2)}, u32[]{:S(2)}) collective-permute-start(f32[16,32,256]{2,1,0:T(8,128)S(1)} %all_to_all.11.own), channel_id=1, source_target_pairs={{0,8},{8,0},{1,9},{9,1},{2,10},{10,2},{3,11},{11,3},{4,12},{12,4},... | collective-permute-start | bytes 1572872 | tf_op jit(solution)/shard_map/ppermute | solution.py:538
  79.3 3.0 %blend.1 = (f32[128,1024]{1,0:T(8,128)}, f32[64,512]{1,0:T(8,128)}) custom-call(f32[3,8,128]{2,1,0:T(8,128)} %get-tuple-element.29.coef, f32[10,160,128]{2,1,0:T(8,128)} %get-tuple-element.30.v0, f32[10,160,128]{2,1,0:T(8,128)} %get-tuple-element.31.v1, f32[10,160,128]{2,1,0:T(8,128)} %get-tuple-element.32.v2), custom_call_target="tpu_custom_call" | custom-call | tf_op jit(solution)/shard_map/blend/pallas_call | solution.py:465
  82.3 0.0 collective-permute-done.4.other
  82.3 0.0 copy-done
  82.3 0.0 copy-start.1
  82.3 0.8 copy-done.1
  83.1 2.7 %assemble.1 = (f32[1024,256]{1,0:T(8,128)}, f32[512,128]{1,0:T(8,128)}) custom-call(f32[16,32,256]{2,1,0:T(8,128)} %copy-done, f32[16,32,256]{2,1,0:T(8,128)} %copy-done.1), custom_call_target="tpu_custom_call" | custom-call | tf_op jit(solution)/shard_map/assemble/pallas_call | solution.py:507
Async XLA Ops:
  2.7 5.2 %collective-permute-start = (f32[16,1024]{1,0:T(8,128)}, f32[16,1024]{1,0:T(8,128)S(1)}, u32[]{:S(2)}, u32[]{:S(2)}) collective-permute-start(f32[16,1024]{1,0:T(8,128)} %get-tuple-element.21), channel_id=1, source_target_pairs={{0,8},{16,24},{32,40},{48,56},{64,72},{80,88},{96,104},{112,120},{... | collective-permute-start | bytes 196616 | tf_op jit(solution)/shard_map/ppermute | solution.py:527
  6.0 5.8 %collective-permute-start.1 = (f32[16,1024]{1,0:T(8,128)}, f32[16,1024]{1,0:T(8,128)S(1)}, u32[]{:S(2)}, u32[]{:S(2)}) collective-permute-start(f32[16,1024]{1,0:T(8,128)} %get-tuple-element.22), channel_id=1, source_target_pairs={{8,16},{24,32},{40,48},{56,64},{72,80},{88,96},{104,112},{120,128}... | collective-permute-start | bytes 196616 | tf_op jit(solution)/shard_map/ppermute | solution.py:527
  7.9 3.9 %copy-start.2 = (f32[16,1024]{1,0:T(8,128)}, f32[16,1024]{1,0:T(8,128)S(1)}, u32[]{:S(2)}) copy-start(f32[16,1024]{1,0:T(8,128)S(1)} %collective-permute-done.got_even.r_even) | copy-start | bytes 196612
  11.8 0.6 copy-start.3
  14.1 3.4 %collective-permute-start.2 = (f32[136,128]{1,0:T(8,128)}, f32[136,128]{1,0:T(8,128)S(1)}, u32[]{:S(2)}, u32[]{:S(2)}) collective-permute-start(f32[136,128]{1,0:T(8,128)} %get-tuple-element.25), channel_id=1, source_target_pairs={{0,1},{2,3},{4,5},{6,7},{1,0},{3,2},{5,4},{7,6},{8,9},{10,11},{12,... | collective-permute-start | bytes 208904 | tf_op jit(solution)/shard_map/ppermute | solution.py:527
  14.1 3.4 %collective-permute-start.3 = (f32[136,128]{1,0:T(8,128)}, f32[136,128]{1,0:T(8,128)S(1)}, u32[]{:S(2)}, u32[]{:S(2)}) collective-permute-start(f32[136,128]{1,0:T(8,128)} %get-tuple-element.26), channel_id=1, source_target_pairs={{1,2},{3,4},{5,6},{2,1},{4,3},{6,5},{9,10},{11,12},{13,14},{10,9},... | collective-permute-start | bytes 208904 | tf_op jit(solution)/shard_map/ppermute | solution.py:527
  17.5 0.6 copy-start.4
  18.1 0.6 copy-start.5
  77.5 4.8 %copy-start = (f32[16,32,256]{2,1,0:T(8,128)}, f32[16,32,256]{2,1,0:T(8,128)S(1)}, u32[]{:S(2)}) copy-start(f32[16,32,256]{2,1,0:T(8,128)S(1)} %all_to_all.11.own) | copy-start | bytes 1572868
  77.5 4.8 %collective-permute-start.4 = (f32[16,32,256]{2,1,0:T(8,128)S(1)}, f32[16,32,256]{2,1,0:T(8,128)S(1)}, u32[]{:S(2)}, u32[]{:S(2)}) collective-permute-start(f32[16,32,256]{2,1,0:T(8,128)S(1)} %all_to_all.11.own), channel_id=1, source_target_pairs={{0,8},{8,0},{1,9},{9,1},{2,10},{10,2},{3,11},{11,3},{4,12},{12,4},... | collective-permute-start | bytes 1572872 | tf_op jit(solution)/shard_map/ppermute | solution.py:538
  82.3 0.8 copy-start.1

commit v2 on v1

v2 whole, which is shorter than its diff:
```python
import jax
import jax.numpy as jnp
from jax import lax
from jax.experimental import pallas as pl
from jax.experimental.pallas import tpu as pltpu
from jax.sharding import Mesh
from jax.sharding import PartitionSpec as P

K = 3
H, W = 128, 1024
TOP = 16
ROWS = TOP + H + 16
LANES = 128
BLOCKS = W // LANES
HALO = 4
ROW = ("row_0", "row_1", "row_2")
CHIP = ("row_0", "row_1")
ALL = ("row_0", "row_1", "row_2", "col")
VMEM = pltpu.MemorySpace.VMEM
WHOLE = pl.BlockSpec(memory_space=VMEM)
FAR = pl.BlockSpec(memory_space=pltpu.MemorySpace.HBM)
LIMIT = pltpu.CompilerParams(vmem_limit_bytes=24 * 2**20)
CHUNK = 3
f32 = jnp.float32


def iota(shape, dim):
    return lax.broadcasted_iota(jnp.int32, shape, dim)


def place():
    row = (lax.axis_index("row_0") * 4 + lax.axis_index("row_1")) * 2 + lax.axis_index("row_2")
    return row, lax.axis_index("col")


def near(shape, dtype=f32):
    return pltpu.VMEM(shape, dtype)


def held(*values):
    return [pltpu.with_memory_space_constraint(v, VMEM) for v in values]


def far(*values):
    return [pltpu.with_memory_space_constraint(v, pltpu.MemorySpace.HBM) for v in values]


def cost(us):
    return pl.CostEstimate(flops=int(us * 3e8), bytes_accessed=0, transcendentals=0)


def merge_strips(parts, side, lane):
    total = jnp.zeros_like(parts[0])
    for k in range(K + 1):
        shift = HALO * k + (HALO if side else 0)
        moved = pltpu.roll(parts[k], shift, 1) if shift else parts[k]
        total = jnp.where((lane >= HALO * k) & (lane < HALO * (k + 1)), moved, total)
    return total


def pack_kernel(src, lab, even_out, odd_out, rows, lrows, sem):
    copies = []
    for side, start in ((0, 0), (1, H - 8)):
        for i, (a, b) in enumerate(
            (
                (src.at[:, pl.ds(start, 8), :], rows.at[side]),
                (lab.at[pl.ds(start, 8), :], lrows.at[side]),
            )
        ):
            c = pltpu.make_async_copy(a, b, sem.at[side, i])
            c.start()
            copies.append(c)
    for c in copies:
        c.wait()
    row, _ = place()
    even = (row % 2) == 0
    upper = iota((8, W), 0) < HALO

    def sides(side):
        a = [rows[side, k] for k in range(K)] + [lrows[side].astype(f32)]
        pairs = []
        for x, y in ((a[0], a[1]), (a[2], a[3])):
            if side == 0:
                pairs.append(jnp.where(upper, x, pltpu.roll(y, HALO, 0)))
            else:
                pairs.append(jnp.where(upper, pltpu.roll(x, HALO, 0), y))
        return pairs

    top, bottom = sides(0), sides(1)
    for i in range(2):
        even_out[pl.ds(8 * i, 8), :] = jnp.where(even, bottom[i], top[i])
        odd_out[pl.ds(8 * i, 8), :] = jnp.where(even, top[i], bottom[i])


def pack_rows(sources, labels):
    return pl.pallas_call(
        pack_kernel,
        out_shape=(near((16, W)), near((16, W))),
        in_specs=[FAR] * 2,
        out_specs=(WHOLE,) * 2,
        scratch_shapes=[
            pltpu.VMEM((2, K, 8, W), f32),
            pltpu.VMEM((2, 8, W), jnp.int32),
            pltpu.SemaphoreType.DMA((2, 2)),
        ],
        compiler_params=LIMIT,
        cost_estimate=cost(1),
        name="pack_rows",
    )(*far(sources, labels))


def load_kernel(src, lab, ext, lext, left_out, right_out, sem):
    copies = {}
    for j in (0, BLOCKS - 1, *range(1, BLOCKS - 1)):
        lanes = pl.ds(j * LANES, LANES)
        for k in range(K + 1):
            a = src.at[k, :, lanes] if k < K else lab.at[:, lanes]
            b = ext.at[k, j + 1, pl.ds(TOP, H), :] if k < K else lext.at[j + 1, pl.ds(TOP, H), :]
            c = pltpu.make_async_copy(a, b, sem.at[k, j])
            c.start()
            copies[k, j] = c
    own = pl.ds(TOP, H)
    lane = iota((H, LANES), 1)
    for side, out in ((0, left_out), (1, right_out)):
        j = side * (BLOCKS - 1)
        for k in range(K + 1):
            copies.pop((k, j)).wait()
        parts = [ext[k, j + 1, own, :] for k in range(K)] + [lext[j + 1, own, :].astype(f32)]
        out[...] = merge_strips(parts, side, lane)
    for c in copies.values():
        c.wait()


def load(sources, labels):
    return pl.pallas_call(
        load_kernel,
        out_shape=(
            near((K, BLOCKS + 2, ROWS, LANES)),
            near((BLOCKS + 2, ROWS, LANES), jnp.int32),
            near((H, LANES)),
            near((H, LANES)),
        ),
        in_specs=[FAR] * 2,
        out_specs=(WHOLE,) * 4,
        scratch_shapes=[pltpu.SemaphoreType.DMA((K + 1, BLOCKS))],
        compiler_params=LIMIT,
        cost_estimate=cost(2),
        name="load_block",
    )(*far(sources, labels))


def corner_kernel(got_even, got_odd, left, right, even_out, odd_out):
    row, col = place()
    row_even = (row % 2) == 0
    col_even = (col % 2) == 0
    upper = iota((8, LANES), 0) < HALO
    lane = iota((8, LANES), 1)
    strips = []
    for side, start in ((0, 0), (1, W - LANES)):
        parts = []
        for k in range(K + 1):
            tile, half = divmod(k, 2)
            at = (pl.ds(8 * tile, 8), pl.ds(start, LANES))
            e, o = got_even[at], got_odd[at]
            above = jnp.where(row_even, o, e)
            below = jnp.where(row_even, e, o)
            if half:
                parts.append(jnp.where(upper, pltpu.roll(above, HALO, 0), below))
            else:
                parts.append(jnp.where(upper, above, pltpu.roll(below, HALO, 0)))
        strips.append(merge_strips(parts, side, lane))
    even_out[pl.ds(0, H), :] = jnp.where(col_even, right[...], left[...])
    odd_out[pl.ds(0, H), :] = jnp.where(col_even, left[...], right[...])
    even_out[pl.ds(H, 8), :] = jnp.where(col_even, strips[1], strips[0])
    odd_out[pl.ds(H, 8), :] = jnp.where(col_even, strips[0], strips[1])


def pack_columns(got_even, got_odd, left, right):
    return pl.pallas_call(
        corner_kernel,
        out_shape=(near((H + 8, LANES)),) * 2,
        in_specs=[WHOLE] * 4,
        out_specs=(WHOLE,) * 2,
        compiler_params=LIMIT,
        cost_estimate=cost(0.5),
        name="pack_columns",
    )(*held(got_even, got_odd, left, right))


def two_sum(a, b):
    s = a + b
    t = s - a
    return s, (a - (s - t)) + (b - t)


def shifted(tiles):
    lane = iota((8, LANES), 1)
    to_left = [pltpu.roll(t, LANES - 1, 1) for t in tiles]
    to_right = [pltpu.roll(t, 1, 1) for t in tiles]
    last, first = lane == LANES - 1, lane == 0
    n = len(tiles)
    after = [jnp.where(last, to_left[min(j + 1, n - 1)], to_left[j]) for j in range(n)]
    before = [jnp.where(first, to_right[max(j - 1, 0)], to_right[j]) for j in range(n)]
    return after, before


def right_side(ext, lext, out, runs):
    def step(t, carry):
        for u in range(CHUNK):
            base = pl.multiple_of(TOP - 8 + 8 * (CHUNK * t + u), 8)
            for start, count, keep in runs:
                total = {j: jnp.zeros((8, LANES), f32) for j in keep}
                picked = {j: lext[j, pl.ds(base, 8), :] for j in keep}
                for k in range(K):
                    tiles = [ext[k, start + i, pl.ds(base, 8), :] for i in range(count)]
                    after, before = shifted(tiles)
                    for j in keep:
                        i = j - start
                        vertical = ext[k, j, pl.ds(base + 1, 8), :] + ext[k, j, pl.ds(base - 1, 8), :]
                        term = 4.0 * tiles[i] - (vertical + after[i] + before[i])
                        total[j] = jnp.where(picked[j] == k, term, total[j])
                for j in keep:
                    out[j, pl.ds(base, 8), :] = total[j]
        return carry

    lax.fori_loop(0, (H // 8 + 2) // CHUNK, step, 0)


def neighbours(source, target, runs):
    def step(t, carry):
        for u in range(2 * CHUNK):
            base = pl.multiple_of(TOP - 8 + 8 * (2 * CHUNK * t + u), 8)
            for start, count, keep in runs:
                tiles = [source[start + i, pl.ds(base, 8), :] for i in range(count)]
                after, before = shifted(tiles)
                for j in keep:
                    i = j - start
                    vertical = source[j, pl.ds(base + 1, 8), :] + source[j, pl.ds(base - 1, 8), :]
                    target[j, pl.ds(base, 8), :] = vertical + after[i] + before[i]
        return carry

    lax.fori_loop(0, (H // 8 + 2) // CHUNK // 2, step, 0)


def products(v0, v1, v2, blocks, totals):
    def step(t, carry):
        totals = carry
        for u in range(2):
            base = pl.multiple_of(TOP + 8 * (2 * t + u), 8)
            at = pl.ds(base, 8)
            last = iota((8, LANES), 1) == LANES - 1
            found = [[] for _ in range(6)]
            rolled = {}
            for j in blocks:
                for i in (j, j + 1):
                    if i not in rolled:
                        rolled[i] = pltpu.roll(v2[i, at, :], LANES - 1, 1)
                x0, x1, x2 = v0[j, at, :], v1[j, at, :], v2[j, at, :]
                x3 = v2[j, pl.ds(base + 1, 8), :] + jnp.where(last, rolled[j + 1], rolled[j])
                for i, (a, b) in enumerate(((x0, x0), (x0, x1), (x1, x1), (x1, x2), (x2, x2), (x2, x3))):
                    found[i].append(a * b)
            out = []
            for i in range(6):
                x = found[i]
                while len(x) > 1:
                    x = [sum(x[a : a + 2][1:], x[a]) for a in range(0, len(x), 2)]
                out.append(totals[i] + x[0])
            totals = tuple(out)
        return totals

    return lax.fori_loop(0, H // 16, step, totals)


def clear_outside(ref, blocks, rows, columns):
    row, col = place()
    zero = jnp.zeros((8, LANES), f32)
    if rows:

        @pl.when(row == 0)
        def _():
            for j in blocks:
                ref[j, pl.ds(TOP - 8, 8), :] = zero

        @pl.when(row == 31)
        def _():
            for j in blocks:
                ref[j, pl.ds(TOP + H, 8), :] = zero

    if columns:

        @pl.when(col == 0)
        def _():
            ref[0, :, :] = jnp.zeros((ROWS, LANES), f32)

        @pl.when(col == 7)
        def _():
            ref[BLOCKS + 1, :, :] = jnp.zeros((ROWS, LANES), f32)


def inner_kernel(ext_in, lext_in, r_even, r_odd, ext, lext, v0, v1, v2, totals_out):
    del ext_in, lext_in
    row, _ = place()
    row_even = (row % 2) == 0
    for k in range(K + 1):
        at = pl.ds(HALO * k, HALO)
        for j in range(BLOCKS):
            lanes = pl.ds(j * LANES, LANES)
            e, o = r_even[at, lanes], r_odd[at, lanes]
            above, below = jnp.where(row_even, o, e), jnp.where(row_even, e, o)
            for start, value in ((TOP - HALO, above), (TOP + H, below)):
                if k < K:
                    ext[k, j + 1, pl.ds(start, HALO), :] = value
                else:
                    lext[j + 1, pl.ds(start, HALO), :] = value.astype(jnp.int32)
    runs = ((1, BLOCKS, range(1, BLOCKS + 1)),)
    right_side(ext, lext, v0, runs)
    clear_outside(v0, range(1, BLOCKS + 1), True, False)
    neighbours(v0, v1, runs)
    clear_outside(v1, range(1, BLOCKS + 1), True, False)
    neighbours(v1, v2, runs)
    clear_outside(v2, range(1, BLOCKS + 1), True, False)
    totals = products(v0, v1, v2, range(2, BLOCKS), (jnp.zeros((8, LANES), f32),) * 6)
    for i in range(6):
        totals_out[i] = totals[i]


def inner(ext, lext, r_even, r_odd):
    field = near((BLOCKS + 2, ROWS, LANES))
    return pl.pallas_call(
        inner_kernel,
        out_shape=(
            near((K, BLOCKS + 2, ROWS, LANES)),
            near((BLOCKS + 2, ROWS, LANES), jnp.int32),
            field,
            field,
            field,
            near((6, 8, LANES)),
        ),
        in_specs=[WHOLE] * 4,
        out_specs=(WHOLE,) * 6,
        input_output_aliases={0: 0, 1: 1},
        compiler_params=LIMIT,
        cost_estimate=cost(3),
        name="inner_fields",
    )(*held(ext, lext, r_even, r_odd))


def outer_kernel(
    ext_in, lext_in, v0_in, v1_in, v2_in, totals_in, c_even, c_odd, ext, lext, v0, v1, v2, sums_out
):
    del ext_in, lext_in, v0_in, v1_in, v2_in
    _, col = place()
    col_even = (col % 2) == 0
    for side, j in ((0, 0), (1, BLOCKS + 1)):
        e, o = c_even[...], c_odd[...]
        got = jnp.where(col_even, o, e) if side == 0 else jnp.where(col_even, e, o)
        for k in range(K + 1):
            shift = (LANES - HALO - HALO * k) if side == 0 else (LANES - HALO * k) % LANES
            moved = pltpu.roll(got, shift, 1) if shift else got
            for start, size, value in (
                (TOP, H, moved[:H]),
                (TOP - HALO, HALO, moved[H : H + HALO]),
                (TOP + H, HALO, moved[H + HALO :]),
            ):
                if k < K:
                    ext[k, j, pl.ds(start, size), :] = value
                else:
                    lext[j, pl.ds(start, size), :] = value.astype(jnp.int32)
    last = BLOCKS + 1
    runs = ((0, 3, (0, 1)), (last - 2, 3, (last - 1, last)))
    blocks = (0, 1, last - 1, last)
    right_side(ext, lext, v0, runs)
    clear_outside(v0, blocks, True, True)
    neighbours(v0, v1, runs)
    clear_outside(v1, blocks, True, True)
    neighbours(v1, v2, runs)
    clear_outside(v2, blocks, True, True)
    totals = products(v0, v1, v2, (1, BLOCKS), tuple(totals_in[i] for i in range(6)))

    lane = iota((8, LANES), 1)
    line = jnp.zeros((8, LANES), f32)
    for i in range(6):
        x = totals[i] + totals[i] if i == 5 else totals[i]
        big = 512.0 * jnp.max(jnp.abs(x), axis=1, keepdims=True)
        high = (x + big) - big
        line = jnp.where(
            (lane == i) | (lane == i + 16),
            jnp.sum(high, axis=1, keepdims=True),
            jnp.where(lane == i + 8, jnp.sum(x - high, axis=1, keepdims=True), line),
        )
    s, e = line, jnp.zeros_like(line)
    for shift in (4, 2, 1):
        s, more = two_sum(s, pltpu.roll(s, shift, 0))
        e = e + pltpu.roll(e, shift, 0) + more
    sums_out[...] = jnp.broadcast_to(jnp.where(lane < 16, s, e)[:1], (256, LANES))


def outer(ext, lext, v0, v1, v2, totals, c_even, c_odd):
    field = near((BLOCKS + 2, ROWS, LANES))
    return pl.pallas_call(
        outer_kernel,
        out_shape=(
            near((K, BLOCKS + 2, ROWS, LANES)),
            near((BLOCKS + 2, ROWS, LANES), jnp.int32),
            field,
            field,
            field,
            near((256, LANES)),
        ),
        in_specs=[WHOLE] * 8,
        out_specs=(WHOLE,) * 6,
        input_output_aliases={i: i for i in range(5)},
        compiler_params=LIMIT,
        cost_estimate=cost(2),
        name="outer_fields",
    )(*held(ext, lext, v0, v1, v2, totals, c_even, c_odd))[2:]


def pool_kernel(v0, v1, v2, out):
    spread = jnp.where(iota((512, LANES), 0) // 4 == iota((512, LANES), 1), f32(0.0625), f32(0.0))
    for i, ref in enumerate((v0, v1, v2)):
        for g in range(2):
            parts = []
            for j in range(4):
                block = 1 + 4 * g + j
                at = [ref[block, pl.ds(TOP + q, H // 4, stride=4), :] for q in range(4)]
                parts.append((at[0] + at[1]) + (at[2] + at[3]))
            out[i, g] = jnp.dot(
                jnp.concatenate(parts, 1), spread, precision=lax.Precision.HIGHEST, preferred_element_type=f32
            )


def pool(v0, v1, v2):
    return pl.pallas_call(
        pool_kernel,
        out_shape=near((3, 2, H // 4, LANES)),
        in_specs=[WHOLE] * 3,
        out_specs=WHOLE,
        compiler_params=LIMIT,
        cost_estimate=cost(2),
        name="pool_fields",
    )(*held(v0, v1, v2))


def two_product(a, b):
    p = a * b
    big = f32(4097.0)
    t = big * a
    ah = t - (t - a)
    al = a - ah
    t = big * b
    bh = t - (t - b)
    bl = b - bh
    return p, ((ah * bh - p) + ah * bl + al * bh) + al * bl


def less_scaled(a, b, scale):
    p, low = two_product(b[0], scale)
    low = low + b[1] * scale
    s, e = two_sum(a[0], -p)
    e = e + (a[1] - low)
    return two_sum(s, e)


def coefficients(n):
    shift = n[1][0] / n[0][0]
    current = n
    m = [n[0][0]]
    for _ in range(5):
        current = [less_scaled(current[i + 1], current[i], shift) for i in range(len(current) - 1)]
        m.append(current[0][0] + current[0][1])
    m0, m1, m2, m3, m4, m5 = m
    t = m1 / m0
    theta0 = shift + t
    m5 = m5 - 5.0 * t * m4
    m4 = m4 - 4.0 * t * m3
    m3 = m3 - 3.0 * t * m2
    m2 = m2 - t * m1
    one = jnp.ones_like(m0)
    zero = jnp.zeros_like(m0)
    second = m2 > 0.0
    safe2 = jnp.where(second, m2, one)
    b1 = jnp.where(second, m2 / m0, zero)
    s = jnp.where(second, m3 / safe2, zero)
    h2 = m4 - s * m3 - b1 * m2
    third = second & (h2 > 0.0)
    safe3 = jnp.where(third, h2, one)
    theta1 = theta0 + s
    theta2 = theta0 - s + (m5 - s * m4 - b1 * m3) / safe3
    b2 = h2 / safe2
    d0, d1, d2 = 4.0 - theta0, 4.0 - theta1, 4.0 - theta2
    e = d1 * d2 - b2
    y2 = jnp.where(third, one / (d0 * e - b1 * d2), zero)
    y1 = jnp.where(third, d2 * y2, jnp.where(second, one / (d0 * d1 - b1), zero))
    y0 = jnp.where(third, e * y2, jnp.where(second, d1 * y1, one / d0))
    return (
        y0 - theta0 * y1 + (theta0 * theta1 - b1) * y2,
        y1 - (theta0 + theta1) * y2,
        y2,
    )


def solve_kernel(all_sums, pooled, coef_out, mid_out):
    tiles = [(all_sums[pl.ds(8 * i, 8), :], jnp.zeros((8, LANES), f32)) for i in range(32)]
    while len(tiles) > 1:
        merged = []
        for a, b in zip(tiles[0::2], tiles[1::2]):
            s, e = two_sum(a[0], b[0])
            merged.append((s, e + (a[1] + b[1])))
        tiles = merged
    s, e = tiles[0]
    for shift in (4, 2, 1):
        s, more = two_sum(s, pltpu.roll(s, shift, 0))
        e = e + pltpu.roll(e, shift, 0) + more
    lane = iota((8, LANES), 1)
    zero = jnp.zeros((8, LANES), f32)

    def over_lanes(x):
        return jnp.broadcast_to(jnp.sum(x, axis=1, keepdims=True), (8, LANES))

    n = []
    for i in range(6):
        high = over_lanes(jnp.where(lane == i, s, zero))
        low = over_lanes(jnp.where((lane == i + 8) | (lane == i + 16), s, jnp.where(lane == i, e, zero)))
        n.append(two_sum(high, low))
    c = coefficients(n)
    for i in range(3):
        coef_out[i] = c[i]
    for g in range(2):
        for q in range(H // 4 // 8):
            at = (g, pl.ds(8 * q, 8), slice(None))
            value = c[0] * pooled[(0, *at)] + c[1] * pooled[(1, *at)] + c[2] * pooled[(2, *at)]
            for d in range(16):
                mid_out[(d, *at)] = value


def solve(all_sums, pooled):
    return pl.pallas_call(
        solve_kernel,
        out_shape=(near((3, 8, LANES)), near((16, 2, H // 4, LANES))),
        in_specs=[WHOLE] * 2,
        out_specs=(WHOLE,) * 2,
        compiler_params=LIMIT,
        cost_estimate=cost(1),
        name="coefficients",
    )(*held(all_sums, pooled))


def half_matrix(rows):
    return jnp.where(iota((rows, rows // 2), 0) // 2 == iota((rows, rows // 2), 1), f32(0.25), f32(0.0))


def blend_kernel(coef, v0, v1, v2, blended_out, fine_out, scratch):
    c = [coef[i] for i in range(3)]

    def step(t, carry):
        for u in range(4):
            base = pl.multiple_of(32 * t + 8 * u, 8)
            for j in range(BLOCKS):
                at = (j + 1, pl.ds(base + TOP, 8), slice(None))
                value = c[0] * v0[at] + c[1] * v1[at] + c[2] * v2[at]
                blended_out[pl.ds(base, 8), pl.ds(j * LANES, LANES)] = value
                scratch[j, pl.ds(base, 8), :] = value
        return carry

    lax.fori_loop(0, H // 32, step, 0)
    half = half_matrix(2 * LANES)
    for g in range(BLOCKS // 2):
        parts = [
            scratch[2 * g + i, pl.ds(0, H // 2, stride=2), :] + scratch[2 * g + i, pl.ds(1, H // 2, stride=2), :]
            for i in range(2)
        ]
        fine_out[:, pl.ds(g * LANES, LANES)] = jnp.dot(
            jnp.concatenate(parts, 1), half, precision=lax.Precision.HIGHEST, preferred_element_type=f32
        )


def blend(coef, v0, v1, v2):
    return pl.pallas_call(
        blend_kernel,
        out_shape=(
            jax.ShapeDtypeStruct((H, W), f32),
            jax.ShapeDtypeStruct((H // 2, W // 2), f32),
        ),
        in_specs=[WHOLE] * 4,
        out_specs=(WHOLE,) * 2,
        scratch_shapes=[pltpu.VMEM((BLOCKS, H, LANES), f32)],
        compiler_params=LIMIT,
        cost_estimate=cost(3),
        name="blend",
    )(*held(coef, v0, v1, v2))


def assemble_kernel(own, other, mid_out, coarse_out, scratch, sem):
    core = lax.axis_index("row_2")
    half = half_matrix(2 * LANES)
    copies = []
    for i, (x, c) in enumerate(((own, core), (other, 1 - core))):
        for g in range(2):
            copy = pltpu.make_async_copy(
                x.at[:, g], mid_out.at[:, c, :, pl.ds(g * LANES, LANES)], sem.at[i, g]
            )
            copy.start()
            copies.append(copy)
    rows = H // 8
    for x, c in ((own, core), (other, 1 - core)):
        parts = [
            jnp.concatenate(
                [x[d, g, pl.ds(0, rows, stride=2), :] + x[d, g, pl.ds(1, rows, stride=2), :] for d in range(16)], 0
            )
            for g in range(2)
        ]
        pooled = jnp.dot(
            jnp.concatenate(parts, 1), half, precision=lax.Precision.HIGHEST, preferred_element_type=f32
        )
        for d in range(16):
            scratch[d, c] = pooled[d * rows : (d + 1) * rows]
    copy = pltpu.make_async_copy(scratch, coarse_out, sem.at[2, 0])
    copy.start()
    copies.append(copy)
    for copy in copies:
        copy.wait()


def assemble(own, other):
    mid, coarse = pl.pallas_call(
        assemble_kernel,
        out_shape=(
            jax.ShapeDtypeStruct((16, 2, H // 4, W // 4), f32),
            jax.ShapeDtypeStruct((16, 2, H // 8, W // 8), f32),
        ),
        in_specs=[WHOLE] * 2,
        out_specs=(FAR,) * 2,
        scratch_shapes=[
            pltpu.VMEM((16, 2, H // 8, LANES), f32),
            pltpu.SemaphoreType.DMA((3, 2)),
        ],
        compiler_params=LIMIT,
        cost_estimate=cost(2),
        name="assemble",
    )(*held(own, other))
    return mid.reshape(8 * H, W // 4), coarse.reshape(4 * H, W // 8)


def swaps(devices, first):
    pairs = [(i, i + 1) for i in range(first, devices - 1, 2)]
    return pairs + [(b, a) for a, b in pairs]


def exchange(even, odd, axis):
    devices = lax.axis_size(axis)
    return lax.ppermute(even, axis, swaps(devices, 0)), lax.ppermute(odd, axis, swaps(devices, 1))


def per_device(sources, labels):
    r_even, r_odd = exchange(*pack_rows(sources, labels), ROW)
    ext, lext, left, right = load(sources, labels)
    c_even, c_odd = exchange(*pack_columns(r_even, r_odd, left, right), "col")
    ext, lext, v0, v1, v2, totals = inner(ext, lext, r_even, r_odd)
    v0, v1, v2, sums = outer(ext, lext, v0, v1, v2, totals, c_even, c_odd)
    pooled = pool(v0, v1, v2)
    sums = lax.all_to_all(sums.reshape(256, 1, LANES), ALL, split_axis=0, concat_axis=0, tiled=True)
    coef, mid = solve(sums.reshape(256, LANES), pooled)
    mid = lax.all_to_all(mid, CHIP, split_axis=0, concat_axis=0, tiled=True)
    other = lax.ppermute(mid, "row_2", [(0, 1), (1, 0)])
    blended, fine = blend(coef, v0, v1, v2)
    overview_mid, overview_coarse = assemble(mid, other)
    return (blended, fine, overview_mid, overview_coarse)


def solution(mesh):
    finer = Mesh(
        mesh.devices.reshape(4, 4, 2, mesh.shape["col"]), ("row_0", "row_1", "row_2", "col")
    )
    return jax.shard_map(
        per_device,
        mesh=finer,
        in_specs=(P(None, ROW, "col"), P(ROW, "col")),
        out_specs=(P(ROW, "col"), P(ROW, "col"), P(None, "col"), P(None, "col")),
        check_vma=False,
    )
```

time: 86.4 us -> 67.5 us (0.78)
  blocking collectives: 45.2 us -> 13.2 us
  starting transfers between devices: 7.66 us -> 25.3 us
  Pallas kernels: 23 us -> 13.5 us
  waiting for transfers between devices: 6.56 us -> 14.3 us
  local copies, waits for them, and re-layouts: 2.67 us -> 0 us
    all_to_all x1 -> x0, blocking collectives: 31 us -> none  [per_device(): lax.all_to_all(sums.reshape(256, 1, LANES), ALL, split_axis=0, concat_axi...]
    all_to_all x0 -> x1, starting transfers between devices: none -> 17.4 us  [per_device(): lax.all_to_all(sums.reshape(256, 1, LANES), ALL, split_axis=0, concat_axi...]
    all_to_all x0 -> x1, waiting for transfers between devices: none -> 12.2 us  [per_device(): lax.all_to_all(sums.reshape(256, 1, LANES), ALL, split_axis=0, concat_axi...]
    pallas_call x5 -> x8, Pallas kernels: 20.1 us -> 12.4 us  [the longest x1 3.64 us: outer(): pl.pallas_call(outer_kernel, out_shape=(near((K, BLOCKS + 2, ROWS, LANES)...]
    ppermute x2, waiting for transfers between devices: 2.71 us -> 0.01 us  [exchange(): lax.ppermute(even, axis, swaps(devices, 0))]
    unnamed x12 -> x0, local copies, waits for them, and re-layouts: 2.67 us -> none
    ppermute x2, waiting for transfers between devices: 3.85 us -> 1.77 us  [exchange(): lax.ppermute(odd, axis, swaps(devices, 1))]
    pallas_call x1, Pallas kernels: 2.97 us -> 1.17 us  [blend(): pl.pallas_call(blend_kernel, out_shape=(jax.ShapeDtypeStruct((H, W), f32)...]
  transfers between devices with their start and end apart: 5 -> 6, of which waited for: 2 -> 3; matrix products, arithmetic and copies ran while one was open for 0% -> 0% of each run, Pallas kernels for 3% -> 11%
where the time goes in v2:
time: 67.5 us; the launch traced here: 67.1 us
  starting transfers between devices  25.3 us (37%)
  waiting for transfers between devices  14.3 us (21%)
  Pallas kernels  13.5 us (20%)
  blocking collectives  13.2 us (20%)
  between operations  0.73 us (1%)
    all_to_all x1, starting transfers between devices, per_device(): lax.all_to_all(sums.reshape(256, 1, LANES), ALL, split_axis=0, concat_axi...  17.4 us
    all_to_all x1, blocking collectives, per_device(): mid = lax.all_to_all(mid, CHIP, split_axis=0, concat_axis=0, tiled=True)  13.2 us
    all_to_all x1, waiting for transfers between devices, per_device(): lax.all_to_all(sums.reshape(256, 1, LANES), ALL, split_axis=0, concat_axi...  12.2 us
    pallas_call x1, Pallas kernels, outer(): pl.pallas_call(outer_kernel, out_shape=(near((K, BLOCKS + 2, ROWS, LANES)...  3.64 us
    ppermute x2, starting transfers between devices, exchange(): lax.ppermute(even, axis, swaps(devices, 0))  3.33 us
    pallas_call x1, Pallas kernels, inner(): pl.pallas_call(inner_kernel, out_shape=(near((K, BLOCKS + 2, ROWS, LANES)...  3.3 us
    ppermute x2, starting transfers between devices, exchange(): lax.ppermute(odd, axis, swaps(devices, 1))  2.57 us
    ppermute x1, starting transfers between devices, per_device(): other = lax.ppermute(mid, 'row_2', [(0, 1), (1, 0)])  2.06 us
  transfers between devices with their start and end apart: 6, of which 3 were waited for; matrix products, arithmetic and copies ran while one was open for 0% of the time, Pallas kernels for 11%

profile of v2, /device:TPU:1, one launch (start us, length us, event | category | flops | bytes accessed | tf_op | source)
XLA Modules:
  0.0 67.1 jit_solution(14068464641626047869)
XLA Ops:
  0.6 1.0 %pack_rows.1 = (f32[16,1024]{1,0:T(8,128)S(1)}, f32[16,1024]{1,0:T(8,128)S(1)}) custom-call(f32[3,128,1024]{2,1,0:T(8,128)} %src.3, s32[128,1024]{1,0:T(8,128)} %lab.3), custom_call_target="tpu_custom_call" | custom-call | flops 300000000 | tf_op jit(solution)/shard_map/pack_rows/pallas_call | solution.py:96
  1.7 3.3 %collective-permute-start = (f32[16,1024]{1,0:T(8,128)S(1)}, f32[16,1024]{1,0:T(8,128)S(1)}, u32[]{:S(2)}, u32[]{:S(2)}) collective-permute-start(f32[16,1024]{1,0:T(8,128)S(1)} %get-tuple-element.30), channel_id=1, source_target_pairs={{0,8},{16,24},{32,40},{48,56},{64,72},{80,88},{96,104},{112,120},{... | collective-permute-start | bytes 196616 | tf_op jit(solution)/shard_map/ppermute | solution.py:652
  5.0 1.9 %collective-permute-start.1 = (f32[16,1024]{1,0:T(8,128)S(1)}, f32[16,1024]{1,0:T(8,128)S(1)}, u32[]{:S(2)}, u32[]{:S(2)}) collective-permute-start(f32[16,1024]{1,0:T(8,128)S(1)} %get-tuple-element.31), channel_id=1, source_target_pairs={{8,16},{24,32},{40,48},{56,64},{72,80},{88,96},{104,112},{120,128}... | collective-permute-start | bytes 196616 | tf_op jit(solution)/shard_map/ppermute | solution.py:652
  6.9 1.9 %load_block.1 = (f32[3,10,160,128]{3,2,1,0:T(8,128)S(1)}, s32[10,160,128]{2,1,0:T(8,128)S(1)}, f32[128,128]{1,0:T(8,128)S(1)}, f32[128,128]{1,0:T(8,128)S(1)}) custom-call(f32[3,128,1024]{2,1,0:T(8,128)} %src.3, s32[128,1024]{1,0:T(8,128)} %lab.3), custom_call_target="tpu_custom_call" | custom-call | flops 600000000 | tf_op jit(solution)/shard_map/load_block/pallas_call | solution.py:135
  8.7 0.0 collective-permute-done.r_even.got_even
  8.8 1.8 %collective-permute-done.1.r_odd.got_odd = f32[16,1024]{1,0:T(8,128)S(1)} collective-permute-done((f32[16,1024]{1,0:T(8,128)S(1)}, f32[16,1024]{1,0:T(8,128)S(1)}, u32[]{:S(2)}, u32[]{:S(2)}) %collective-permute-start.1) | collective-permute-done | bytes 65568 | tf_op jit(solution)/shard_map/ppermute | solution.py:652
  10.5 0.1 pack_columns.1
  10.6 0.0 collective-permute-start.2
  10.7 0.7 collective-permute-start.3
  11.3 3.3 %inner_fields.1 = (f32[3,10,160,128]{3,2,1,0:T(8,128)S(1)}, s32[10,160,128]{2,1,0:T(8,128)S(1)}, f32[10,160,128]{2,1,0:T(8,128)S(1)}, f32[10,160,128]{2,1,0:T(8,...) custom-call(f32[3,10,160,128]{3,2,1,0:T(8,128)S(1)} %get-tuple-eleme, ...), custom_call_target="tpu_custom_call", output_to_operand_aliasing={{0}: (0, {}), {1}: (1, {})} | custom-call | flops 900000000 | tf_op jit(solution)/shard_map/inner_fields/pallas_call | solution.py:329
  14.7 0.0 collective-permute-done.2.c_even
  14.7 0.0 collective-permute-done.3.c_odd
  14.7 3.6 %outer_fields.1 = (f32[3,10,160,128]{3,2,1,0:T(8,128)S(1)}, s32[10,160,128]{2,1,0:T(8,128)S(1)}, f32[10,160,128]{2,1,0:T(8,128)S(1)}, f32[10,160,128]{2,1,0:T(8,...) custom-call(f32[3,10,160,128]{3,2,1,0:T(8,128)S(1)} %get-tuple-eleme, ...), custom_call_target="tpu_custom_call", output_to_operand_aliasing={{0}: (0, {}), {1}: (1, {}), {2}: (2, {}), {3}: (3, {}), {4}... | custom-call | flops 600000000 | tf_op jit(solution)/shard_map/outer_fields/pallas_call | solution.py:400
  18.3 17.4 %all-to-all-start = ((f32[256,1,128]{2,1,0:T(1,128)}), f32[256,1,128]{2,1,0:T(1,128)S(1)}, u32[]{:S(2)}, u32[]{:S(2)}) async-start(f32[256,1,128]{2,1,0:T(1,128)} %bitcast.1), calls=%async_computation | async-start | bytes 262144 | tf_op jit(solution)/shard_map/all_to_all | solution.py:662
  35.7 0.8 %pool_fields.1.pooled = f32[3,2,32,128]{3,2,1,0:T(8,128)S(1)} custom-call(f32[10,160,128]{2,1,0:T(8,128)S(1)} %get-tuple-element.43.v0, f32[10,160,128]{2,1,0:T(8,128)S(1)} %get-tuple-element.44.v1, f32[10,160,128]{2,1,0:T(8,128)S(1)} %get-tuple-element.45.v2), custom_call_target="tpu_custom_call" | custom-call | flops 600000000 | tf_op jit(solution)/shard_map/pool_fields/pallas_call | solution.py:434
  36.5 12.2 %all-to-all-done = f32[256,1,128]{2,1,0:T(1,128)S(1)} async-done(((f32[256,1,128]{2,1,0:T(1,128)}), f32[256,1,128]{2,1,0:T(1,128)S(1)}, u32[]{:S(2)}, u32[]{:S(2)}) %all-to-all-start) | async-done | bytes 131104 | tf_op jit(solution)/shard_map/all_to_all | solution.py:662
  48.7 0.3 coefficients.1
  48.9 13.2 %all_to_all.10.own = f32[16,2,32,128]{3,2,1,0:T(8,128)S(1)} all-to-all(f32[16,2,32,128]{3,2,1,0:T(8,128)S(1)} %get-tuple-element.49), channel_id=1, replica_groups=mesh['row_0'=4,'row_1'=4,'row_2'=2,'col'=8] {'row_0','row_1'}, dimensions={0} | all-to-all | bytes 1048576 | tf_op jit(solution)/shard_map/all_to_all | solution.py:664
  62.2 2.1 %collective-permute-start.4 = (f32[16,2,32,128]{3,2,1,0:T(8,128)S(1)}, f32[16,2,32,128]{3,2,1,0:T(8,128)S(1)}, u32[]{:S(2)}, u32[]{:S(2)}) collective-permute-start(f32[16,2,32,128]{3,2,1,0:T(8,128)S(1)} %all_to_all.10.own), channel_id=1, source_target_pairs={{0,8},{8,0},{1,9},{9,1},{2,10},{10,2},{3,11},{11,3},{4,12},{12,4},... | collective-permute-start | bytes 1572872 | tf_op jit(solution)/shard_map/ppermute | solution.py:665
  64.2 1.2 %blend.1 = (f32[128,1024]{1,0:T(8,128)}, f32[64,512]{1,0:T(8,128)}) custom-call(f32[3,8,128]{2,1,0:T(8,128)S(1)} %get-tuple-element.46.coef, f32[10,160,128]{2,1,0:T(8,128)S(1)} %get-tuple-element.43.v0, f32[10,160,128]{2,1,0:T(8,128)S(1)} %get-tuple-element.44.v1, f32[10,160,128]{2,1,0:T(8,128)S(1)} %get-tuple-element.45.v2), custom_call_target="tpu_custom_call" | custom-call | flops 900000000 | tf_op jit(solution)/shard_map/blend/pallas_call | solution.py:579
  65.4 0.4 collective-permute-done.4.other
  65.8 1.4 %assemble.1 = (f32[16,2,32,256]{3,2,1,0:T(8,128)}, f32[16,2,16,128]{3,2,1,0:T(8,128)}) custom-call(f32[16,2,32,128]{3,2,1,0:T(8,128)S(1)} %all_to_all.10.own, f32[16,2,32,128]{3,2,1,0:T(8,128)S(1)} %collective-permute-done.4.other), custom_call_target="tpu_custom_call" | custom-call | flops 600000000 | tf_op jit(solution)/shard_map/assemble/pallas_call | solution.py:626
Async XLA Ops:
  1.7 7.1 %collective-permute-start = (f32[16,1024]{1,0:T(8,128)S(1)}, f32[16,1024]{1,0:T(8,128)S(1)}, u32[]{:S(2)}, u32[]{:S(2)}) collective-permute-start(f32[16,1024]{1,0:T(8,128)S(1)} %get-tuple-element.30), channel_id=1, source_target_pairs={{0,8},{16,24},{32,40},{48,56},{64,72},{80,88},{96,104},{112,120},{... | collective-permute-start | bytes 196616 | tf_op jit(solution)/shard_map/ppermute | solution.py:652
  5.0 5.6 %collective-permute-start.1 = (f32[16,1024]{1,0:T(8,128)S(1)}, f32[16,1024]{1,0:T(8,128)S(1)}, u32[]{:S(2)}, u32[]{:S(2)}) collective-permute-start(f32[16,1024]{1,0:T(8,128)S(1)} %get-tuple-element.31), channel_id=1, source_target_pairs={{8,16},{24,32},{40,48},{56,64},{72,80},{88,96},{104,112},{120,128}... | collective-permute-start | bytes 196616 | tf_op jit(solution)/shard_map/ppermute | solution.py:652
  10.6 4.0 %collective-permute-start.2 = (f32[136,128]{1,0:T(8,128)S(1)}, f32[136,128]{1,0:T(8,128)S(1)}, u32[]{:S(2)}, u32[]{:S(2)}) collective-permute-start(f32[136,128]{1,0:T(8,128)S(1)} %get-tuple-element.40), channel_id=1, source_target_pairs={{0,1},{2,3},{4,5},{6,7},{1,0},{3,2},{5,4},{7,6},{8,9},{10,11},{12,... | collective-permute-start | bytes 208904 | tf_op jit(solution)/shard_map/ppermute | solution.py:652
  10.7 4.0 %collective-permute-start.3 = (f32[136,128]{1,0:T(8,128)S(1)}, f32[136,128]{1,0:T(8,128)S(1)}, u32[]{:S(2)}, u32[]{:S(2)}) collective-permute-start(f32[136,128]{1,0:T(8,128)S(1)} %get-tuple-element.41), channel_id=1, source_target_pairs={{1,2},{3,4},{5,6},{2,1},{4,3},{6,5},{9,10},{11,12},{13,14},{10,9},... | collective-permute-start | bytes 208904 | tf_op jit(solution)/shard_map/ppermute | solution.py:652
  18.3 30.3 %all-to-all-start = ((f32[256,1,128]{2,1,0:T(1,128)}), f32[256,1,128]{2,1,0:T(1,128)S(1)}, u32[]{:S(2)}, u32[]{:S(2)}) async-start(f32[256,1,128]{2,1,0:T(1,128)} %bitcast.1), calls=%async_computation | async-start | bytes 262144 | tf_op jit(solution)/shard_map/all_to_all | solution.py:662
  62.2 3.6 %collective-permute-start.4 = (f32[16,2,32,128]{3,2,1,0:T(8,128)S(1)}, f32[16,2,32,128]{3,2,1,0:T(8,128)S(1)}, u32[]{:S(2)}, u32[]{:S(2)}) collective-permute-start(f32[16,2,32,128]{3,2,1,0:T(8,128)S(1)} %all_to_all.10.own), channel_id=1, source_target_pairs={{0,8},{8,0},{1,9},{9,1},{2,10},{10,2},{3,11},{11,3},{4,12},{12,4},... | collective-permute-start | bytes 1572872 | tf_op jit(solution)/shard_map/ppermute | solution.py:665

commit v3 on v2

--- a/solution.py
+++ b/solution.py
@@ -9,7 +9,7 @@
 K = 3
 H, W = 128, 1024
 TOP = 16
-ROWS = TOP + H + 16
+ROWS = TOP + H + 24
 LANES = 128
 BLOCKS = W // LANES
 HALO = 4
@@ -21,6 +21,9 @@
 FAR = pl.BlockSpec(memory_space=pltpu.MemorySpace.HBM)
 LIMIT = pltpu.CompilerParams(vmem_limit_bytes=24 * 2**20)
 CHUNK = 3
+TILES = H // 8
+LEFT, RIGHT = HALO, 64
+SEAM = 12
 f32 = jnp.float32
 
 
@@ -47,15 +50,6 @@
 
 def cost(us):
     return pl.CostEstimate(flops=int(us * 3e8), bytes_accessed=0, transcendentals=0)
-
-
-def merge_strips(parts, side, lane):
-    total = jnp.zeros_like(parts[0])
-    for k in range(K + 1):
-        shift = HALO * k + (HALO if side else 0)
-        moved = pltpu.roll(parts[k], shift, 1) if shift else parts[k]
-        total = jnp.where((lane >= HALO * k) & (lane < HALO * (k + 1)), moved, total)
-    return total
 
 
 def pack_kernel(src, lab, even_out, odd_out, rows, lrows, sem):
@@ -109,24 +103,38 @@
     )(*far(sources, labels))
 
 
+def window(lane, start, size):
+    return (lane >= start) & (lane < start + size)
+
+
+def turn(x, shift):
+    shift %= LANES
+    return pltpu.roll(x, shift, 1) if shift else x
+
+
 def load_kernel(src, lab, ext, lext, left_out, right_out, sem):
     copies = {}
     for j in (0, BLOCKS - 1, *range(1, BLOCKS - 1)):
         lanes = pl.ds(j * LANES, LANES)
         for k in range(K + 1):
             a = src.at[k, :, lanes] if k < K else lab.at[:, lanes]
-            b = ext.at[k, j + 1, pl.ds(TOP, H), :] if k < K else lext.at[j + 1, pl.ds(TOP, H), :]
+            b = ext.at[k, j, pl.ds(TOP, H), :] if k < K else lext.at[j, pl.ds(TOP, H), :]
             c = pltpu.make_async_copy(a, b, sem.at[k, j])
             c.start()
             copies[k, j] = c
-    own = pl.ds(TOP, H)
-    lane = iota((H, LANES), 1)
-    for side, out in ((0, left_out), (1, right_out)):
-        j = side * (BLOCKS - 1)
+    lane = iota((8, LANES), 1)
+    for j, out, first in ((0, left_out, 0), (BLOCKS - 1, right_out, LANES - HALO)):
         for k in range(K + 1):
             copies.pop((k, j)).wait()
-        parts = [ext[k, j + 1, own, :] for k in range(K)] + [lext[j + 1, own, :].astype(f32)]
-        out[...] = merge_strips(parts, side, lane)
+        for half in range(2):
+            total = jnp.zeros((8, LANES), f32)
+            for g in range(8):
+                at = pl.ds(TOP + 64 * half + 8 * g, 8)
+                for k in range(K + 1):
+                    x = ext[k, j, at, :] if k < K else lext[j, at, :].astype(f32)
+                    to = 16 * g + HALO * k
+                    total = jnp.where(window(lane, to, HALO), turn(x, to - first), total)
+            out[pl.ds(8 * half, 8), :] = total
     for c in copies.values():
         c.wait()
 
@@ -135,10 +143,10 @@
     return pl.pallas_call(
         load_kernel,
         out_shape=(
-            near((K, BLOCKS + 2, ROWS, LANES)),
-            near((BLOCKS + 2, ROWS, LANES), jnp.int32),
-            near((H, LANES)),
-            near((H, LANES)),
+            near((K, BLOCKS, ROWS, LANES)),
+            near((BLOCKS, ROWS, LANES), jnp.int32),
+            near((16, LANES)),
+            near((16, LANES)),
         ),
         in_specs=[FAR] * 2,
         out_specs=(WHOLE,) * 4,
@@ -156,8 +164,8 @@
     upper = iota((8, LANES), 0) < HALO
     lane = iota((8, LANES), 1)
     strips = []
-    for side, start in ((0, 0), (1, W - LANES)):
-        parts = []
+    for start, first in ((0, 0), (W - LANES, LANES - HALO)):
+        total = jnp.zeros((8, LANES), f32)
         for k in range(K + 1):
             tile, half = divmod(k, 2)
             at = (pl.ds(8 * tile, 8), pl.ds(start, LANES))
@@ -165,20 +173,21 @@
             above = jnp.where(row_even, o, e)
             below = jnp.where(row_even, e, o)
             if half:
-                parts.append(jnp.where(upper, pltpu.roll(above, HALO, 0), below))
+                both = jnp.where(upper, pltpu.roll(above, HALO, 0), below)
             else:
-                parts.append(jnp.where(upper, above, pltpu.roll(below, HALO, 0)))
-        strips.append(merge_strips(parts, side, lane))
-    even_out[pl.ds(0, H), :] = jnp.where(col_even, right[...], left[...])
-    odd_out[pl.ds(0, H), :] = jnp.where(col_even, left[...], right[...])
-    even_out[pl.ds(H, 8), :] = jnp.where(col_even, strips[1], strips[0])
-    odd_out[pl.ds(H, 8), :] = jnp.where(col_even, strips[0], strips[1])
+                both = jnp.where(upper, above, pltpu.roll(below, HALO, 0))
+            total = jnp.where(window(lane, HALO * k, HALO), turn(both, HALO * k - first), total)
+        strips.append(total)
+    even_out[pl.ds(0, 16), :] = jnp.where(col_even, right[...], left[...])
+    odd_out[pl.ds(0, 16), :] = jnp.where(col_even, left[...], right[...])
+    even_out[pl.ds(16, 8), :] = jnp.where(col_even, strips[1], strips[0])
+    odd_out[pl.ds(16, 8), :] = jnp.where(col_even, strips[0], strips[1])
 
 
 def pack_columns(got_even, got_odd, left, right):
     return pl.pallas_call(
         corner_kernel,
-        out_shape=(near((H + 8, LANES)),) * 2,
+        out_shape=(near((24, LANES)),) * 2,
         in_specs=[WHOLE] * 4,
         out_specs=(WHOLE,) * 2,
         compiler_params=LIMIT,
@@ -204,100 +213,86 @@
     return after, before
 
 
-def right_side(ext, lext, out, runs):
+PAIRS = ((0, 0), (0, 1), (1, 1), (1, 2), (2, 2), (2, 3))
+
+
+def right_side(ext, lext, out):
     def step(t, carry):
         for u in range(CHUNK):
             base = pl.multiple_of(TOP - 8 + 8 * (CHUNK * t + u), 8)
-            for start, count, keep in runs:
-                total = {j: jnp.zeros((8, LANES), f32) for j in keep}
-                picked = {j: lext[j, pl.ds(base, 8), :] for j in keep}
-                for k in range(K):
-                    tiles = [ext[k, start + i, pl.ds(base, 8), :] for i in range(count)]
-                    after, before = shifted(tiles)
-                    for j in keep:
-                        i = j - start
-                        vertical = ext[k, j, pl.ds(base + 1, 8), :] + ext[k, j, pl.ds(base - 1, 8), :]
-                        term = 4.0 * tiles[i] - (vertical + after[i] + before[i])
-                        total[j] = jnp.where(picked[j] == k, term, total[j])
-                for j in keep:
-                    out[j, pl.ds(base, 8), :] = total[j]
+            total = [jnp.zeros((8, LANES), f32)] * BLOCKS
+            picked = [lext[j, pl.ds(base, 8), :] for j in range(BLOCKS)]
+            for k in range(K):
+                tiles = [ext[k, j, pl.ds(base, 8), :] for j in range(BLOCKS)]
+                after, before = shifted(tiles)
+                for j in range(BLOCKS):
+                    vertical = ext[k, j, pl.ds(base + 1, 8), :] + ext[k, j, pl.ds(base - 1, 8), :]
+                    term = 4.0 * tiles[j] - (vertical + after[j] + before[j])
+                    total[j] = jnp.where(picked[j] == k, term, total[j])
+            for j in range(BLOCKS):
+                out[j, pl.ds(base, 8), :] = total[j]
         return carry
 
-    lax.fori_loop(0, (H // 8 + 2) // CHUNK, step, 0)
-
-
-def neighbours(source, target, runs):
+    lax.fori_loop(0, (TILES + 2) // CHUNK, step, 0)
+
+
+def neighbours(source, target):
     def step(t, carry):
         for u in range(2 * CHUNK):
             base = pl.multiple_of(TOP - 8 + 8 * (2 * CHUNK * t + u), 8)
-            for start, count, keep in runs:
-                tiles = [source[start + i, pl.ds(base, 8), :] for i in range(count)]
-                after, before = shifted(tiles)
-                for j in keep:
-                    i = j - start
-                    vertical = source[j, pl.ds(base + 1, 8), :] + source[j, pl.ds(base - 1, 8), :]
-                    target[j, pl.ds(base, 8), :] = vertical + after[i] + before[i]
+            tiles = [source[j, pl.ds(base, 8), :] for j in range(BLOCKS)]
+            after, before = shifted(tiles)
+            for j in range(BLOCKS):
+                vertical = source[j, pl.ds(base + 1, 8), :] + source[j, pl.ds(base - 1, 8), :]
+                target[j, pl.ds(base, 8), :] = vertical + after[j] + before[j]
         return carry
 
-    lax.fori_loop(0, (H // 8 + 2) // CHUNK // 2, step, 0)
-
-
-def products(v0, v1, v2, blocks, totals):
-    def step(t, carry):
-        totals = carry
+    lax.fori_loop(0, (TILES + 2) // CHUNK // 2, step, 0)
+
+
+def tree(x):
+    while len(x) > 1:
+        x = [sum(x[a : a + 2][1:], x[a]) for a in range(0, len(x), 2)]
+    return x[0]
+
+
+def products(v0, v1, v2):
+    lane = iota((8, LANES), 1)
+    last = lane == LANES - 1
+    kept = {0: lane >= HALO, BLOCKS - 1: lane < LANES - HALO}
+
+    def step(t, totals):
         for u in range(2):
             base = pl.multiple_of(TOP + 8 * (2 * t + u), 8)
             at = pl.ds(base, 8)
-            last = iota((8, LANES), 1) == LANES - 1
-            found = [[] for _ in range(6)]
-            rolled = {}
-            for j in blocks:
-                for i in (j, j + 1):
-                    if i not in rolled:
-                        rolled[i] = pltpu.roll(v2[i, at, :], LANES - 1, 1)
-                x0, x1, x2 = v0[j, at, :], v1[j, at, :], v2[j, at, :]
-                x3 = v2[j, pl.ds(base + 1, 8), :] + jnp.where(last, rolled[j + 1], rolled[j])
-                for i, (a, b) in enumerate(((x0, x0), (x0, x1), (x1, x1), (x1, x2), (x2, x2), (x2, x3))):
-                    found[i].append(a * b)
-            out = []
-            for i in range(6):
-                x = found[i]
-                while len(x) > 1:
-                    x = [sum(x[a : a + 2][1:], x[a]) for a in range(0, len(x), 2)]
-                out.append(totals[i] + x[0])
-            totals = tuple(out)
+            found = [[] for _ in PAIRS]
+            rolled = [turn(v2[j, at, :], -1) for j in range(BLOCKS)]
+            for j in range(BLOCKS):
+                x = [v[j, at, :] for v in (v0, v1, v2)]
+                right = jnp.where(last, rolled[min(j + 1, BLOCKS - 1)], rolled[j])
+                x.append(v2[j, pl.ds(base + 1, 8), :] + right)
+                own = [jnp.where(kept[j], a, 0.0) for a in x[:3]] if j in kept else x
+                for i, (a, b) in enumerate(PAIRS):
+                    found[i].append(own[a] * x[b])
+            totals = tuple(total + tree(f) for total, f in zip(totals, found))
         return totals
 
-    return lax.fori_loop(0, H // 16, step, totals)
-
-
-def clear_outside(ref, blocks, rows, columns):
-    row, col = place()
-    zero = jnp.zeros((8, LANES), f32)
-    if rows:
-
-        @pl.when(row == 0)
-        def _():
-            for j in blocks:
-                ref[j, pl.ds(TOP - 8, 8), :] = zero
-
-        @pl.when(row == 31)
-        def _():
-            for j in blocks:
-                ref[j, pl.ds(TOP + H, 8), :] = zero
-
-    if columns:
-
-        @pl.when(col == 0)
-        def _():
-            ref[0, :, :] = jnp.zeros((ROWS, LANES), f32)
-
-        @pl.when(col == 7)
-        def _():
-            ref[BLOCKS + 1, :, :] = jnp.zeros((ROWS, LANES), f32)
-
-
-def inner_kernel(ext_in, lext_in, r_even, r_odd, ext, lext, v0, v1, v2, totals_out):
+    return lax.fori_loop(0, TILES // 2, step, (jnp.zeros((8, LANES), f32),) * 6)
+
+
+def clear_rows(ref, row):
+    @pl.when(row == 0)
+    def _():
+        for j in range(BLOCKS):
+            ref[j, pl.ds(TOP - 8, 8), :] = jnp.zeros((8, LANES), f32)
+
+    @pl.when(row == 31)
+    def _():
+        for j in range(BLOCKS):
+            ref[j, pl.ds(TOP + H, 8), :] = jnp.zeros((8, LANES), f32)
+
+
+def inner_kernel(ext_in, lext_in, r_even, r_odd, ext, lext, v0, v1, v2, totals_out, seam_out):
     del ext_in, lext_in
     row, _ = place()
     row_even = (row % 2) == 0
@@ -309,75 +304,106 @@
             above, below = jnp.where(row_even, o, e), jnp.where(row_even, e, o)
             for start, value in ((TOP - HALO, above), (TOP + H, below)):
                 if k < K:
-                    ext[k, j + 1, pl.ds(start, HALO), :] = value
+                    ext[k, j, pl.ds(start, HALO), :] = value
                 else:
-                    lext[j + 1, pl.ds(start, HALO), :] = value.astype(jnp.int32)
-    runs = ((1, BLOCKS, range(1, BLOCKS + 1)),)
-    right_side(ext, lext, v0, runs)
-    clear_outside(v0, range(1, BLOCKS + 1), True, False)
-    neighbours(v0, v1, runs)
-    clear_outside(v1, range(1, BLOCKS + 1), True, False)
-    neighbours(v1, v2, runs)
-    clear_outside(v2, range(1, BLOCKS + 1), True, False)
-    totals = products(v0, v1, v2, range(2, BLOCKS), (jnp.zeros((8, LANES), f32),) * 6)
+                    lext[j, pl.ds(start, HALO), :] = value.astype(jnp.int32)
+    right_side(ext, lext, v0)
+    clear_rows(v0, row)
+    neighbours(v0, v1)
+    clear_rows(v1, row)
+    neighbours(v1, v2)
+    clear_rows(v2, row)
+    totals = products(v0, v1, v2)
     for i in range(6):
         totals_out[i] = totals[i]
+    lane = iota((8, LANES), 1)
+    for k in range(K + 1):
+        for t in range(TILES + 2):
+            at = pl.ds(TOP - 8 + 8 * t, 8)
+            a, b = [
+                ext[k, j, at, :] if k < K else lext[j, at, :].astype(f32) for j in (0, BLOCKS - 1)
+            ]
+            seam_out[k, at, :] = jnp.where(lane < 64, turn(a, LEFT), turn(b, RIGHT + SEAM))
 
 
 def inner(ext, lext, r_even, r_odd):
-    field = near((BLOCKS + 2, ROWS, LANES))
+    field = near((BLOCKS, ROWS, LANES))
     return pl.pallas_call(
         inner_kernel,
         out_shape=(
-            near((K, BLOCKS + 2, ROWS, LANES)),
-            near((BLOCKS + 2, ROWS, LANES), jnp.int32),
+            near((K, BLOCKS, ROWS, LANES)),
+            near((BLOCKS, ROWS, LANES), jnp.int32),
             field,
             field,
             field,
             near((6, 8, LANES)),
+            near((K + 1, ROWS, LANES)),
         ),
         in_specs=[WHOLE] * 4,
-        out_specs=(WHOLE,) * 6,
+        out_specs=(WHOLE,) * 7,
         input_output_aliases={0: 0, 1: 1},
         compiler_params=LIMIT,
         cost_estimate=cost(3),
         name="inner_fields",
-    )(*held(ext, lext, r_even, r_odd))
-
-
-def outer_kernel(
-    ext_in, lext_in, v0_in, v1_in, v2_in, totals_in, c_even, c_odd, ext, lext, v0, v1, v2, sums_out
-):
-    del ext_in, lext_in, v0_in, v1_in, v2_in
-    _, col = place()
+    )(*held(ext, lext, r_even, r_odd))[2:]
+
+
+def seam_kernel(base, totals_in, c_even, c_odd, w, sums_out, planes):
+    row, col = place()
     col_even = (col % 2) == 0
-    for side, j in ((0, 0), (1, BLOCKS + 1)):
-        e, o = c_even[...], c_odd[...]
-        got = jnp.where(col_even, o, e) if side == 0 else jnp.where(col_even, e, o)
+    lane = iota((8, LANES), 1)
+    from_left, from_right = lane < LEFT, window(lane, RIGHT + SEAM, HALO)
+    outside = (from_left & (col == 0)) | (from_right & (col == 7))
+    for t in range(TILES + 2):
+        at = pl.ds(TOP - 8 + 8 * t, 8)
+        corner = t in (0, TILES + 1)
+        tile, g = (2, 0) if corner else divmod(t - 1, 8)
+        e, o = c_even[pl.ds(8 * tile, 8), :], c_odd[pl.ds(8 * tile, 8), :]
+        a, b = jnp.where(col_even, o, e), jnp.where(col_even, e, o)
+        if corner:
+            a, b = pltpu.roll(a, HALO, 0), pltpu.roll(b, HALO, 0)
         for k in range(K + 1):
-            shift = (LANES - HALO - HALO * k) if side == 0 else (LANES - HALO * k) % LANES
-            moved = pltpu.roll(got, shift, 1) if shift else got
-            for start, size, value in (
-                (TOP, H, moved[:H]),
-                (TOP - HALO, HALO, moved[H : H + HALO]),
-                (TOP + H, HALO, moved[H + HALO :]),
-            ):
-                if k < K:
-                    ext[k, j, pl.ds(start, size), :] = value
-                else:
-                    lext[j, pl.ds(start, size), :] = value.astype(jnp.int32)
-    last = BLOCKS + 1
-    runs = ((0, 3, (0, 1)), (last - 2, 3, (last - 1, last)))
-    blocks = (0, 1, last - 1, last)
-    right_side(ext, lext, v0, runs)
-    clear_outside(v0, blocks, True, True)
-    neighbours(v0, v1, runs)
-    clear_outside(v1, blocks, True, True)
-    neighbours(v1, v2, runs)
-    clear_outside(v2, blocks, True, True)
-    totals = products(v0, v1, v2, (1, BLOCKS), tuple(totals_in[i] for i in range(6)))
-
-    lane = iota((8, LANES), 1)
+            lanes = 16 * g + HALO * k
+            planes[k, at, :] = jnp.where(
+                from_left,
+                turn(a, -lanes),
+                jnp.where(from_right, turn(b, RIGHT + SEAM - lanes), base[k, at, :]),
+            )
+
+    def put(i, t, value):
+        hidden = outside
+        if t == 0:
+            hidden = hidden | (row == 0)
+        if t == TILES + 1:
+            hidden = hidden | (row == 31)
+        w[i, pl.ds(TOP - 8 + 8 * t, 8), :] = jnp.where(hidden, 0.0, value)
+
+    for t in range(TILES + 2):
+        start = TOP - 8 + 8 * t
+        total = jnp.zeros((8, LANES), f32)
+        picked = planes[K, pl.ds(start, 8), :]
+        for k in range(K):
+            x = planes[k, pl.ds(start, 8), :]
+            vertical = planes[k, pl.ds(start + 1, 8), :] + planes[k, pl.ds(start - 1, 8), :]
+            term = 4.0 * x - (vertical + turn(x, -1) + turn(x, 1))
+            total = jnp.where(picked == k, term, total)
+        put(0, t, total)
+    for i in range(2):
+        for t in range(TILES + 2):
+            start = TOP - 8 + 8 * t
+            x = w[i, pl.ds(start, 8), :]
+            vertical = w[i, pl.ds(start + 1, 8), :] + w[i, pl.ds(start - 1, 8), :]
+            put(i + 1, t, vertical + turn(x, -1) + turn(x, 1))
+    own_lane = window(lane, LEFT, HALO) | window(lane, RIGHT + SEAM - HALO, HALO)
+    found = [[] for _ in PAIRS]
+    for t in range(TILES):
+        start = TOP + 8 * t
+        x = [w[i, pl.ds(start, 8), :] for i in range(3)]
+        x.append(w[2, pl.ds(start + 1, 8), :] + turn(x[2], -1))
+        for i, (a, b) in enumerate(PAIRS):
+            found[i].append(x[a] * x[b])
+    totals = [totals_in[i] + jnp.where(own_lane, tree(found[i]), 0.0) for i in range(6)]
+
     line = jnp.zeros((8, LANES), f32)
     for i in range(6):
         x = totals[i] + totals[i] if i == 5 else totals[i]
@@ -395,51 +421,53 @@
     sums_out[...] = jnp.broadcast_to(jnp.where(lane < 16, s, e)[:1], (256, LANES))
 
 
-def outer(ext, lext, v0, v1, v2, totals, c_even, c_odd):
-    field = near((BLOCKS + 2, ROWS, LANES))
+def seam(base, totals, c_even, c_odd):
     return pl.pallas_call(
-        outer_kernel,
-        out_shape=(
-            near((K, BLOCKS + 2, ROWS, LANES)),
-            near((BLOCKS + 2, ROWS, LANES), jnp.int32),
-            field,
-            field,
-            field,
-            near((256, LANES)),
-        ),
-        in_specs=[WHOLE] * 8,
-        out_specs=(WHOLE,) * 6,
-        input_output_aliases={i: i for i in range(5)},
-        compiler_params=LIMIT,
-        cost_estimate=cost(2),
-        name="outer_fields",
-    )(*held(ext, lext, v0, v1, v2, totals, c_even, c_odd))[2:]
-
-
-def pool_kernel(v0, v1, v2, out):
+        seam_kernel,
+        out_shape=(near((3, ROWS, LANES)), near((256, LANES))),
+        in_specs=[WHOLE] * 4,
+        out_specs=(WHOLE,) * 2,
+        scratch_shapes=[pltpu.VMEM((K + 1, ROWS, LANES), f32)],
+        compiler_params=LIMIT,
+        cost_estimate=cost(1),
+        name="seam_fields",
+    )(*held(base, totals, c_even, c_odd))
+
+
+def pool_kernel(v0_in, v1_in, v2_in, w, v0, v1, v2, out):
+    del v0_in, v1_in, v2_in
+    lane = iota((H, LANES), 1)
+    rows = pl.ds(TOP, H)
     spread = jnp.where(iota((512, LANES), 0) // 4 == iota((512, LANES), 1), f32(0.0625), f32(0.0))
     for i, ref in enumerate((v0, v1, v2)):
+        edge = w[i, rows, :]
+        ref[0, rows, :] = jnp.where(lane < HALO, turn(edge, -LEFT), ref[0, rows, :])
+        to = LANES - RIGHT - SEAM
+        ref[BLOCKS - 1, rows, :] = jnp.where(
+            lane >= LANES - HALO, turn(edge, to), ref[BLOCKS - 1, rows, :]
+        )
         for g in range(2):
             parts = []
             for j in range(4):
-                block = 1 + 4 * g + j
-                at = [ref[block, pl.ds(TOP + q, H // 4, stride=4), :] for q in range(4)]
+                at = [ref[4 * g + j, pl.ds(TOP + q, H // 4, stride=4), :] for q in range(4)]
                 parts.append((at[0] + at[1]) + (at[2] + at[3]))
             out[i, g] = jnp.dot(
                 jnp.concatenate(parts, 1), spread, precision=lax.Precision.HIGHEST, preferred_element_type=f32
             )
 
 
-def pool(v0, v1, v2):
+def pool(v0, v1, v2, w):
+    field = near((BLOCKS, ROWS, LANES))
     return pl.pallas_call(
         pool_kernel,
-        out_shape=near((3, 2, H // 4, LANES)),
-        in_specs=[WHOLE] * 3,
-        out_specs=WHOLE,
+        out_shape=(field, field, field, near((3, 2, H // 4, LANES))),
+        in_specs=[WHOLE] * 4,
+        out_specs=(WHOLE,) * 4,
+        input_output_aliases={0: 0, 1: 1, 2: 2},
         compiler_params=LIMIT,
         cost_estimate=cost(2),
         name="pool_fields",
-    )(*held(v0, v1, v2))
+    )(*held(v0, v1, v2, w))
 
 
 def two_product(a, b):
@@ -557,7 +585,7 @@
         for u in range(4):
             base = pl.multiple_of(32 * t + 8 * u, 8)
             for j in range(BLOCKS):
-                at = (j + 1, pl.ds(base + TOP, 8), slice(None))
+                at = (j, pl.ds(base + TOP, 8), slice(None))
                 value = c[0] * v0[at] + c[1] * v1[at] + c[2] * v2[at]
                 blended_out[pl.ds(base, 8), pl.ds(j * LANES, LANES)] = value
                 scratch[j, pl.ds(base, 8), :] = value
@@ -656,9 +684,9 @@
     r_even, r_odd = exchange(*pack_rows(sources, labels), ROW)
     ext, lext, left, right = load(sources, labels)
     c_even, c_odd = exchange(*pack_columns(r_even, r_odd, left, right), "col")
-    ext, lext, v0, v1, v2, totals = inner(ext, lext, r_even, r_odd)
-    v0, v1, v2, sums = outer(ext, lext, v0, v1, v2, totals, c_even, c_odd)
-    pooled = pool(v0, v1, v2)
+    v0, v1, v2, totals, base = inner(ext, lext, r_even, r_odd)
+    w, sums = seam(base, totals, c_even, c_odd)
+    v0, v1, v2, pooled = pool(v0, v1, v2, w)
     sums = lax.all_to_all(sums.reshape(256, 1, LANES), ALL, split_axis=0, concat_axis=0, tiled=True)
     coef, mid = solve(sums.reshape(256, LANES), pooled)
     mid = lax.all_to_all(mid, CHIP, split_axis=0, concat_axis=0, tiled=True)

time: 67.5 us -> 64.7 us (0.959)
  Pallas kernels: 13.5 us -> 11.5 us
  starting transfers between devices: 25.3 us -> 24.6 us
    pallas_call x5, Pallas kernels: 9.69 us -> 7.66 us  [the longest x1 3.46 us: inner(): pl.pallas_call(inner_kernel, out_shape=(near((K, BLOCKS, ROWS, LANES)), n...]
    all_to_all x1, starting transfers between devices: 17.4 us -> 16.7 us  [per_device(): lax.all_to_all(sums.reshape(256, 1, LANES), ALL, split_axis=0, concat_axi...]
where the time goes in v3:
time: 64.7 us; the launch traced here: 64.4 us
  starting transfers between devices  24.6 us (38%)
  waiting for transfers between devices  14.3 us (22%)
  blocking collectives  13.2 us (20%)
  Pallas kernels  11.5 us (18%)
  between operations  0.73 us (1%)
    all_to_all x1, starting transfers between devices, per_device(): lax.all_to_all(sums.reshape(256, 1, LANES), ALL, split_axis=0, concat_axi...  16.7 us
    all_to_all x1, blocking collectives, per_device(): mid = lax.all_to_all(mid, CHIP, split_axis=0, concat_axis=0, tiled=True)  13.2 us
    all_to_all x1, waiting for transfers between devices, per_device(): lax.all_to_all(sums.reshape(256, 1, LANES), ALL, split_axis=0, concat_axi...  12.2 us
    pallas_call x1, Pallas kernels, inner(): pl.pallas_call(inner_kernel, out_shape=(near((K, BLOCKS, ROWS, LANES)), n...  3.46 us
    ppermute x2, starting transfers between devices, exchange(): lax.ppermute(even, axis, swaps(devices, 0))  3.32 us
    ppermute x2, starting transfers between devices, exchange(): lax.ppermute(odd, axis, swaps(devices, 1))  2.57 us
    ppermute x1, starting transfers between devices, per_device(): other = lax.ppermute(mid, 'row_2', [(0, 1), (1, 0)])  2.06 us
    pallas_call x1, Pallas kernels, load(): pl.pallas_call(load_kernel, out_shape=(near((K, BLOCKS, ROWS, LANES)), ne...  1.87 us
  transfers between devices with their start and end apart: 6, of which 3 were waited for; matrix products, arithmetic and copies ran while one was open for 0% of the time, Pallas kernels for 11%

profile of v3, /device:TPU:1, one launch (start us, length us, event | category | flops | bytes accessed | tf_op | source)
XLA Modules:
  0.0 64.4 jit_solution(18107082704547140856)
XLA Ops:
  0.6 1.0 %pack_rows.1 = (f32[16,1024]{1,0:T(8,128)S(1)}, f32[16,1024]{1,0:T(8,128)S(1)}) custom-call(f32[3,128,1024]{2,1,0:T(8,128)} %src.3, s32[128,1024]{1,0:T(8,128)} %lab.3), custom_call_target="tpu_custom_call" | custom-call | flops 300000000 | tf_op jit(solution)/shard_map/pack_rows/pallas_call | solution.py:90
  1.7 3.3 %collective-permute-start = (f32[16,1024]{1,0:T(8,128)S(1)}, f32[16,1024]{1,0:T(8,128)S(1)}, u32[]{:S(2)}, u32[]{:S(2)}) collective-permute-start(f32[16,1024]{1,0:T(8,128)S(1)} %get-tuple-element.31), channel_id=1, source_target_pairs={{0,8},{16,24},{32,40},{48,56},{64,72},{80,88},{96,104},{112,120},{... | collective-permute-start | bytes 196616 | tf_op jit(solution)/shard_map/ppermute | solution.py:680
  5.0 1.9 %collective-permute-start.1 = (f32[16,1024]{1,0:T(8,128)S(1)}, f32[16,1024]{1,0:T(8,128)S(1)}, u32[]{:S(2)}, u32[]{:S(2)}) collective-permute-start(f32[16,1024]{1,0:T(8,128)S(1)} %get-tuple-element.32), channel_id=1, source_target_pairs={{8,16},{24,32},{40,48},{56,64},{72,80},{88,96},{104,112},{120,128}... | collective-permute-start | bytes 196616 | tf_op jit(solution)/shard_map/ppermute | solution.py:680
  6.9 1.9 %load_block.1 = (f32[3,8,168,128]{3,2,1,0:T(8,128)S(1)}, s32[8,168,128]{2,1,0:T(8,128)S(1)}, f32[16,128]{1,0:T(8,128)S(1)}, f32[16,128]{1,0:T(8,128)S(1)}) custom-call(f32[3,128,1024]{2,1,0:T(8,128)} %src.3, s32[128,1024]{1,0:T(8,128)} %lab.3), custom_call_target="tpu_custom_call" | custom-call | flops 600000000 | tf_op jit(solution)/shard_map/load_block/pallas_call | solution.py:143
  8.7 0.0 collective-permute-done.r_even.got_even
  8.8 1.8 %collective-permute-done.1.r_odd.got_odd = f32[16,1024]{1,0:T(8,128)S(1)} collective-permute-done((f32[16,1024]{1,0:T(8,128)S(1)}, f32[16,1024]{1,0:T(8,128)S(1)}, u32[]{:S(2)}, u32[]{:S(2)}) %collective-permute-start.1) | collective-permute-done | bytes 65568 | tf_op jit(solution)/shard_map/ppermute | solution.py:680
  10.5 0.1 pack_columns.1
  10.6 0.0 collective-permute-start.2
  10.6 0.7 %collective-permute-start.3 = (f32[24,128]{1,0:T(8,128)S(1)}, f32[24,128]{1,0:T(8,128)S(1)}, u32[]{:S(2)}, u32[]{:S(2)}) collective-permute-start(f32[24,128]{1,0:T(8,128)S(1)} %get-tuple-element.38), channel_id=1, source_target_pairs={{1,2},{3,4},{5,6},{2,1},{4,3},{6,5},{9,10},{11,12},{13,14},{10,9},... | collective-permute-start | bytes 36872 | tf_op jit(solution)/shard_map/ppermute | solution.py:680
  11.3 3.5 %inner_fields.1 = (f32[3,8,168,128]{3,2,1,0:T(8,128)S(1)}, s32[8,168,128]{2,1,0:T(8,128)S(1)}, f32[8,168,128]{2,1,0:T(8,128)S(1)}, f32[8,168,128]{2,1,0:T(8,128)...) custom-call(f32[3,8,168,128]{3,2,1,0:T(8,128)S(1)} %get-tuple-elemen, ...), custom_call_target="tpu_custom_call", output_to_operand_aliasing={{0}: (0, {}), {1}: (1, {})} | custom-call | flops 900000000 | tf_op jit(solution)/shard_map/inner_fields/pallas_call | solution.py:331
  14.8 0.0 collective-permute-done.2.c_even
  14.8 0.0 collective-permute-done.3.c_odd
  14.8 1.4 %seam_fields.1 = (f32[3,168,128]{2,1,0:T(8,128)S(1)}, f32[256,128]{1,0:T(8,128)}) custom-call(f32[4,168,128]{2,1,0:T(8,128)S(1)} %get-tuple-element.33.base, f32[6,8,128]{2,1,0:T(8,128)S(1)} %get-tuple-element.34.totals_in, f32[24,128]{1,0:T(8,128)S(1)} %collective-permute-done.2.c_even, f32[24,128]{1,0:T(8,128)S(1)} %collective-permute-done.3.c_odd), custom_call_target="tpu_custom_call" | custom-call | flops 300000000 | tf_op jit(solution)/shard_map/seam_fields/pallas_call | solution.py:425
  16.2 16.7 %all-to-all-start = ((f32[256,1,128]{2,1,0:T(1,128)}), f32[256,1,128]{2,1,0:T(1,128)S(1)}, u32[]{:S(2)}, u32[]{:S(2)}) async-start(f32[256,1,128]{2,1,0:T(1,128)} %bitcast.1), calls=%async_computation | async-start | bytes 262144 | tf_op jit(solution)/shard_map/all_to_all | solution.py:690
  32.9 0.8 %pool_fields.1 = (f32[8,168,128]{2,1,0:T(8,128)S(1)}, f32[8,168,128]{2,1,0:T(8,128)S(1)}, f32[8,168,128]{2,1,0:T(8,128)S(1)}, f32[3,2,32,128]{3,2,1,0:T(8,128)S(1)}) custom-call(f32[8,168,128]{2,1,0:T(8,128)S(1)} %get-tuple-element.40.v0_in, f32[8,168,128]{2,1,0:T(8,128)S(1)} %get-tuple-element.41.v1_in, ...), custom_call_target="tpu_custom_call", output_to_operand_aliasing={{0}: (0, {}), {1}: (1, {}), {2}: (2, {})} | custom-call | flops 600000000 | tf_op jit(solution)/shard_map/pool_fields/pallas_call | solution.py:461
  33.7 12.2 %all-to-all-done = f32[256,1,128]{2,1,0:T(1,128)S(1)} async-done(((f32[256,1,128]{2,1,0:T(1,128)}), f32[256,1,128]{2,1,0:T(1,128)S(1)}, u32[]{:S(2)}, u32[]{:S(2)}) %all-to-all-start) | async-done | bytes 131104 | tf_op jit(solution)/shard_map/all_to_all | solution.py:690
  45.9 0.3 coefficients.1
  46.2 13.2 %all_to_all.10.own = f32[16,2,32,128]{3,2,1,0:T(8,128)S(1)} all-to-all(f32[16,2,32,128]{3,2,1,0:T(8,128)S(1)} %get-tuple-element.51), channel_id=1, replica_groups=mesh['row_0'=4,'row_1'=4,'row_2'=2,'col'=8] {'row_0','row_1'}, dimensions={0} | all-to-all | bytes 1048576 | tf_op jit(solution)/shard_map/all_to_all | solution.py:692
  59.4 2.1 %collective-permute-start.4 = (f32[16,2,32,128]{3,2,1,0:T(8,128)S(1)}, f32[16,2,32,128]{3,2,1,0:T(8,128)S(1)}, u32[]{:S(2)}, u32[]{:S(2)}) collective-permute-start(f32[16,2,32,128]{3,2,1,0:T(8,128)S(1)} %all_to_all.10.own), channel_id=1, source_target_pairs={{0,8},{8,0},{1,9},{9,1},{2,10},{10,2},{3,11},{11,3},{4,12},{12,4},... | collective-permute-start | bytes 1572872 | tf_op jit(solution)/shard_map/ppermute | solution.py:693
  61.5 1.2 %blend.1 = (f32[128,1024]{1,0:T(8,128)}, f32[64,512]{1,0:T(8,128)}) custom-call(f32[3,8,128]{2,1,0:T(8,128)S(1)} %get-tuple-element.45.coef, f32[8,168,128]{2,1,0:T(8,128)S(1)} %get-tuple-element.46.v0, f32[8,168,128]{2,1,0:T(8,128)S(1)} %get-tuple-element.47.v1, f32[8,168,128]{2,1,0:T(8,128)S(1)} %get-tuple-element.48.v2), custom_call_target="tpu_custom_call" | custom-call | flops 900000000 | tf_op jit(solution)/shard_map/blend/pallas_call | solution.py:607
  62.6 0.4 collective-permute-done.4.other
  63.0 1.4 %assemble.1 = (f32[16,2,32,256]{3,2,1,0:T(8,128)}, f32[16,2,16,128]{3,2,1,0:T(8,128)}) custom-call(f32[16,2,32,128]{3,2,1,0:T(8,128)S(1)} %all_to_all.10.own, f32[16,2,32,128]{3,2,1,0:T(8,128)S(1)} %collective-permute-done.4.other), custom_call_target="tpu_custom_call" | custom-call | flops 600000000 | tf_op jit(solution)/shard_map/assemble/pallas_call | solution.py:654
Async XLA Ops:
  1.7 7.1 %collective-permute-start = (f32[16,1024]{1,0:T(8,128)S(1)}, f32[16,1024]{1,0:T(8,128)S(1)}, u32[]{:S(2)}, u32[]{:S(2)}) collective-permute-start(f32[16,1024]{1,0:T(8,128)S(1)} %get-tuple-element.31), channel_id=1, source_target_pairs={{0,8},{16,24},{32,40},{48,56},{64,72},{80,88},{96,104},{112,120},{... | collective-permute-start | bytes 196616 | tf_op jit(solution)/shard_map/ppermute | solution.py:680
  5.0 5.6 %collective-permute-start.1 = (f32[16,1024]{1,0:T(8,128)S(1)}, f32[16,1024]{1,0:T(8,128)S(1)}, u32[]{:S(2)}, u32[]{:S(2)}) collective-permute-start(f32[16,1024]{1,0:T(8,128)S(1)} %get-tuple-element.32), channel_id=1, source_target_pairs={{8,16},{24,32},{40,48},{56,64},{72,80},{88,96},{104,112},{120,128}... | collective-permute-start | bytes 196616 | tf_op jit(solution)/shard_map/ppermute | solution.py:680
  10.6 4.2 %collective-permute-start.2 = (f32[24,128]{1,0:T(8,128)S(1)}, f32[24,128]{1,0:T(8,128)S(1)}, u32[]{:S(2)}, u32[]{:S(2)}) collective-permute-start(f32[24,128]{1,0:T(8,128)S(1)} %get-tuple-element.37), channel_id=1, source_target_pairs={{0,1},{2,3},{4,5},{6,7},{1,0},{3,2},{5,4},{7,6},{8,9},{10,11},{12,... | collective-permute-start | bytes 36872 | tf_op jit(solution)/shard_map/ppermute | solution.py:680
  10.6 4.2 %collective-permute-start.3 = (f32[24,128]{1,0:T(8,128)S(1)}, f32[24,128]{1,0:T(8,128)S(1)}, u32[]{:S(2)}, u32[]{:S(2)}) collective-permute-start(f32[24,128]{1,0:T(8,128)S(1)} %get-tuple-element.38), channel_id=1, source_target_pairs={{1,2},{3,4},{5,6},{2,1},{4,3},{6,5},{9,10},{11,12},{13,14},{10,9},... | collective-permute-start | bytes 36872 | tf_op jit(solution)/shard_map/ppermute | solution.py:680
  16.2 29.6 %all-to-all-start = ((f32[256,1,128]{2,1,0:T(1,128)}), f32[256,1,128]{2,1,0:T(1,128)S(1)}, u32[]{:S(2)}, u32[]{:S(2)}) async-start(f32[256,1,128]{2,1,0:T(1,128)} %bitcast.1), calls=%async_computation | async-start | bytes 262144 | tf_op jit(solution)/shard_map/all_to_all | solution.py:690
  59.4 3.6 %collective-permute-start.4 = (f32[16,2,32,128]{3,2,1,0:T(8,128)S(1)}, f32[16,2,32,128]{3,2,1,0:T(8,128)S(1)}, u32[]{:S(2)}, u32[]{:S(2)}) collective-permute-start(f32[16,2,32,128]{3,2,1,0:T(8,128)S(1)} %all_to_all.10.own), channel_id=1, source_target_pairs={{0,8},{8,0},{1,9},{9,1},{2,10},{10,2},{3,11},{11,3},{4,12},{12,4},... | collective-permute-start | bytes 1572872 | tf_op jit(solution)/shard_map/ppermute | solution.py:693

commit v4 on v3

--- a/solution.py
+++ b/solution.py
@@ -20,7 +20,7 @@
 WHOLE = pl.BlockSpec(memory_space=VMEM)
 FAR = pl.BlockSpec(memory_space=pltpu.MemorySpace.HBM)
 LIMIT = pltpu.CompilerParams(vmem_limit_bytes=24 * 2**20)
-CHUNK = 3
+CHUNK, NEAR, MANY = 7, 9, 4
 TILES = H // 8
 LEFT, RIGHT = HALO, 64
 SEAM = 12
@@ -112,7 +112,7 @@
     return pltpu.roll(x, shift, 1) if shift else x
 
 
-def load_kernel(src, lab, ext, lext, left_out, right_out, sem):
+def load_kernel(src, lab, ext, lext, left_out, right_out, v0, sem):
     copies = {}
     for j in (0, BLOCKS - 1, *range(1, BLOCKS - 1)):
         lanes = pl.ds(j * LANES, LANES)
@@ -138,6 +138,13 @@
     for c in copies.values():
         c.wait()
 
+    def step(t, carry):
+        for u in range(CHUNK):
+            right_side(ext, lext, v0, pl.multiple_of(TOP + 8 + 8 * (CHUNK * t + u), 8))
+        return carry
+
+    lax.fori_loop(0, (TILES - 2) // CHUNK, step, 0)
+
 
 def load(sources, labels):
     return pl.pallas_call(
@@ -147,9 +154,10 @@
             near((BLOCKS, ROWS, LANES), jnp.int32),
             near((16, LANES)),
             near((16, LANES)),
+            near((BLOCKS, ROWS, LANES)),
         ),
         in_specs=[FAR] * 2,
-        out_specs=(WHOLE,) * 4,
+        out_specs=(WHOLE,) * 5,
         scratch_shapes=[pltpu.SemaphoreType.DMA((K + 1, BLOCKS))],
         compiler_params=LIMIT,
         cost_estimate=cost(2),
@@ -216,30 +224,27 @@
 PAIRS = ((0, 0), (0, 1), (1, 1), (1, 2), (2, 2), (2, 3))
 
 
-def right_side(ext, lext, out):
-    def step(t, carry):
-        for u in range(CHUNK):
-            base = pl.multiple_of(TOP - 8 + 8 * (CHUNK * t + u), 8)
-            total = [jnp.zeros((8, LANES), f32)] * BLOCKS
-            picked = [lext[j, pl.ds(base, 8), :] for j in range(BLOCKS)]
-            for k in range(K):
-                tiles = [ext[k, j, pl.ds(base, 8), :] for j in range(BLOCKS)]
-                after, before = shifted(tiles)
-                for j in range(BLOCKS):
-                    vertical = ext[k, j, pl.ds(base + 1, 8), :] + ext[k, j, pl.ds(base - 1, 8), :]
-                    term = 4.0 * tiles[j] - (vertical + after[j] + before[j])
-                    total[j] = jnp.where(picked[j] == k, term, total[j])
-            for j in range(BLOCKS):
-                out[j, pl.ds(base, 8), :] = total[j]
-        return carry
-
-    lax.fori_loop(0, (TILES + 2) // CHUNK, step, 0)
+def right_side(ext, lext, out, base):
+    at = pl.ds(base, 8)
+    picked = [lext[j, at, :] for j in range(BLOCKS)]
+    center, around = [None] * BLOCKS, [None] * BLOCKS
+    for k in range(K):
+        tiles = [ext[k, j, at, :] for j in range(BLOCKS)]
+        after, before = shifted(tiles)
+        for j in range(BLOCKS):
+            near_sum = ext[k, j, pl.ds(base + 1, 8), :] + ext[k, j, pl.ds(base - 1, 8), :]
+            near_sum = near_sum + after[j] + before[j]
+            here = picked[j] == k
+            center[j] = jnp.where(here, tiles[j], center[j]) if k else tiles[j]
+            around[j] = jnp.where(here, near_sum, around[j]) if k else near_sum
+    for j in range(BLOCKS):
+        out[j, at, :] = 4.0 * center[j] - around[j]
 
 
 def neighbours(source, target):
     def step(t, carry):
-        for u in range(2 * CHUNK):
-            base = pl.multiple_of(TOP - 8 + 8 * (2 * CHUNK * t + u), 8)
+        for u in range(NEAR):
+            base = pl.multiple_of(TOP - 8 + 8 * (NEAR * t + u), 8)
             tiles = [source[j, pl.ds(base, 8), :] for j in range(BLOCKS)]
             after, before = shifted(tiles)
             for j in range(BLOCKS):
@@ -247,7 +252,7 @@
                 target[j, pl.ds(base, 8), :] = vertical + after[j] + before[j]
         return carry
 
-    lax.fori_loop(0, (TILES + 2) // CHUNK // 2, step, 0)
+    lax.fori_loop(0, (TILES + 2) // NEAR, step, 0)
 
 
 def tree(x):
@@ -262,8 +267,8 @@
     kept = {0: lane >= HALO, BLOCKS - 1: lane < LANES - HALO}
 
     def step(t, totals):
-        for u in range(2):
-            base = pl.multiple_of(TOP + 8 * (2 * t + u), 8)
+        for u in range(MANY):
+            base = pl.multiple_of(TOP + 8 * (MANY * t + u), 8)
             at = pl.ds(base, 8)
             found = [[] for _ in PAIRS]
             rolled = [turn(v2[j, at, :], -1) for j in range(BLOCKS)]
@@ -277,7 +282,7 @@
             totals = tuple(total + tree(f) for total, f in zip(totals, found))
         return totals
 
-    return lax.fori_loop(0, TILES // 2, step, (jnp.zeros((8, LANES), f32),) * 6)
+    return lax.fori_loop(0, TILES // MANY, step, (jnp.zeros((8, LANES), f32),) * 6)
 
 
 def clear_rows(ref, row):
@@ -292,8 +297,10 @@
             ref[j, pl.ds(TOP + H, 8), :] = jnp.zeros((8, LANES), f32)
 
 
-def inner_kernel(ext_in, lext_in, r_even, r_odd, ext, lext, v0, v1, v2, totals_out, seam_out):
-    del ext_in, lext_in
+def inner_kernel(
+    ext_in, lext_in, v0_in, r_even, r_odd, ext, lext, v0, v1, v2, totals_out, seam_out
+):
+    del ext_in, lext_in, v0_in
     row, _ = place()
     row_even = (row % 2) == 0
     for k in range(K + 1):
@@ -307,7 +314,8 @@
                     ext[k, j, pl.ds(start, HALO), :] = value
                 else:
                     lext[j, pl.ds(start, HALO), :] = value.astype(jnp.int32)
-    right_side(ext, lext, v0)
+    for t in (-1, 0, TILES - 1, TILES):
+        right_side(ext, lext, v0, TOP + 8 * t)
     clear_rows(v0, row)
     neighbours(v0, v1)
     clear_rows(v1, row)
@@ -326,7 +334,7 @@
             seam_out[k, at, :] = jnp.where(lane < 64, turn(a, LEFT), turn(b, RIGHT + SEAM))
 
 
-def inner(ext, lext, r_even, r_odd):
+def inner(ext, lext, v0, r_even, r_odd):
     field = near((BLOCKS, ROWS, LANES))
     return pl.pallas_call(
         inner_kernel,
@@ -339,13 +347,13 @@
             near((6, 8, LANES)),
             near((K + 1, ROWS, LANES)),
         ),
-        in_specs=[WHOLE] * 4,
+        in_specs=[WHOLE] * 5,
         out_specs=(WHOLE,) * 7,
-        input_output_aliases={0: 0, 1: 1},
+        input_output_aliases={0: 0, 1: 1, 2: 2},
         compiler_params=LIMIT,
         cost_estimate=cost(3),
         name="inner_fields",
-    )(*held(ext, lext, r_even, r_odd))[2:]
+    )(*held(ext, lext, v0, r_even, r_odd))[2:]
 
 
 def seam_kernel(base, totals_in, c_even, c_odd, w, sums_out, planes):
@@ -418,13 +426,14 @@
     for shift in (4, 2, 1):
         s, more = two_sum(s, pltpu.roll(s, shift, 0))
         e = e + pltpu.roll(e, shift, 0) + more
-    sums_out[...] = jnp.broadcast_to(jnp.where(lane < 16, s, e)[:1], (256, LANES))
+    line = jnp.where(lane < 16, s, e)[:1].reshape(1, 1, LANES)
+    sums_out[...] = jnp.broadcast_to(line, (256, 1, LANES))
 
 
 def seam(base, totals, c_even, c_odd):
     return pl.pallas_call(
         seam_kernel,
-        out_shape=(near((3, ROWS, LANES)), near((256, LANES))),
+        out_shape=(near((3, ROWS, LANES)), near((256, 1, LANES))),
         in_specs=[WHOLE] * 4,
         out_specs=(WHOLE,) * 2,
         scratch_shapes=[pltpu.VMEM((K + 1, ROWS, LANES), f32)],
@@ -578,96 +587,124 @@
     return jnp.where(iota((rows, rows // 2), 0) // 2 == iota((rows, rows // 2), 1), f32(0.25), f32(0.0))
 
 
-def blend_kernel(coef, v0, v1, v2, blended_out, fine_out, scratch):
+def pooled_rows(parts):
+    return jnp.dot(
+        jnp.concatenate(parts, 1),
+        half_matrix(2 * LANES),
+        precision=lax.Precision.HIGHEST,
+        preferred_element_type=f32,
+    )
+
+
+def store_mid(x, core, mid_out, sem):
+    copies = []
+    for g in range(2):
+        to = mid_out.at[:, core, :, pl.ds(g * LANES, LANES)]
+        copies.append(pltpu.make_async_copy(x.at[:, g], to, sem.at[g]))
+        copies[-1].start()
+    return copies
+
+
+def store_coarse(x, core, coarse_out, scratch, sem):
+    rows = H // 8
+    parts = [
+        jnp.concatenate(
+            [x[d, g, pl.ds(0, rows, stride=2), :] + x[d, g, pl.ds(1, rows, stride=2), :] for d in range(16)], 0
+        )
+        for g in range(2)
+    ]
+    pooled = pooled_rows(parts)
+    for d in range(16):
+        scratch[d] = pooled[d * rows : (d + 1) * rows]
+    copy = pltpu.make_async_copy(scratch, coarse_out.at[:, core], sem)
+    copy.start()
+    return copy
+
+
+def own_kernel(
+    x, coef, v0, v1, v2, blended_out, fine_out, mid_out, coarse_out, flat, stacked, fine, coarse, sem
+):
+    core = lax.axis_index("row_2")
+    copies = store_mid(x, core, mid_out, sem)
     c = [coef[i] for i in range(3)]
-
-    def step(t, carry):
-        for u in range(4):
-            base = pl.multiple_of(32 * t + 8 * u, 8)
+    parts = 4
+    for p in range(parts):
+        for u in range(TILES // parts):
+            base = 8 * (p * (TILES // parts) + u)
             for j in range(BLOCKS):
                 at = (j, pl.ds(base + TOP, 8), slice(None))
                 value = c[0] * v0[at] + c[1] * v1[at] + c[2] * v2[at]
-                blended_out[pl.ds(base, 8), pl.ds(j * LANES, LANES)] = value
-                scratch[j, pl.ds(base, 8), :] = value
-        return carry
-
-    lax.fori_loop(0, H // 32, step, 0)
-    half = half_matrix(2 * LANES)
+                flat[pl.ds(base, 8), pl.ds(j * LANES, LANES)] = value
+                stacked[j, pl.ds(base, 8), :] = value
+        rows = pl.ds(p * H // parts, H // parts)
+        copies.append(pltpu.make_async_copy(flat.at[rows, :], blended_out.at[rows, :], sem.at[3 + p]))
+        copies[-1].start()
     for g in range(BLOCKS // 2):
-        parts = [
-            scratch[2 * g + i, pl.ds(0, H // 2, stride=2), :] + scratch[2 * g + i, pl.ds(1, H // 2, stride=2), :]
+        halves = [
+            stacked[2 * g + i, pl.ds(0, H // 2, stride=2), :] + stacked[2 * g + i, pl.ds(1, H // 2, stride=2), :]
             for i in range(2)
         ]
-        fine_out[:, pl.ds(g * LANES, LANES)] = jnp.dot(
-            jnp.concatenate(parts, 1), half, precision=lax.Precision.HIGHEST, preferred_element_type=f32
-        )
-
-
-def blend(coef, v0, v1, v2):
-    return pl.pallas_call(
-        blend_kernel,
+        fine[:, pl.ds(g * LANES, LANES)] = pooled_rows(halves)
+    copies.append(pltpu.make_async_copy(fine, fine_out, sem.at[3 + parts]))
+    copies[-1].start()
+    copies.append(store_coarse(x, core, coarse_out, coarse, sem.at[2]))
+    for copy in copies:
+        copy.wait()
+
+
+LEVELS = (
+    jax.ShapeDtypeStruct((16, 2, H // 4, W // 4), f32),
+    jax.ShapeDtypeStruct((16, 2, H // 8, W // 8), f32),
+)
+
+
+def own_levels(x, coef, v0, v1, v2):
+    return pl.pallas_call(
+        own_kernel,
         out_shape=(
             jax.ShapeDtypeStruct((H, W), f32),
             jax.ShapeDtypeStruct((H // 2, W // 2), f32),
+            *LEVELS,
         ),
-        in_specs=[WHOLE] * 4,
-        out_specs=(WHOLE,) * 2,
-        scratch_shapes=[pltpu.VMEM((BLOCKS, H, LANES), f32)],
-        compiler_params=LIMIT,
-        cost_estimate=cost(3),
-        name="blend",
-    )(*held(coef, v0, v1, v2))
-
-
-def assemble_kernel(own, other, mid_out, coarse_out, scratch, sem):
-    core = lax.axis_index("row_2")
-    half = half_matrix(2 * LANES)
-    copies = []
-    for i, (x, c) in enumerate(((own, core), (other, 1 - core))):
-        for g in range(2):
-            copy = pltpu.make_async_copy(
-                x.at[:, g], mid_out.at[:, c, :, pl.ds(g * LANES, LANES)], sem.at[i, g]
-            )
-            copy.start()
-            copies.append(copy)
-    rows = H // 8
-    for x, c in ((own, core), (other, 1 - core)):
-        parts = [
-            jnp.concatenate(
-                [x[d, g, pl.ds(0, rows, stride=2), :] + x[d, g, pl.ds(1, rows, stride=2), :] for d in range(16)], 0
-            )
-            for g in range(2)
-        ]
-        pooled = jnp.dot(
-            jnp.concatenate(parts, 1), half, precision=lax.Precision.HIGHEST, preferred_element_type=f32
-        )
-        for d in range(16):
-            scratch[d, c] = pooled[d * rows : (d + 1) * rows]
-    copy = pltpu.make_async_copy(scratch, coarse_out, sem.at[2, 0])
-    copy.start()
-    copies.append(copy)
+        in_specs=[WHOLE] * 5,
+        out_specs=(FAR,) * 4,
+        scratch_shapes=[
+            pltpu.VMEM((H, W), f32),
+            pltpu.VMEM((BLOCKS, H, LANES), f32),
+            pltpu.VMEM((H // 2, W // 2), f32),
+            pltpu.VMEM((16, H // 8, LANES), f32),
+            pltpu.SemaphoreType.DMA((8,)),
+        ],
+        compiler_params=LIMIT,
+        cost_estimate=cost(2),
+        name="own_levels",
+    )(*held(x, coef, v0, v1, v2))
+
+
+def other_kernel(x, mid_in, coarse_in, mid_out, coarse_out, coarse, sem):
+    del mid_in, coarse_in
+    core = 1 - lax.axis_index("row_2")
+    copies = store_mid(x, core, mid_out, sem)
+    copies.append(store_coarse(x, core, coarse_out, coarse, sem.at[2]))
     for copy in copies:
         copy.wait()
 
 
-def assemble(own, other):
-    mid, coarse = pl.pallas_call(
-        assemble_kernel,
-        out_shape=(
-            jax.ShapeDtypeStruct((16, 2, H // 4, W // 4), f32),
-            jax.ShapeDtypeStruct((16, 2, H // 8, W // 8), f32),
-        ),
-        in_specs=[WHOLE] * 2,
+def other_levels(x, mid, coarse):
+    return pl.pallas_call(
+        other_kernel,
+        out_shape=LEVELS,
+        in_specs=[WHOLE, FAR, FAR],
         out_specs=(FAR,) * 2,
         scratch_shapes=[
-            pltpu.VMEM((16, 2, H // 8, LANES), f32),
-            pltpu.SemaphoreType.DMA((3, 2)),
+            pltpu.VMEM((16, H // 8, LANES), f32),
+            pltpu.SemaphoreType.DMA((3,)),
         ],
-        compiler_params=LIMIT,
-        cost_estimate=cost(2),
-        name="assemble",
-    )(*held(own, other))
-    return mid.reshape(8 * H, W // 4), coarse.reshape(4 * H, W // 8)
+        input_output_aliases={1: 0, 2: 1},
+        compiler_params=LIMIT,
+        cost_estimate=cost(1),
+        name="other_levels",
+    )(*held(x), *far(mid, coarse))
 
 
 def swaps(devices, first):
@@ -682,17 +719,19 @@
 
 def per_device(sources, labels):
     r_even, r_odd = exchange(*pack_rows(sources, labels), ROW)
-    ext, lext, left, right = load(sources, labels)
+    ext, lext, left, right, v0 = load(sources, labels)
     c_even, c_odd = exchange(*pack_columns(r_even, r_odd, left, right), "col")
-    v0, v1, v2, totals, base = inner(ext, lext, r_even, r_odd)
+    v0, v1, v2, totals, base = inner(ext, lext, v0, r_even, r_odd)
     w, sums = seam(base, totals, c_even, c_odd)
     v0, v1, v2, pooled = pool(v0, v1, v2, w)
-    sums = lax.all_to_all(sums.reshape(256, 1, LANES), ALL, split_axis=0, concat_axis=0, tiled=True)
+    sums = lax.all_to_all(sums, ALL, split_axis=0, concat_axis=0, tiled=True)
     coef, mid = solve(sums.reshape(256, LANES), pooled)
     mid = lax.all_to_all(mid, CHIP, split_axis=0, concat_axis=0, tiled=True)
     other = lax.ppermute(mid, "row_2", [(0, 1), (1, 0)])
-    blended, fine = blend(coef, v0, v1, v2)
-    overview_mid, overview_coarse = assemble(mid, other)
+    blended, fine, overview_mid, overview_coarse = own_levels(mid, coef, v0, v1, v2)
+    overview_mid, overview_coarse = other_levels(other, overview_mid, overview_coarse)
+    overview_mid = overview_mid.reshape(8 * H, W // 4)
+    overview_coarse = overview_coarse.reshape(4 * H, W // 8)
     return (blended, fine, overview_mid, overview_coarse)
 
 

time: 64.7 us -> 64.4 us (level)
  starting transfers between devices: 24.6 us -> 26.1 us
  waiting for transfers between devices: 14.3 us -> 13.1 us
    pallas_call x1, Pallas kernels: 3.46 us -> 1.89 us  [inner(): pl.pallas_call(inner_kernel, out_shape=(near((K, BLOCKS, ROWS, LANES)), n...]
    all_to_all x1, starting transfers between devices: 16.7 us -> 17.9 us  [per_device(): sums = lax.all_to_all(sums, ALL, split_axis=0, concat_axis=0, tiled=True)]
    ppermute x2, waiting for transfers between devices: 1.77 us -> 0.81 us  [exchange(): lax.ppermute(odd, axis, swaps(devices, 1))]
    pallas_call x1, Pallas kernels: 1.87 us -> 2.83 us  [load(): pl.pallas_call(load_kernel, out_shape=(near((K, BLOCKS, ROWS, LANES)), ne...]
where the time goes in v4:
time: 64.4 us; the launch traced here: 64.1 us
  starting transfers between devices  26.1 us (41%)
  blocking collectives  13.2 us (20%)
  waiting for transfers between devices  13.1 us (20%)
  Pallas kernels  10.9 us (17%)
  between operations  0.73 us (1%)
    all_to_all x1, starting transfers between devices, per_device(): sums = lax.all_to_all(sums, ALL, split_axis=0, concat_axis=0, tiled=True)  17.9 us
    all_to_all x1, blocking collectives, per_device(): mid = lax.all_to_all(mid, CHIP, split_axis=0, concat_axis=0, tiled=True)  13.2 us
    all_to_all x1, waiting for transfers between devices, per_device(): sums = lax.all_to_all(sums, ALL, split_axis=0, concat_axis=0, tiled=True)  12.2 us
    ppermute x2, starting transfers between devices, exchange(): lax.ppermute(even, axis, swaps(devices, 0))  3.58 us
    pallas_call x1, Pallas kernels, load(): pl.pallas_call(load_kernel, out_shape=(near((K, BLOCKS, ROWS, LANES)), ne...  2.83 us
    ppermute x2, starting transfers between devices, exchange(): lax.ppermute(odd, axis, swaps(devices, 1))  2.56 us
    ppermute x1, starting transfers between devices, per_device(): other = lax.ppermute(mid, 'row_2', [(0, 1), (1, 0)])  2.06 us
    pallas_call x1, Pallas kernels, inner(): pl.pallas_call(inner_kernel, out_shape=(near((K, BLOCKS, ROWS, LANES)), n...  1.89 us
  transfers between devices with their start and end apart: 6, of which 3 were waited for; matrix products, arithmetic and copies ran while one was open for 0% of the time, Pallas kernels for 11%

profile of v4, /device:TPU:1, one launch (start us, length us, event | category | flops | bytes accessed | tf_op | source)
XLA Modules:
  0.0 64.1 jit_solution(15598447839295882881)
XLA Ops:
  0.6 1.0 %pack_rows.1 = (f32[16,1024]{1,0:T(8,128)S(1)}, f32[16,1024]{1,0:T(8,128)S(1)}) custom-call(f32[3,128,1024]{2,1,0:T(8,128)} %src.3, s32[128,1024]{1,0:T(8,128)} %lab.3), custom_call_target="tpu_custom_call" | custom-call | flops 300000000 | tf_op jit(solution)/shard_map/pack_rows/pallas_call | solution.py:90
  1.7 3.3 %collective-permute-start = (f32[16,1024]{1,0:T(8,128)S(1)}, f32[16,1024]{1,0:T(8,128)S(1)}, u32[]{:S(2)}, u32[]{:S(2)}) collective-permute-start(f32[16,1024]{1,0:T(8,128)S(1)} %get-tuple-element.35), channel_id=1, source_target_pairs={{0,8},{16,24},{32,40},{48,56},{64,72},{80,88},{96,104},{112,120},{... | collective-permute-start | bytes 196616 | tf_op jit(solution)/shard_map/ppermute | solution.py:717
  5.0 1.9 %collective-permute-start.1 = (f32[16,1024]{1,0:T(8,128)S(1)}, f32[16,1024]{1,0:T(8,128)S(1)}, u32[]{:S(2)}, u32[]{:S(2)}) collective-permute-start(f32[16,1024]{1,0:T(8,128)S(1)} %get-tuple-element.36), channel_id=1, source_target_pairs={{8,16},{24,32},{40,48},{56,64},{72,80},{88,96},{104,112},{120,128}... | collective-permute-start | bytes 196616 | tf_op jit(solution)/shard_map/ppermute | solution.py:717
  6.9 2.8 %load_block.1 = (f32[3,8,168,128]{3,2,1,0:T(8,128)S(1)}, s32[8,168,128]{2,1,0:T(8,128)S(1)}, f32[16,128]{1,0:T(8,128)S(1)}, f32[16,128]{1,0:T(8,128)S(1)}, f32[8,168,128]{2,1,0:T(8,128)S(1)}) custom-call(f32[3,128,1024]{2,1,0:T(8,128)} %src.3, s32[128,1024]{1,0:T(8,128)} %lab.3), custom_call_target="tpu_custom_call" | custom-call | flops 600000000 | tf_op jit(solution)/shard_map/load_block/pallas_call | solution.py:150
  9.7 0.0 collective-permute-done.r_even.got_even
  9.7 0.8 %collective-permute-done.1.r_odd.got_odd = f32[16,1024]{1,0:T(8,128)S(1)} collective-permute-done((f32[16,1024]{1,0:T(8,128)S(1)}, f32[16,1024]{1,0:T(8,128)S(1)}, u32[]{:S(2)}, u32[]{:S(2)}) %collective-permute-start.1) | collective-permute-done | bytes 65568 | tf_op jit(solution)/shard_map/ppermute | solution.py:717
  10.5 0.1 pack_columns.1
  10.6 0.3 collective-permute-start.2
  10.9 0.7 %collective-permute-start.3 = (f32[24,128]{1,0:T(8,128)S(1)}, f32[24,128]{1,0:T(8,128)S(1)}, u32[]{:S(2)}, u32[]{:S(2)}) collective-permute-start(f32[24,128]{1,0:T(8,128)S(1)} %get-tuple-element.42), channel_id=1, source_target_pairs={{1,2},{3,4},{5,6},{2,1},{4,3},{6,5},{9,10},{11,12},{13,14},{10,9},... | collective-permute-start | bytes 36872 | tf_op jit(solution)/shard_map/ppermute | solution.py:717
  11.6 1.9 %inner_fields.1 = (f32[3,8,168,128]{3,2,1,0:T(8,128)S(1)}, s32[8,168,128]{2,1,0:T(8,128)S(1)}, f32[8,168,128]{2,1,0:T(8,128)S(1)}, f32[8,168,128]{2,1,0:T(8,128)...) custom-call(f32[3,8,168,128]{3,2,1,0:T(8,128)S(1)} %get-tuple-elemen, ...), custom_call_target="tpu_custom_call", output_to_operand_aliasing={{0}: (0, {}), {1}: (1, {}), {2}: (2, {})} | custom-call | flops 900000000 | tf_op jit(solution)/shard_map/inner_fields/pallas_call | solution.py:339
  13.5 0.0 collective-permute-done.2.c_even
  13.5 0.0 collective-permute-done.3.c_odd
  13.5 1.5 %seam_fields.1 = (f32[3,168,128]{2,1,0:T(8,128)S(1)}, f32[256,1,128]{2,1,0:T(1,128)}) custom-call(f32[4,168,128]{2,1,0:T(8,128)S(1)} %get-tuple-element.37.base, f32[6,8,128]{2,1,0:T(8,128)S(1)} %get-tuple-element.38.totals_in, f32[24,128]{1,0:T(8,128)S(1)} %collective-permute-done.2.c_even, f32[24,128]{1,0:T(8,128)S(1)} %collective-permute-done.3.c_odd), custom_call_target="tpu_custom_call" | custom-call | flops 300000000 | tf_op jit(solution)/shard_map/seam_fields/pallas_call | solution.py:434
  15.0 17.9 %all-to-all-start = ((f32[256,1,128]{2,1,0:T(1,128)}), f32[256,1,128]{2,1,0:T(1,128)S(1)}, u32[]{:S(2)}, u32[]{:S(2)}) async-start(f32[256,1,128]{2,1,0:T(1,128)} %get-tuple-element.43), calls=%async_computation | async-start | bytes 262144 | tf_op jit(solution)/shard_map/all_to_all | solution.py:727
  32.9 0.8 %pool_fields.1 = (f32[8,168,128]{2,1,0:T(8,128)S(1)}, f32[8,168,128]{2,1,0:T(8,128)S(1)}, f32[8,168,128]{2,1,0:T(8,128)S(1)}, f32[3,2,32,128]{3,2,1,0:T(8,128)S(1)}) custom-call(f32[8,168,128]{2,1,0:T(8,128)S(1)} %get-tuple-element.44.v0_in, f32[8,168,128]{2,1,0:T(8,128)S(1)} %get-tuple-element.45.v1_in, ...), custom_call_target="tpu_custom_call", output_to_operand_aliasing={{0}: (0, {}), {1}: (1, {}), {2}: (2, {})} | custom-call | flops 600000000 | tf_op jit(solution)/shard_map/pool_fields/pallas_call | solution.py:470
  33.7 12.2 %all-to-all-done = f32[256,1,128]{2,1,0:T(1,128)S(1)} async-done(((f32[256,1,128]{2,1,0:T(1,128)}), f32[256,1,128]{2,1,0:T(1,128)S(1)}, u32[]{:S(2)}, u32[]{:S(2)}) %all-to-all-start) | async-done | bytes 131104 | tf_op jit(solution)/shard_map/all_to_all | solution.py:727
  45.9 0.3 coefficients.1
  46.2 13.2 %all_to_all.10.x = f32[16,2,32,128]{3,2,1,0:T(8,128)S(1)} all-to-all(f32[16,2,32,128]{3,2,1,0:T(8,128)S(1)} %get-tuple-element.49), channel_id=1, replica_groups=mesh['row_0'=4,'row_1'=4,'row_2'=2,'col'=8] {'row_0','row_1'}, dimensions={0} | all-to-all | bytes 1048576 | tf_op jit(solution)/shard_map/all_to_all | solution.py:729
  59.4 2.1 %collective-permute-start.4 = (f32[16,2,32,128]{3,2,1,0:T(8,128)S(1)}, f32[16,2,32,128]{3,2,1,0:T(8,128)S(1)}, u32[]{:S(2)}, u32[]{:S(2)}) collective-permute-start(f32[16,2,32,128]{3,2,1,0:T(8,128)S(1)} %all_to_all.10.x), channel_id=1, source_target_pairs={{0,8},{8,0},{1,9},{9,1},{2,10},{10,2},{3,11},{11,3},{4,12},{12,4},... | collective-permute-start | bytes 1572872 | tf_op jit(solution)/shard_map/ppermute | solution.py:730
  61.5 1.4 %own_levels.1 = (f32[128,1024]{1,0:T(8,128)}, f32[64,512]{1,0:T(8,128)}, f32[16,2,32,256]{3,2,1,0:T(8,128)}, f32[16,2,16,128]{3,2,1,0:T(8,128)}) custom-call(f32[16,2,32,128]{3,2,1,0:T(8,128)S(1)} %all_to_all.10.x, f32[3,8,128]{2,1,0:T(8,128)S(1)} %get-tuple-element.50.coef, f32[8,168,128]{2,1,0:T(8,128)S(1)} %get-tuple-element.51.v0, ...), custom_call_target="tpu_custom_call" | custom-call | flops 600000000 | tf_op jit(solution)/shard_map/own_levels/pallas_call | solution.py:662
  62.9 0.1 collective-permute-done.4.x
  63.0 1.1 %other_levels.1 = (f32[16,2,32,256]{3,2,1,0:T(8,128)}, f32[16,2,16,128]{3,2,1,0:T(8,128)}) custom-call(f32[16,2,32,128]{3,2,1,0:T(8,128)S(1)} %collective-permute-done.4.x, f32[16,2,32,256]{3,2,1,0:T(8,128)} %get-tuple-element.56.mid_in, f32[16,2,16,128]{3,2,1,0:T(8,128)} %get-tuple-element.57.coarse_in), custom_call_target="tpu_custom_call", output_to_operand_aliasing={{0}: (1, {}), {1}: (2, {})} | custom-call | flops 300000000 | tf_op jit(solution)/shard_map/other_levels/pallas_call | solution.py:694
Async XLA Ops:
  1.7 8.0 %collective-permute-start = (f32[16,1024]{1,0:T(8,128)S(1)}, f32[16,1024]{1,0:T(8,128)S(1)}, u32[]{:S(2)}, u32[]{:S(2)}) collective-permute-start(f32[16,1024]{1,0:T(8,128)S(1)} %get-tuple-element.35), channel_id=1, source_target_pairs={{0,8},{16,24},{32,40},{48,56},{64,72},{80,88},{96,104},{112,120},{... | collective-permute-start | bytes 196616 | tf_op jit(solution)/shard_map/ppermute | solution.py:717
  5.0 5.6 %collective-permute-start.1 = (f32[16,1024]{1,0:T(8,128)S(1)}, f32[16,1024]{1,0:T(8,128)S(1)}, u32[]{:S(2)}, u32[]{:S(2)}) collective-permute-start(f32[16,1024]{1,0:T(8,128)S(1)} %get-tuple-element.36), channel_id=1, source_target_pairs={{8,16},{24,32},{40,48},{56,64},{72,80},{88,96},{104,112},{120,128}... | collective-permute-start | bytes 196616 | tf_op jit(solution)/shard_map/ppermute | solution.py:717
  10.6 2.9 %collective-permute-start.2 = (f32[24,128]{1,0:T(8,128)S(1)}, f32[24,128]{1,0:T(8,128)S(1)}, u32[]{:S(2)}, u32[]{:S(2)}) collective-permute-start(f32[24,128]{1,0:T(8,128)S(1)} %get-tuple-element.41), channel_id=1, source_target_pairs={{0,1},{2,3},{4,5},{6,7},{1,0},{3,2},{5,4},{7,6},{8,9},{10,11},{12,... | collective-permute-start | bytes 36872 | tf_op jit(solution)/shard_map/ppermute | solution.py:717
  10.9 2.6 %collective-permute-start.3 = (f32[24,128]{1,0:T(8,128)S(1)}, f32[24,128]{1,0:T(8,128)S(1)}, u32[]{:S(2)}, u32[]{:S(2)}) collective-permute-start(f32[24,128]{1,0:T(8,128)S(1)} %get-tuple-element.42), channel_id=1, source_target_pairs={{1,2},{3,4},{5,6},{2,1},{4,3},{6,5},{9,10},{11,12},{13,14},{10,9},... | collective-permute-start | bytes 36872 | tf_op jit(solution)/shard_map/ppermute | solution.py:717
  15.0 30.9 %all-to-all-start = ((f32[256,1,128]{2,1,0:T(1,128)}), f32[256,1,128]{2,1,0:T(1,128)S(1)}, u32[]{:S(2)}, u32[]{:S(2)}) async-start(f32[256,1,128]{2,1,0:T(1,128)} %get-tuple-element.43), calls=%async_computation | async-start | bytes 262144 | tf_op jit(solution)/shard_map/all_to_all | solution.py:727
  59.4 3.6 %collective-permute-start.4 = (f32[16,2,32,128]{3,2,1,0:T(8,128)S(1)}, f32[16,2,32,128]{3,2,1,0:T(8,128)S(1)}, u32[]{:S(2)}, u32[]{:S(2)}) collective-permute-start(f32[16,2,32,128]{3,2,1,0:T(8,128)S(1)} %all_to_all.10.x), channel_id=1, source_target_pairs={{0,8},{8,0},{1,9},{9,1},{2,10},{10,2},{3,11},{11,3},{4,12},{12,4},... | collective-permute-start | bytes 1572872 | tf_op jit(solution)/shard_map/ppermute | solution.py:730

commit v5 on v4

--- a/solution.py
+++ b/solution.py
@@ -5,6 +5,7 @@
 from jax.experimental.pallas import tpu as pltpu
 from jax.sharding import Mesh
 from jax.sharding import PartitionSpec as P
+
 
 K = 3
 H, W = 128, 1024
@@ -20,7 +21,6 @@
 WHOLE = pl.BlockSpec(memory_space=VMEM)
 FAR = pl.BlockSpec(memory_space=pltpu.MemorySpace.HBM)
 LIMIT = pltpu.CompilerParams(vmem_limit_bytes=24 * 2**20)
-CHUNK, NEAR, MANY = 7, 9, 4
 TILES = H // 8
 LEFT, RIGHT = HALO, 64
 SEAM = 12
@@ -112,20 +112,17 @@
     return pltpu.roll(x, shift, 1) if shift else x
 
 
-def load_kernel(src, lab, ext, lext, left_out, right_out, v0, sem):
-    copies = {}
+def load_kernel(
+    src, lab, ext, lext, left_out, right_out, v0, v1, v2, totals_out, seam_out
+):
+    own = pl.ds(TOP, H)
     for j in (0, BLOCKS - 1, *range(1, BLOCKS - 1)):
         lanes = pl.ds(j * LANES, LANES)
-        for k in range(K + 1):
-            a = src.at[k, :, lanes] if k < K else lab.at[:, lanes]
-            b = ext.at[k, j, pl.ds(TOP, H), :] if k < K else lext.at[j, pl.ds(TOP, H), :]
-            c = pltpu.make_async_copy(a, b, sem.at[k, j])
-            c.start()
-            copies[k, j] = c
+        for k in range(K):
+            ext[k, j, own, :] = src[k, :, lanes]
+        lext[j, own, :] = lab[:, lanes]
     lane = iota((8, LANES), 1)
     for j, out, first in ((0, left_out, 0), (BLOCKS - 1, right_out, LANES - HALO)):
-        for k in range(K + 1):
-            copies.pop((k, j)).wait()
         for half in range(2):
             total = jnp.zeros((8, LANES), f32)
             for g in range(8):
@@ -135,18 +132,20 @@
                     to = 16 * g + HALO * k
                     total = jnp.where(window(lane, to, HALO), turn(x, to - first), total)
             out[pl.ds(8 * half, 8), :] = total
-    for c in copies.values():
-        c.wait()
-
-    def step(t, carry):
-        for u in range(CHUNK):
-            right_side(ext, lext, v0, pl.multiple_of(TOP + 8 + 8 * (CHUNK * t + u), 8))
-        return carry
-
-    lax.fori_loop(0, (TILES - 2) // CHUNK, step, 0)
+
+    over_tiles(1, TILES - 2, 7, lambda base, c: (right_side(ext, lext, v0, base), c)[1], 0)
+    over_tiles(2, TILES - 3, 6, lambda base, c: (neighbours(v0, v1, base), c)[1], 0)
+    over_tiles(3, TILES - 4, 5, lambda base, c: (neighbours(v1, v2, base), c)[1], 0)
+    zero = jnp.zeros((8, LANES), f32)
+    totals = over_tiles(3, TILES - 5, 3, lambda base, c: products(v0, v1, v2, base, c), (zero,) * 6)
+    for i in range(6):
+        totals_out[i] = totals[i]
+    for tile in range(TILES):
+        seam_base(ext, lext, seam_out, tile)
 
 
 def load(sources, labels):
+    field = near((BLOCKS, ROWS, LANES))
     return pl.pallas_call(
         load_kernel,
         out_shape=(
@@ -154,15 +153,18 @@
             near((BLOCKS, ROWS, LANES), jnp.int32),
             near((16, LANES)),
             near((16, LANES)),
-            near((BLOCKS, ROWS, LANES)),
+            field,
+            field,
+            field,
+            near((6, 8, LANES)),
+            near((K + 1, ROWS, LANES)),
         ),
-        in_specs=[FAR] * 2,
-        out_specs=(WHOLE,) * 5,
-        scratch_shapes=[pltpu.SemaphoreType.DMA((K + 1, BLOCKS))],
-        compiler_params=LIMIT,
-        cost_estimate=cost(2),
+        in_specs=[WHOLE] * 2,
+        out_specs=(WHOLE,) * 9,
+        compiler_params=LIMIT,
+        cost_estimate=cost(3),
         name="load_block",
-    )(*far(sources, labels))
+    )(*held(sources, labels))
 
 
 def corner_kernel(got_even, got_odd, left, right, even_out, odd_out):
@@ -241,18 +243,21 @@
         out[j, at, :] = 4.0 * center[j] - around[j]
 
 
-def neighbours(source, target):
-    def step(t, carry):
-        for u in range(NEAR):
-            base = pl.multiple_of(TOP - 8 + 8 * (NEAR * t + u), 8)
-            tiles = [source[j, pl.ds(base, 8), :] for j in range(BLOCKS)]
-            after, before = shifted(tiles)
-            for j in range(BLOCKS):
-                vertical = source[j, pl.ds(base + 1, 8), :] + source[j, pl.ds(base - 1, 8), :]
-                target[j, pl.ds(base, 8), :] = vertical + after[j] + before[j]
+def neighbours(source, target, base):
+    tiles = [source[j, pl.ds(base, 8), :] for j in range(BLOCKS)]
+    after, before = shifted(tiles)
+    for j in range(BLOCKS):
+        vertical = source[j, pl.ds(base + 1, 8), :] + source[j, pl.ds(base - 1, 8), :]
+        target[j, pl.ds(base, 8), :] = vertical + after[j] + before[j]
+
+
+def over_tiles(first, last, chunk, step, carry):
+    def turn_of(t, carry):
+        for u in range(chunk):
+            carry = step(pl.multiple_of(TOP + 8 * first + 8 * (chunk * t + u), 8), carry)
         return carry
 
-    lax.fori_loop(0, (TILES + 2) // NEAR, step, 0)
+    return lax.fori_loop(0, (last - first + 1) // chunk, turn_of, carry)
 
 
 def tree(x):
@@ -261,28 +266,29 @@
     return x[0]
 
 
-def products(v0, v1, v2):
+def products(v0, v1, v2, base, totals):
     lane = iota((8, LANES), 1)
     last = lane == LANES - 1
     kept = {0: lane >= HALO, BLOCKS - 1: lane < LANES - HALO}
-
-    def step(t, totals):
-        for u in range(MANY):
-            base = pl.multiple_of(TOP + 8 * (MANY * t + u), 8)
-            at = pl.ds(base, 8)
-            found = [[] for _ in PAIRS]
-            rolled = [turn(v2[j, at, :], -1) for j in range(BLOCKS)]
-            for j in range(BLOCKS):
-                x = [v[j, at, :] for v in (v0, v1, v2)]
-                right = jnp.where(last, rolled[min(j + 1, BLOCKS - 1)], rolled[j])
-                x.append(v2[j, pl.ds(base + 1, 8), :] + right)
-                own = [jnp.where(kept[j], a, 0.0) for a in x[:3]] if j in kept else x
-                for i, (a, b) in enumerate(PAIRS):
-                    found[i].append(own[a] * x[b])
-            totals = tuple(total + tree(f) for total, f in zip(totals, found))
-        return totals
-
-    return lax.fori_loop(0, TILES // MANY, step, (jnp.zeros((8, LANES), f32),) * 6)
+    at = pl.ds(base, 8)
+    found = [[] for _ in PAIRS]
+    rolled = [turn(v2[j, at, :], -1) for j in range(BLOCKS)]
+    for j in range(BLOCKS):
+        x = [v[j, at, :] for v in (v0, v1, v2)]
+        right = jnp.where(last, rolled[min(j + 1, BLOCKS - 1)], rolled[j])
+        x.append(v2[j, pl.ds(base + 1, 8), :] + right)
+        own = [jnp.where(kept[j], a, 0.0) for a in x[:3]] if j in kept else x
+        for i, (a, b) in enumerate(PAIRS):
+            found[i].append(own[a] * x[b])
+    return tuple(total + tree(f) for total, f in zip(totals, found))
+
+
+def seam_base(ext, lext, out, tile):
+    lane = iota((8, LANES), 1)
+    at = pl.ds(TOP + 8 * tile, 8)
+    for k in range(K + 1):
+        a, b = [ext[k, j, at, :] if k < K else lext[j, at, :].astype(f32) for j in (0, BLOCKS - 1)]
+        out[k, at, :] = jnp.where(lane < 64, turn(a, LEFT), turn(b, RIGHT + SEAM))
 
 
 def clear_rows(ref, row):
@@ -297,10 +303,9 @@
             ref[j, pl.ds(TOP + H, 8), :] = jnp.zeros((8, LANES), f32)
 
 
-def inner_kernel(
-    ext_in, lext_in, v0_in, r_even, r_odd, ext, lext, v0, v1, v2, totals_out, seam_out
-):
-    del ext_in, lext_in, v0_in
+def inner_kernel(*refs):
+    r_even, r_odd, totals_in = refs[6:9]
+    ext, lext, v0, v1, v2, seam_out, totals_out = refs[9:]
     row, _ = place()
     row_even = (row % 2) == 0
     for k in range(K + 1):
@@ -314,27 +319,25 @@
                     ext[k, j, pl.ds(start, HALO), :] = value
                 else:
                     lext[j, pl.ds(start, HALO), :] = value.astype(jnp.int32)
+    seam_base(ext, lext, seam_out, -1)
+    seam_base(ext, lext, seam_out, TILES)
     for t in (-1, 0, TILES - 1, TILES):
         right_side(ext, lext, v0, TOP + 8 * t)
     clear_rows(v0, row)
-    neighbours(v0, v1)
+    for t in (-1, 0, 1, TILES - 2, TILES - 1, TILES):
+        neighbours(v0, v1, TOP + 8 * t)
     clear_rows(v1, row)
-    neighbours(v1, v2)
+    for t in (-1, 0, 1, 2, TILES - 3, TILES - 2, TILES - 1, TILES):
+        neighbours(v1, v2, TOP + 8 * t)
     clear_rows(v2, row)
-    totals = products(v0, v1, v2)
+    totals = tuple(totals_in[i] for i in range(6))
+    for t in (0, 1, 2, *range(TILES - 4, TILES)):
+        totals = products(v0, v1, v2, TOP + 8 * t, totals)
     for i in range(6):
         totals_out[i] = totals[i]
-    lane = iota((8, LANES), 1)
-    for k in range(K + 1):
-        for t in range(TILES + 2):
-            at = pl.ds(TOP - 8 + 8 * t, 8)
-            a, b = [
-                ext[k, j, at, :] if k < K else lext[j, at, :].astype(f32) for j in (0, BLOCKS - 1)
-            ]
-            seam_out[k, at, :] = jnp.where(lane < 64, turn(a, LEFT), turn(b, RIGHT + SEAM))
-
-
-def inner(ext, lext, v0, r_even, r_odd):
+
+
+def inner(ext, lext, v0, v1, v2, base, r_even, r_odd, totals):
     field = near((BLOCKS, ROWS, LANES))
     return pl.pallas_call(
         inner_kernel,
@@ -344,16 +347,16 @@
             field,
             field,
             field,
+            near((K + 1, ROWS, LANES)),
             near((6, 8, LANES)),
-            near((K + 1, ROWS, LANES)),
         ),
-        in_specs=[WHOLE] * 5,
+        in_specs=[WHOLE] * 9,
         out_specs=(WHOLE,) * 7,
-        input_output_aliases={0: 0, 1: 1, 2: 2},
-        compiler_params=LIMIT,
-        cost_estimate=cost(3),
+        input_output_aliases={i: i for i in range(6)},
+        compiler_params=LIMIT,
+        cost_estimate=cost(2),
         name="inner_fields",
-    )(*held(ext, lext, v0, r_even, r_odd))[2:]
+    )(*held(ext, lext, v0, v1, v2, base, r_even, r_odd, totals))[2:]
 
 
 def seam_kernel(base, totals_in, c_even, c_odd, w, sums_out, planes):
@@ -714,14 +717,18 @@
 
 def exchange(even, odd, axis):
     devices = lax.axis_size(axis)
-    return lax.ppermute(even, axis, swaps(devices, 0)), lax.ppermute(odd, axis, swaps(devices, 1))
+    odd = lax.ppermute(odd, axis, swaps(devices, 1))
+    even = lax.ppermute(even, axis, swaps(devices, 0))
+    return even, odd
 
 
 def per_device(sources, labels):
-    r_even, r_odd = exchange(*pack_rows(sources, labels), ROW)
-    ext, lext, left, right, v0 = load(sources, labels)
+    even, odd = pack_rows(sources, labels)
+    even, odd, planes, marks = lax.optimization_barrier((even, odd, sources, labels))
+    r_even, r_odd = exchange(even, odd, ROW)
+    ext, lext, left, right, v0, v1, v2, totals, base = load(planes, marks)
     c_even, c_odd = exchange(*pack_columns(r_even, r_odd, left, right), "col")
-    v0, v1, v2, totals, base = inner(ext, lext, v0, r_even, r_odd)
+    v0, v1, v2, base, totals = inner(ext, lext, v0, v1, v2, base, r_even, r_odd, totals)
     w, sums = seam(base, totals, c_even, c_odd)
     v0, v1, v2, pooled = pool(v0, v1, v2, w)
     sums = lax.all_to_all(sums, ALL, split_axis=0, concat_axis=0, tiled=True)

time: 64.4 us -> 64.4 us (level)
  waiting for transfers between devices: 13.1 us -> 14.5 us
  Pallas kernels: 10.9 us -> 9.58 us
    ppermute x4, waiting for transfers between devices: 0.81 us -> 2.22 us  [the longest x2 1.22 us: exchange(): odd = lax.ppermute(odd, axis, swaps(devices, 1))]
    pallas_call x1, Pallas kernels: 1.89 us -> 0.86 us  [inner(): pl.pallas_call(inner_kernel, out_shape=(near((K, BLOCKS, ROWS, LANES)), n...]
  transfers between devices with their start and end apart: 6 -> 6, of which waited for: 3 -> 4; matrix products, arithmetic and copies ran while one was open for 0% -> 0% of each run, Pallas kernels for 11% -> 9%
where the time goes in v5:
time: 64.4 us; the launch traced here: 64.2 us
  starting transfers between devices  26.2 us (41%)
  waiting for transfers between devices  14.5 us (23%)
  blocking collectives  13.2 us (20%)
  Pallas kernels  9.58 us (15%)
  between operations  0.75 us (1%)
    all_to_all x1, starting transfers between devices, per_device(): sums = lax.all_to_all(sums, ALL, split_axis=0, concat_axis=0, tiled=True)  18.2 us
    all_to_all x1, blocking collectives, per_device(): mid = lax.all_to_all(mid, CHIP, split_axis=0, concat_axis=0, tiled=True)  13.2 us
    all_to_all x1, waiting for transfers between devices, per_device(): sums = lax.all_to_all(sums, ALL, split_axis=0, concat_axis=0, tiled=True)  12.2 us
    ppermute x2, starting transfers between devices, exchange(): even = lax.ppermute(even, axis, swaps(devices, 0))  3.32 us
    ppermute x2, starting transfers between devices, exchange(): odd = lax.ppermute(odd, axis, swaps(devices, 1))  2.57 us
    pallas_call x1, Pallas kernels, load(): pl.pallas_call(load_kernel, out_shape=(near((K, BLOCKS, ROWS, LANES)), ne...  2.4 us
    ppermute x1, starting transfers between devices, per_device(): other = lax.ppermute(mid, 'row_2', [(0, 1), (1, 0)])  2.06 us
    pallas_call x1, Pallas kernels, seam(): pl.pallas_call(seam_kernel, out_shape=(near((3, ROWS, LANES)), near((256,...  1.49 us
  transfers between devices with their start and end apart: 6, of which 4 were waited for; matrix products, arithmetic and copies ran while one was open for 0% of the time, Pallas kernels for 9%

profile of v5, /device:TPU:1, one launch (start us, length us, event | category | flops | bytes accessed | tf_op | source)
XLA Modules:
  0.0 64.2 jit_solution(11537587524192960345)
XLA Ops:
  0.6 0.0 copy-start.1
  0.6 0.0 copy-start
  0.7 1.2 %pack_rows.1 = (f32[16,1024]{1,0:T(8,128)S(1)}, f32[16,1024]{1,0:T(8,128)S(1)}) custom-call(f32[3,128,1024]{2,1,0:T(8,128)} %src.2, s32[128,1024]{1,0:T(8,128)} %lab.2), custom_call_target="tpu_custom_call" | custom-call | flops 300000000 | tf_op jit(solution)/shard_map/pack_rows/pallas_call | solution.py:90
  1.8 3.3 %collective-permute-start = (f32[16,1024]{1,0:T(8,128)S(1)}, f32[16,1024]{1,0:T(8,128)S(1)}, u32[]{:S(2)}, u32[]{:S(2)}) collective-permute-start(f32[16,1024]{1,0:T(8,128)S(1)} %get-tuple-element.50), channel_id=1, source_target_pairs={{0,8},{16,24},{32,40},{48,56},{64,72},{80,88},{96,104},{112,120},{... | collective-permute-start | bytes 196616 | tf_op jit(solution)/shard_map/ppermute | solution.py:721
  5.1 1.9 %collective-permute-start.1 = (f32[16,1024]{1,0:T(8,128)S(1)}, f32[16,1024]{1,0:T(8,128)S(1)}, u32[]{:S(2)}, u32[]{:S(2)}) collective-permute-start(f32[16,1024]{1,0:T(8,128)S(1)} %get-tuple-element.51), channel_id=1, source_target_pairs={{8,16},{24,32},{40,48},{56,64},{72,80},{88,96},{104,112},{120,128}... | collective-permute-start | bytes 196616 | tf_op jit(solution)/shard_map/ppermute | solution.py:720
  7.0 0.0 copy-done.1
  7.0 0.0 copy-done
  7.0 2.4 %load_block.1 = (f32[3,8,168,128]{3,2,1,0:T(8,128)S(1)}, s32[8,168,128]{2,1,0:T(8,128)S(1)}, f32[16,128]{1,0:T(8,128)S(1)}, f32[16,128]{1,0:T(8,128)S(1)}, f32[8...) custom-call(f32[3,128,1024]{2,1,0:T(8,128)S(1)} %copy-done, ...), custom_call_target="tpu_custom_call" | custom-call | flops 900000000 | tf_op jit(solution)/shard_map/load_block/pallas_call | solution.py:149
  9.5 0.0 collective-permute-done.refs_6_.got_even
  9.5 1.2 %collective-permute-done.1.refs_7_.got_odd = f32[16,1024]{1,0:T(8,128)S(1)} collective-permute-done((f32[16,1024]{1,0:T(8,128)S(1)}, f32[16,1024]{1,0:T(8,128)S(1)}, u32[]{:S(2)}, u32[]{:S(2)}) %collective-permute-start.1) | collective-permute-done | bytes 65568 | tf_op jit(solution)/shard_map/ppermute | solution.py:720
  10.7 0.1 pack_columns.1
  10.8 0.0 collective-permute-start.2
  10.8 0.7 %collective-permute-start.3 = (f32[24,128]{1,0:T(8,128)S(1)}, f32[24,128]{1,0:T(8,128)S(1)}, u32[]{:S(2)}, u32[]{:S(2)}) collective-permute-start(f32[24,128]{1,0:T(8,128)S(1)} %get-tuple-element.58), channel_id=1, source_target_pairs={{1,2},{3,4},{5,6},{2,1},{4,3},{6,5},{9,10},{11,12},{13,14},{10,9},... | collective-permute-start | bytes 36872 | tf_op jit(solution)/shard_map/ppermute | solution.py:720
  11.5 0.9 %inner_fields.1 = (f32[3,8,168,128]{3,2,1,0:T(8,128)S(1)}, s32[8,168,128]{2,1,0:T(8,128)S(1)}, f32[8,168,128]{2,1,0:T(8,128)S(1)}, f32[8,168,128]{2,1,0:T(8,128)...) custom-call(f32[3,8,168,128]{3,2,1,0:T(8,128)S(1)} %get-tuple-elemen, ...), custom_call_target="tpu_custom_call", output_to_operand_aliasing={{0}: (0, {}), {1}: (1, {}), {2}: (2, {}), {3}: (3, {}), {4}... | custom-call | flops 600000000 | tf_op jit(solution)/shard_map/inner_fields/pallas_call | solution.py:342
  12.3 1.0 %collective-permute-done.2.c_even = f32[24,128]{1,0:T(8,128)S(1)} collective-permute-done((f32[24,128]{1,0:T(8,128)S(1)}, f32[24,128]{1,0:T(8,128)S(1)}, u32[]{:S(2)}, u32[]{:S(2)}) %collective-permute-start.2) | collective-permute-done | bytes 12320 | tf_op jit(solution)/shard_map/ppermute | solution.py:721
  13.3 0.0 collective-permute-done.3.c_odd
  13.3 1.5 %seam_fields.1 = (f32[3,168,128]{2,1,0:T(8,128)S(1)}, f32[256,1,128]{2,1,0:T(1,128)}) custom-call(f32[4,168,128]{2,1,0:T(8,128)S(1)} %get-tuple-element.53.base, f32[6,8,128]{2,1,0:T(8,128)S(1)} %get-tuple-element.54.totals_in, f32[24,128]{1,0:T(8,128)S(1)} %collective-permute-done.2.c_even, f32[24,128]{1,0:T(8,128)S(1)} %collective-permute-done.3.c_odd), custom_call_target="tpu_custom_call" | custom-call | flops 300000000 | tf_op jit(solution)/shard_map/seam_fields/pallas_call | solution.py:437
  14.8 18.2 %all-to-all-start = ((f32[256,1,128]{2,1,0:T(1,128)}), f32[256,1,128]{2,1,0:T(1,128)S(1)}, u32[]{:S(2)}, u32[]{:S(2)}) async-start(f32[256,1,128]{2,1,0:T(1,128)} %get-tuple-element.59), calls=%async_computation | async-start | bytes 262144 | tf_op jit(solution)/shard_map/all_to_all | solution.py:734
  33.1 0.8 %pool_fields.1 = (f32[8,168,128]{2,1,0:T(8,128)S(1)}, f32[8,168,128]{2,1,0:T(8,128)S(1)}, f32[8,168,128]{2,1,0:T(8,128)S(1)}, f32[3,2,32,128]{3,2,1,0:T(8,128)S(1)}) custom-call(f32[8,168,128]{2,1,0:T(8,128)S(1)} %get-tuple-element.60.v0_in, f32[8,168,128]{2,1,0:T(8,128)S(1)} %get-tuple-element.61.v1_in, ...), custom_call_target="tpu_custom_call", output_to_operand_aliasing={{0}: (0, {}), {1}: (1, {}), {2}: (2, {})} | custom-call | flops 600000000 | tf_op jit(solution)/shard_map/pool_fields/pallas_call | solution.py:473
  33.9 12.2 %all-to-all-done = f32[256,1,128]{2,1,0:T(1,128)S(1)} async-done(((f32[256,1,128]{2,1,0:T(1,128)}), f32[256,1,128]{2,1,0:T(1,128)S(1)}, u32[]{:S(2)}, u32[]{:S(2)}) %all-to-all-start) | async-done | bytes 131104 | tf_op jit(solution)/shard_map/all_to_all | solution.py:734
  46.0 0.3 coefficients.1
  46.3 13.2 %all_to_all.10.x = f32[16,2,32,128]{3,2,1,0:T(8,128)S(1)} all-to-all(f32[16,2,32,128]{3,2,1,0:T(8,128)S(1)} %get-tuple-element.65), channel_id=1, replica_groups=mesh['row_0'=4,'row_1'=4,'row_2'=2,'col'=8] {'row_0','row_1'}, dimensions={0} | all-to-all | bytes 1048576 | tf_op jit(solution)/shard_map/all_to_all | solution.py:736
  59.6 2.1 %collective-permute-start.4 = (f32[16,2,32,128]{3,2,1,0:T(8,128)S(1)}, f32[16,2,32,128]{3,2,1,0:T(8,128)S(1)}, u32[]{:S(2)}, u32[]{:S(2)}) collective-permute-start(f32[16,2,32,128]{3,2,1,0:T(8,128)S(1)} %all_to_all.10.x), channel_id=1, source_target_pairs={{0,8},{8,0},{1,9},{9,1},{2,10},{10,2},{3,11},{11,3},{4,12},{12,4},... | collective-permute-start | bytes 1572872 | tf_op jit(solution)/shard_map/ppermute | solution.py:737
  61.6 1.4 %own_levels.1 = (f32[128,1024]{1,0:T(8,128)}, f32[64,512]{1,0:T(8,128)}, f32[16,2,32,256]{3,2,1,0:T(8,128)}, f32[16,2,16,128]{3,2,1,0:T(8,128)}) custom-call(f32[16,2,32,128]{3,2,1,0:T(8,128)S(1)} %all_to_all.10.x, f32[3,8,128]{2,1,0:T(8,128)S(1)} %get-tuple-element.66.coef, f32[8,168,128]{2,1,0:T(8,128)S(1)} %get-tuple-element.67.v0, ...), custom_call_target="tpu_custom_call" | custom-call | flops 600000000 | tf_op jit(solution)/shard_map/own_levels/pallas_call | solution.py:665
  63.1 0.1 collective-permute-done.4.x
  63.2 1.1 %other_levels.1 = (f32[16,2,32,256]{3,2,1,0:T(8,128)}, f32[16,2,16,128]{3,2,1,0:T(8,128)}) custom-call(f32[16,2,32,128]{3,2,1,0:T(8,128)S(1)} %collective-permute-done.4.x, f32[16,2,32,256]{3,2,1,0:T(8,128)} %get-tuple-element.72.mid_in, f32[16,2,16,128]{3,2,1,0:T(8,128)} %get-tuple-element.73.coarse_in), custom_call_target="tpu_custom_call", output_to_operand_aliasing={{0}: (1, {}), {1}: (2, {})} | custom-call | flops 300000000 | tf_op jit(solution)/shard_map/other_levels/pallas_call | solution.py:697
Async XLA Ops:
  0.6 6.4 %copy-start.1 = (s32[128,1024]{1,0:T(8,128)S(1)}, s32[128,1024]{1,0:T(8,128)}, u32[]{:S(2)}) copy-start(s32[128,1024]{1,0:T(8,128)} %lab.2) | copy-start | bytes 1572868
  0.6 6.4 %copy-start = (f32[3,128,1024]{2,1,0:T(8,128)S(1)}, f32[3,128,1024]{2,1,0:T(8,128)}, u32[]{:S(2)}) copy-start(f32[3,128,1024]{2,1,0:T(8,128)} %src.2) | copy-start | bytes 4718596
  1.8 7.6 %collective-permute-start = (f32[16,1024]{1,0:T(8,128)S(1)}, f32[16,1024]{1,0:T(8,128)S(1)}, u32[]{:S(2)}, u32[]{:S(2)}) collective-permute-start(f32[16,1024]{1,0:T(8,128)S(1)} %get-tuple-element.50), channel_id=1, source_target_pairs={{0,8},{16,24},{32,40},{48,56},{64,72},{80,88},{96,104},{112,120},{... | collective-permute-start | bytes 196616 | tf_op jit(solution)/shard_map/ppermute | solution.py:721
  5.1 5.6 %collective-permute-start.1 = (f32[16,1024]{1,0:T(8,128)S(1)}, f32[16,1024]{1,0:T(8,128)S(1)}, u32[]{:S(2)}, u32[]{:S(2)}) collective-permute-start(f32[16,1024]{1,0:T(8,128)S(1)} %get-tuple-element.51), channel_id=1, source_target_pairs={{8,16},{24,32},{40,48},{56,64},{72,80},{88,96},{104,112},{120,128}... | collective-permute-start | bytes 196616 | tf_op jit(solution)/shard_map/ppermute | solution.py:720
  10.8 2.6 %collective-permute-start.2 = (f32[24,128]{1,0:T(8,128)S(1)}, f32[24,128]{1,0:T(8,128)S(1)}, u32[]{:S(2)}, u32[]{:S(2)}) collective-permute-start(f32[24,128]{1,0:T(8,128)S(1)} %get-tuple-element.57), channel_id=1, source_target_pairs={{0,1},{2,3},{4,5},{6,7},{1,0},{3,2},{5,4},{7,6},{8,9},{10,11},{12,... | collective-permute-start | bytes 36872 | tf_op jit(solution)/shard_map/ppermute | solution.py:721
  10.8 2.5 %collective-permute-start.3 = (f32[24,128]{1,0:T(8,128)S(1)}, f32[24,128]{1,0:T(8,128)S(1)}, u32[]{:S(2)}, u32[]{:S(2)}) collective-permute-start(f32[24,128]{1,0:T(8,128)S(1)} %get-tuple-element.58), channel_id=1, source_target_pairs={{1,2},{3,4},{5,6},{2,1},{4,3},{6,5},{9,10},{11,12},{13,14},{10,9},... | collective-permute-start | bytes 36872 | tf_op jit(solution)/shard_map/ppermute | solution.py:720
  14.8 31.2 %all-to-all-start = ((f32[256,1,128]{2,1,0:T(1,128)}), f32[256,1,128]{2,1,0:T(1,128)S(1)}, u32[]{:S(2)}, u32[]{:S(2)}) async-start(f32[256,1,128]{2,1,0:T(1,128)} %get-tuple-element.59), calls=%async_computation | async-start | bytes 262144 | tf_op jit(solution)/shard_map/all_to_all | solution.py:734
  59.6 3.6 %collective-permute-start.4 = (f32[16,2,32,128]{3,2,1,0:T(8,128)S(1)}, f32[16,2,32,128]{3,2,1,0:T(8,128)S(1)}, u32[]{:S(2)}, u32[]{:S(2)}) collective-permute-start(f32[16,2,32,128]{3,2,1,0:T(8,128)S(1)} %all_to_all.10.x), channel_id=1, source_target_pairs={{0,8},{8,0},{1,9},{9,1},{2,10},{10,2},{3,11},{11,3},{4,12},{12,4},... | collective-permute-start | bytes 1572872 | tf_op jit(solution)/shard_map/ppermute | solution.py:737

commit v6 on v5

--- a/solution.py
+++ b/solution.py
@@ -446,18 +446,9 @@
     )(*held(base, totals, c_even, c_odd))
 
 
-def pool_kernel(v0_in, v1_in, v2_in, w, v0, v1, v2, out):
-    del v0_in, v1_in, v2_in
-    lane = iota((H, LANES), 1)
-    rows = pl.ds(TOP, H)
+def pool_kernel(v0, v1, v2, out):
     spread = jnp.where(iota((512, LANES), 0) // 4 == iota((512, LANES), 1), f32(0.0625), f32(0.0))
     for i, ref in enumerate((v0, v1, v2)):
-        edge = w[i, rows, :]
-        ref[0, rows, :] = jnp.where(lane < HALO, turn(edge, -LEFT), ref[0, rows, :])
-        to = LANES - RIGHT - SEAM
-        ref[BLOCKS - 1, rows, :] = jnp.where(
-            lane >= LANES - HALO, turn(edge, to), ref[BLOCKS - 1, rows, :]
-        )
         for g in range(2):
             parts = []
             for j in range(4):
@@ -468,18 +459,16 @@
             )
 
 
-def pool(v0, v1, v2, w):
-    field = near((BLOCKS, ROWS, LANES))
+def pool(v0, v1, v2):
     return pl.pallas_call(
         pool_kernel,
-        out_shape=(field, field, field, near((3, 2, H // 4, LANES))),
-        in_specs=[WHOLE] * 4,
-        out_specs=(WHOLE,) * 4,
-        input_output_aliases={0: 0, 1: 1, 2: 2},
-        compiler_params=LIMIT,
-        cost_estimate=cost(2),
+        out_shape=near((3, 2, H // 4, LANES)),
+        in_specs=[WHOLE] * 3,
+        out_specs=WHOLE,
+        compiler_params=LIMIT,
+        cost_estimate=cost(1),
         name="pool_fields",
-    )(*held(v0, v1, v2, w))
+    )(*held(v0, v1, v2))
 
 
 def two_product(a, b):
@@ -540,7 +529,20 @@
     )
 
 
-def solve_kernel(all_sums, pooled, coef_out, mid_out):
+def solve_kernel(all_sums, pooled, w, coef_out, mid_out):
+    frm, to = iota((LANES, LANES), 0), iota((LANES, LANES), 1)
+    first = window(frm, LEFT, HALO) & (to == 0)
+    final = window(frm, RIGHT + SEAM - HALO, HALO) & (to == LANES - 1)
+    rows = []
+    for i in range(3):
+        at = [w[i, pl.ds(TOP + q, H // 4, stride=4), :] for q in range(4)]
+        rows.append((at[0] + at[1]) + (at[2] + at[3]))
+    edges = jnp.dot(
+        jnp.concatenate(rows, 0),
+        jnp.where(first | final, f32(0.0625), f32(0.0)),
+        precision=lax.Precision.HIGHEST,
+        preferred_element_type=f32,
+    )
     tiles = [(all_sums[pl.ds(8 * i, 8), :], jnp.zeros((8, LANES), f32)) for i in range(32)]
     while len(tiles) > 1:
         merged = []
@@ -567,23 +569,27 @@
     for i in range(3):
         coef_out[i] = c[i]
     for g in range(2):
+        edge = lane == (LANES - 1 if g else 0)
         for q in range(H // 4 // 8):
             at = (g, pl.ds(8 * q, 8), slice(None))
-            value = c[0] * pooled[(0, *at)] + c[1] * pooled[(1, *at)] + c[2] * pooled[(2, *at)]
+            value = zero
+            for i in range(3):
+                start = H // 4 * i + 8 * q
+                value = value + c[i] * jnp.where(edge, edges[start : start + 8], pooled[(i, *at)])
             for d in range(16):
                 mid_out[(d, *at)] = value
 
 
-def solve(all_sums, pooled):
+def solve(all_sums, pooled, w):
     return pl.pallas_call(
         solve_kernel,
         out_shape=(near((3, 8, LANES)), near((16, 2, H // 4, LANES))),
-        in_specs=[WHOLE] * 2,
+        in_specs=[WHOLE] * 3,
         out_specs=(WHOLE,) * 2,
         compiler_params=LIMIT,
         cost_estimate=cost(1),
         name="coefficients",
-    )(*held(all_sums, pooled))
+    )(*held(all_sums, pooled, w))
 
 
 def half_matrix(rows):
@@ -625,18 +631,25 @@
 
 
 def own_kernel(
-    x, coef, v0, v1, v2, blended_out, fine_out, mid_out, coarse_out, flat, stacked, fine, coarse, sem
+    x, coef, v0, v1, v2, w, blended_out, fine_out, mid_out, coarse_out, flat, stacked, fine, coarse, sem
 ):
     core = lax.axis_index("row_2")
     copies = store_mid(x, core, mid_out, sem)
     c = [coef[i] for i in range(3)]
+    lane = iota((8, LANES), 1)
     parts = 4
     for p in range(parts):
         for u in range(TILES // parts):
             base = 8 * (p * (TILES // parts) + u)
+            rows = pl.ds(base + TOP, 8)
+            seams = c[0] * w[0, rows, :] + c[1] * w[1, rows, :] + c[2] * w[2, rows, :]
             for j in range(BLOCKS):
-                at = (j, pl.ds(base + TOP, 8), slice(None))
+                at = (j, rows, slice(None))
                 value = c[0] * v0[at] + c[1] * v1[at] + c[2] * v2[at]
+                if j == 0:
+                    value = jnp.where(lane < HALO, turn(seams, -LEFT), value)
+                if j == BLOCKS - 1:
+                    value = jnp.where(lane >= LANES - HALO, turn(seams, LANES - RIGHT - SEAM), value)
                 flat[pl.ds(base, 8), pl.ds(j * LANES, LANES)] = value
                 stacked[j, pl.ds(base, 8), :] = value
         rows = pl.ds(p * H // parts, H // parts)
@@ -661,7 +674,7 @@
 )
 
 
-def own_levels(x, coef, v0, v1, v2):
+def own_levels(x, coef, v0, v1, v2, w):
     return pl.pallas_call(
         own_kernel,
         out_shape=(
@@ -669,7 +682,7 @@
             jax.ShapeDtypeStruct((H // 2, W // 2), f32),
             *LEVELS,
         ),
-        in_specs=[WHOLE] * 5,
+        in_specs=[WHOLE] * 6,
         out_specs=(FAR,) * 4,
         scratch_shapes=[
             pltpu.VMEM((H, W), f32),
@@ -681,7 +694,7 @@
         compiler_params=LIMIT,
         cost_estimate=cost(2),
         name="own_levels",
-    )(*held(x, coef, v0, v1, v2))
+    )(*held(x, coef, v0, v1, v2, w))
 
 
 def other_kernel(x, mid_in, coarse_in, mid_out, coarse_out, coarse, sem):
@@ -729,13 +742,13 @@
     ext, lext, left, right, v0, v1, v2, totals, base = load(planes, marks)
     c_even, c_odd = exchange(*pack_columns(r_even, r_odd, left, right), "col")
     v0, v1, v2, base, totals = inner(ext, lext, v0, v1, v2, base, r_even, r_odd, totals)
+    pooled, totals = lax.optimization_barrier((pool(v0, v1, v2), totals))
     w, sums = seam(base, totals, c_even, c_odd)
-    v0, v1, v2, pooled = pool(v0, v1, v2, w)
     sums = lax.all_to_all(sums, ALL, split_axis=0, concat_axis=0, tiled=True)
-    coef, mid = solve(sums.reshape(256, LANES), pooled)
+    coef, mid = solve(sums.reshape(256, LANES), pooled, w)
     mid = lax.all_to_all(mid, CHIP, split_axis=0, concat_axis=0, tiled=True)
     other = lax.ppermute(mid, "row_2", [(0, 1), (1, 0)])
-    blended, fine, overview_mid, overview_coarse = own_levels(mid, coef, v0, v1, v2)
+    blended, fine, overview_mid, overview_coarse = own_levels(mid, coef, v0, v1, v2, w)
     overview_mid, overview_coarse = other_levels(other, overview_mid, overview_coarse)
     overview_mid = overview_mid.reshape(8 * H, W // 4)
     overview_coarse = overview_coarse.reshape(4 * H, W // 8)

time: 64.4 us -> 63.7 us (0.989)
  blocking collectives: 13.2 us -> 44.3 us
  starting transfers between devices: 26.2 us -> 7.95 us
  waiting for transfers between devices: 14.5 us -> 1.5 us
    all_to_all x0 -> x1, blocking collectives: none -> 31.1 us  [per_device(): sums = lax.all_to_all(sums, ALL, split_axis=0, concat_axis=0, tiled=True)]
    all_to_all x1 -> x0, starting transfers between devices: 18.2 us -> none  [per_device(): sums = lax.all_to_all(sums, ALL, split_axis=0, concat_axis=0, tiled=True)]
    all_to_all x1 -> x0, waiting for transfers between devices: 12.2 us -> none  [per_device(): sums = lax.all_to_all(sums, ALL, split_axis=0, concat_axis=0, tiled=True)]
    ppermute x2, waiting for transfers between devices: 1 us -> 0.21 us  [exchange(): even = lax.ppermute(even, axis, swaps(devices, 0))]
    pallas_call x1, Pallas kernels: 1.49 us -> 0.83 us  [seam(): pl.pallas_call(seam_kernel, out_shape=(near((3, ROWS, LANES)), near((256,...]
  transfers between devices with their start and end apart: 6 -> 5, of which waited for: 4 -> 3; matrix products, arithmetic and copies ran while one was open for 0% -> 0% of each run, Pallas kernels for 9% -> 9%
where the time goes in v6:
time: 63.7 us; the launch traced here: 63.5 us
  blocking collectives  44.3 us (70%)
  Pallas kernels  8.95 us (14%)
  starting transfers between devices  7.95 us (12%)
  waiting for transfers between devices  1.5 us (2%)
  between operations  0.75 us (1%)
    all_to_all x1, blocking collectives, per_device(): sums = lax.all_to_all(sums, ALL, split_axis=0, concat_axis=0, tiled=True)  31.1 us
    all_to_all x1, blocking collectives, per_device(): mid = lax.all_to_all(mid, CHIP, split_axis=0, concat_axis=0, tiled=True)  13.2 us
    ppermute x2, starting transfers between devices, exchange(): even = lax.ppermute(even, axis, swaps(devices, 0))  3.32 us
    ppermute x2, starting transfers between devices, exchange(): odd = lax.ppermute(odd, axis, swaps(devices, 1))  2.57 us
    pallas_call x1, Pallas kernels, load(): pl.pallas_call(load_kernel, out_shape=(near((K, BLOCKS, ROWS, LANES)), ne...  2.4 us
    ppermute x1, starting transfers between devices, per_device(): other = lax.ppermute(mid, 'row_2', [(0, 1), (1, 0)])  2.06 us
    pallas_call x1, Pallas kernels, own_levels(): pl.pallas_call(own_kernel, out_shape=(jax.ShapeDtypeStruct((H, W), f32),...  1.46 us
  transfers between devices with their start and end apart: 5, of which 3 were waited for; matrix products, arithmetic and copies ran while one was open for 0% of the time, Pallas kernels for 9%

profile of v6, /device:TPU:1, one launch (start us, length us, event | category | flops | bytes accessed | tf_op | source)
XLA Modules:
  0.0 63.5 jit_solution(8034909307151486890)
XLA Ops:
  0.6 0.0 copy-start.1
  0.6 0.0 copy-start
  0.7 1.2 %pack_rows.1 = (f32[16,1024]{1,0:T(8,128)S(1)}, f32[16,1024]{1,0:T(8,128)S(1)}) custom-call(f32[3,128,1024]{2,1,0:T(8,128)} %src.2, s32[128,1024]{1,0:T(8,128)} %lab.2), custom_call_target="tpu_custom_call" | custom-call | flops 300000000 | tf_op jit(solution)/shard_map/pack_rows/pallas_call | solution.py:90
  1.8 3.3 %collective-permute-start = (f32[16,1024]{1,0:T(8,128)S(1)}, f32[16,1024]{1,0:T(8,128)S(1)}, u32[]{:S(2)}, u32[]{:S(2)}) collective-permute-start(f32[16,1024]{1,0:T(8,128)S(1)} %get-tuple-element.48), channel_id=1, source_target_pairs={{0,8},{16,24},{32,40},{48,56},{64,72},{80,88},{96,104},{112,120},{... | collective-permute-start | bytes 196616 | tf_op jit(solution)/shard_map/ppermute | solution.py:734
  5.1 1.9 %collective-permute-start.1 = (f32[16,1024]{1,0:T(8,128)S(1)}, f32[16,1024]{1,0:T(8,128)S(1)}, u32[]{:S(2)}, u32[]{:S(2)}) collective-permute-start(f32[16,1024]{1,0:T(8,128)S(1)} %get-tuple-element.49), channel_id=1, source_target_pairs={{8,16},{24,32},{40,48},{56,64},{72,80},{88,96},{104,112},{120,128}... | collective-permute-start | bytes 196616 | tf_op jit(solution)/shard_map/ppermute | solution.py:733
  7.0 0.0 copy-done.1
  7.0 0.0 copy-done
  7.0 2.4 %load_block.1 = (f32[3,8,168,128]{3,2,1,0:T(8,128)S(1)}, s32[8,168,128]{2,1,0:T(8,128)S(1)}, f32[16,128]{1,0:T(8,128)S(1)}, f32[16,128]{1,0:T(8,128)S(1)}, f32[8...) custom-call(f32[3,128,1024]{2,1,0:T(8,128)S(1)} %copy-done, ...), custom_call_target="tpu_custom_call" | custom-call | flops 900000000 | tf_op jit(solution)/shard_map/load_block/pallas_call | solution.py:149
  9.5 0.0 collective-permute-done.refs_6_.got_even
  9.5 1.2 %collective-permute-done.1.refs_7_.got_odd = f32[16,1024]{1,0:T(8,128)S(1)} collective-permute-done((f32[16,1024]{1,0:T(8,128)S(1)}, f32[16,1024]{1,0:T(8,128)S(1)}, u32[]{:S(2)}, u32[]{:S(2)}) %collective-permute-start.1) | collective-permute-done | bytes 65568 | tf_op jit(solution)/shard_map/ppermute | solution.py:733
  10.7 0.1 pack_columns.1
  10.8 0.0 collective-permute-start.2
  10.8 0.7 %collective-permute-start.3 = (f32[24,128]{1,0:T(8,128)S(1)}, f32[24,128]{1,0:T(8,128)S(1)}, u32[]{:S(2)}, u32[]{:S(2)}) collective-permute-start(f32[24,128]{1,0:T(8,128)S(1)} %get-tuple-element.60), channel_id=1, source_target_pairs={{1,2},{3,4},{5,6},{2,1},{4,3},{6,5},{9,10},{11,12},{13,14},{10,9},... | collective-permute-start | bytes 36872 | tf_op jit(solution)/shard_map/ppermute | solution.py:733
  11.5 0.9 %inner_fields.1 = (f32[3,8,168,128]{3,2,1,0:T(8,128)S(1)}, s32[8,168,128]{2,1,0:T(8,128)S(1)}, f32[8,168,128]{2,1,0:T(8,128)S(1)}, f32[8,168,128]{2,1,0:T(8,128)...) custom-call(f32[3,8,168,128]{3,2,1,0:T(8,128)S(1)} %get-tuple-elemen, ...), custom_call_target="tpu_custom_call", output_to_operand_aliasing={{0}: (0, {}), {1}: (1, {}), {2}: (2, {}), {3}: (3, {}), {4}... | custom-call | flops 600000000 | tf_op jit(solution)/shard_map/inner_fields/pallas_call | solution.py:342
  12.3 0.8 %pool_fields.1.pooled = f32[3,2,32,128]{3,2,1,0:T(8,128)S(1)} custom-call(f32[8,168,128]{2,1,0:T(8,128)S(1)} %get-tuple-element.52.v0, f32[8,168,128]{2,1,0:T(8,128)S(1)} %get-tuple-element.53.v1, f32[8,168,128]{2,1,0:T(8,128)S(1)} %get-tuple-element.54.v2), custom_call_target="tpu_custom_call" | custom-call | flops 300000000 | tf_op jit(solution)/shard_map/pool_fields/pallas_call | solution.py:463
  13.1 0.2 collective-permute-done.2.c_even
  13.3 0.0 collective-permute-done.3.c_odd
  13.3 0.8 %seam_fields.1 = (f32[3,168,128]{2,1,0:T(8,128)S(1)}, f32[256,1,128]{2,1,0:T(1,128)S(1)}) custom-call(f32[4,168,128]{2,1,0:T(8,128)S(1)} %get-tuple-element.51.base, f32[6,8,128]{2,1,0:T(8,128)S(1)} %get-tuple-element.56.totals_in, f32[24,128]{1,0:T(8,128)S(1)} %collective-permute-done.2.c_even, f32[24,128]{1,0:T(8,128)S(1)} %collective-permute-done.3.c_odd), custom_call_target="tpu_custom_call" | custom-call | flops 300000000 | tf_op jit(solution)/shard_map/seam_fields/pallas_call | solution.py:437
  14.2 31.1 %all_to_all.10 = f32[256,1,128]{2,1,0:T(1,128)S(1)} all-to-all(f32[256,1,128]{2,1,0:T(1,128)S(1)} %get-tuple-element.61), channel_id=1, replica_groups=mesh['row_0'=4,'row_1'=4,'row_2'=2,'col'=8] {'row_0','row_1','row_2','col'}, dimensions={0} | all-to-all | bytes 262144 | tf_op jit(solution)/shard_map/all_to_all | solution.py:747
  45.3 0.3 coefficients.1
  45.6 13.2 %all_to_all.11.x = f32[16,2,32,128]{3,2,1,0:T(8,128)S(1)} all-to-all(f32[16,2,32,128]{3,2,1,0:T(8,128)S(1)} %get-tuple-element.64), channel_id=1, replica_groups=mesh['row_0'=4,'row_1'=4,'row_2'=2,'col'=8] {'row_0','row_1'}, dimensions={0} | all-to-all | bytes 1048576 | tf_op jit(solution)/shard_map/all_to_all | solution.py:749
  58.8 2.1 %collective-permute-start.4 = (f32[16,2,32,128]{3,2,1,0:T(8,128)S(1)}, f32[16,2,32,128]{3,2,1,0:T(8,128)S(1)}, u32[]{:S(2)}, u32[]{:S(2)}) collective-permute-start(f32[16,2,32,128]{3,2,1,0:T(8,128)S(1)} %all_to_all.11.x), channel_id=1, source_target_pairs={{0,8},{8,0},{1,9},{9,1},{2,10},{10,2},{3,11},{11,3},{4,12},{12,4},... | collective-permute-start | bytes 1572872 | tf_op jit(solution)/shard_map/ppermute | solution.py:750
  60.9 1.5 %own_levels.1 = (f32[128,1024]{1,0:T(8,128)}, f32[64,512]{1,0:T(8,128)}, f32[16,2,32,256]{3,2,1,0:T(8,128)}, f32[16,2,16,128]{3,2,1,0:T(8,128)}) custom-call(f32[16,2,32,128]{3,2,1,0:T(8,128)S(1)} %all_to_all.11.x, f32[3,8,128]{2,1,0:T(8,128)S(1)} %get-tuple-element.65.coef, f32[8,168,128]{2,1,0:T(8,128)S(1)} %get-tuple-element.52.v0, ...), custom_call_target="tpu_custom_call" | custom-call | flops 600000000 | tf_op jit(solution)/shard_map/own_levels/pallas_call | solution.py:678
  62.3 0.1 collective-permute-done.4.x
  62.4 1.1 %other_levels.1 = (f32[16,2,32,256]{3,2,1,0:T(8,128)}, f32[16,2,16,128]{3,2,1,0:T(8,128)}) custom-call(f32[16,2,32,128]{3,2,1,0:T(8,128)S(1)} %collective-permute-done.4.x, f32[16,2,32,256]{3,2,1,0:T(8,128)} %get-tuple-element.68.mid_in, f32[16,2,16,128]{3,2,1,0:T(8,128)} %get-tuple-element.69.coarse_in), custom_call_target="tpu_custom_call", output_to_operand_aliasing={{0}: (1, {}), {1}: (2, {})} | custom-call | flops 300000000 | tf_op jit(solution)/shard_map/other_levels/pallas_call | solution.py:710
Async XLA Ops:
  0.6 6.4 %copy-start.1 = (s32[128,1024]{1,0:T(8,128)S(1)}, s32[128,1024]{1,0:T(8,128)}, u32[]{:S(2)}) copy-start(s32[128,1024]{1,0:T(8,128)} %lab.2) | copy-start | bytes 1572868
  0.6 6.4 %copy-start = (f32[3,128,1024]{2,1,0:T(8,128)S(1)}, f32[3,128,1024]{2,1,0:T(8,128)}, u32[]{:S(2)}) copy-start(f32[3,128,1024]{2,1,0:T(8,128)} %src.2) | copy-start | bytes 4718596
  1.8 7.6 %collective-permute-start = (f32[16,1024]{1,0:T(8,128)S(1)}, f32[16,1024]{1,0:T(8,128)S(1)}, u32[]{:S(2)}, u32[]{:S(2)}) collective-permute-start(f32[16,1024]{1,0:T(8,128)S(1)} %get-tuple-element.48), channel_id=1, source_target_pairs={{0,8},{16,24},{32,40},{48,56},{64,72},{80,88},{96,104},{112,120},{... | collective-permute-start | bytes 196616 | tf_op jit(solution)/shard_map/ppermute | solution.py:734
  5.1 5.6 %collective-permute-start.1 = (f32[16,1024]{1,0:T(8,128)S(1)}, f32[16,1024]{1,0:T(8,128)S(1)}, u32[]{:S(2)}, u32[]{:S(2)}) collective-permute-start(f32[16,1024]{1,0:T(8,128)S(1)} %get-tuple-element.49), channel_id=1, source_target_pairs={{8,16},{24,32},{40,48},{56,64},{72,80},{88,96},{104,112},{120,128}... | collective-permute-start | bytes 196616 | tf_op jit(solution)/shard_map/ppermute | solution.py:733
  10.8 2.6 %collective-permute-start.2 = (f32[24,128]{1,0:T(8,128)S(1)}, f32[24,128]{1,0:T(8,128)S(1)}, u32[]{:S(2)}, u32[]{:S(2)}) collective-permute-start(f32[24,128]{1,0:T(8,128)S(1)} %get-tuple-element.59), channel_id=1, source_target_pairs={{0,1},{2,3},{4,5},{6,7},{1,0},{3,2},{5,4},{7,6},{8,9},{10,11},{12,... | collective-permute-start | bytes 36872 | tf_op jit(solution)/shard_map/ppermute | solution.py:734
  10.8 2.5 %collective-permute-start.3 = (f32[24,128]{1,0:T(8,128)S(1)}, f32[24,128]{1,0:T(8,128)S(1)}, u32[]{:S(2)}, u32[]{:S(2)}) collective-permute-start(f32[24,128]{1,0:T(8,128)S(1)} %get-tuple-element.60), channel_id=1, source_target_pairs={{1,2},{3,4},{5,6},{2,1},{4,3},{6,5},{9,10},{11,12},{13,14},{10,9},... | collective-permute-start | bytes 36872 | tf_op jit(solution)/shard_map/ppermute | solution.py:733
  58.8 3.6 %collective-permute-start.4 = (f32[16,2,32,128]{3,2,1,0:T(8,128)S(1)}, f32[16,2,32,128]{3,2,1,0:T(8,128)S(1)}, u32[]{:S(2)}, u32[]{:S(2)}) collective-permute-start(f32[16,2,32,128]{3,2,1,0:T(8,128)S(1)} %all_to_all.11.x), channel_id=1, source_target_pairs={{0,8},{8,0},{1,9},{9,1},{2,10},{10,2},{3,11},{11,3},{4,12},{12,4},... | collective-permute-start | bytes 1572872 | tf_op jit(solution)/shard_map/ppermute | solution.py:750

commit v7 on v6

--- a/solution.py
+++ b/solution.py
@@ -50,6 +50,16 @@
 
 def cost(us):
     return pl.CostEstimate(flops=int(us * 3e8), bytes_accessed=0, transcendentals=0)
+
+
+def sums_of(x, weights):
+    total = None
+    for _ in range(3):
+        part = x.astype(jnp.bfloat16)
+        x = x - part.astype(f32)
+        term = jnp.dot(part, weights, preferred_element_type=f32)
+        total = term if total is None else total + term
+    return total
 
 
 def pack_kernel(src, lab, even_out, odd_out, rows, lrows, sem):
@@ -454,9 +464,7 @@
             for j in range(4):
                 at = [ref[4 * g + j, pl.ds(TOP + q, H // 4, stride=4), :] for q in range(4)]
                 parts.append((at[0] + at[1]) + (at[2] + at[3]))
-            out[i, g] = jnp.dot(
-                jnp.concatenate(parts, 1), spread, precision=lax.Precision.HIGHEST, preferred_element_type=f32
-            )
+            out[i, g] = sums_of(jnp.concatenate(parts, 1), spread.astype(jnp.bfloat16))
 
 
 def pool(v0, v1, v2):
@@ -514,13 +522,16 @@
     h2 = m4 - s * m3 - b1 * m2
     third = second & (h2 > 0.0)
     safe3 = jnp.where(third, h2, one)
-    theta1 = theta0 + s
-    theta2 = theta0 - s + (m5 - s * m4 - b1 * m3) / safe3
+    theta1 = jnp.clip(theta0 + s, -4.0, 4.0)
+    theta2 = jnp.clip(theta0 - s + (m5 - s * m4 - b1 * m3) / safe3, -4.0, 4.0)
     b2 = h2 / safe2
     d0, d1, d2 = 4.0 - theta0, 4.0 - theta1, 4.0 - theta2
     e = d1 * d2 - b2
-    y2 = jnp.where(third, one / (d0 * e - b1 * d2), zero)
-    y1 = jnp.where(third, d2 * y2, jnp.where(second, one / (d0 * d1 - b1), zero))
+    two, three = d0 * d1 - b1, d0 * e - b1 * d2
+    second = second & (two > 0.0)
+    third = second & third & (three > 0.0)
+    y2 = jnp.where(third, one / three, zero)
+    y1 = jnp.where(third, d2 * y2, jnp.where(second, one / two, zero))
     y0 = jnp.where(third, e * y2, jnp.where(second, d1 * y1, one / d0))
     return (
         y0 - theta0 * y1 + (theta0 * theta1 - b1) * y2,
@@ -537,12 +548,8 @@
     for i in range(3):
         at = [w[i, pl.ds(TOP + q, H // 4, stride=4), :] for q in range(4)]
         rows.append((at[0] + at[1]) + (at[2] + at[3]))
-    edges = jnp.dot(
-        jnp.concatenate(rows, 0),
-        jnp.where(first | final, f32(0.0625), f32(0.0)),
-        precision=lax.Precision.HIGHEST,
-        preferred_element_type=f32,
-    )
+    weights = jnp.where(first | final, f32(0.0625), f32(0.0)).astype(jnp.bfloat16)
+    edges = sums_of(jnp.concatenate(rows, 0), weights)
     tiles = [(all_sums[pl.ds(8 * i, 8), :], jnp.zeros((8, LANES), f32)) for i in range(32)]
     while len(tiles) > 1:
         merged = []
@@ -597,12 +604,7 @@
 
 
 def pooled_rows(parts):
-    return jnp.dot(
-        jnp.concatenate(parts, 1),
-        half_matrix(2 * LANES),
-        precision=lax.Precision.HIGHEST,
-        preferred_element_type=f32,
-    )
+    return sums_of(jnp.concatenate(parts, 1), half_matrix(2 * LANES).astype(jnp.bfloat16))
 
 
 def store_mid(x, core, mid_out, sem):

time: 63.7 us -> 63.6 us (level)
  Pallas kernels: 8.95 us -> 8.3 us
  transfers between devices with their start and end apart: 5 -> 5, of which waited for: 3 -> 3; matrix products, arithmetic and copies ran while one was open for 0% -> 0% of each run, Pallas kernels for 9% -> 8%
where the time goes in v7:
time: 63.6 us; the launch traced here: 63.4 us
  blocking collectives  44.3 us (70%)
  Pallas kernels  8.3 us (13%)
  starting transfers between devices  7.95 us (12%)
  waiting for transfers between devices  2.04 us (3%)
  between operations  0.75 us (1%)
    all_to_all x1, blocking collectives, per_device(): sums = lax.all_to_all(sums, ALL, split_axis=0, concat_axis=0, tiled=True)  31.1 us
    all_to_all x1, blocking collectives, per_device(): mid = lax.all_to_all(mid, CHIP, split_axis=0, concat_axis=0, tiled=True)  13.2 us
    ppermute x2, starting transfers between devices, exchange(): even = lax.ppermute(even, axis, swaps(devices, 0))  3.32 us
    ppermute x2, starting transfers between devices, exchange(): odd = lax.ppermute(odd, axis, swaps(devices, 1))  2.57 us
    pallas_call x1, Pallas kernels, load(): pl.pallas_call(load_kernel, out_shape=(near((K, BLOCKS, ROWS, LANES)), ne...  2.4 us
    ppermute x1, starting transfers between devices, per_device(): other = lax.ppermute(mid, 'row_2', [(0, 1), (1, 0)])  2.06 us
  transfers between devices with their start and end apart: 5, of which 3 were waited for; matrix products, arithmetic and copies ran while one was open for 0% of the time, Pallas kernels for 8%

profile of v7, /device:TPU:1, one launch (start us, length us, event | category | flops | bytes accessed | tf_op | source)
XLA Modules:
  0.0 63.4 jit_solution(13041103386228710347)
XLA Ops:
  0.6 0.0 copy-start.1
  0.6 0.0 copy-start
  0.7 1.2 %pack_rows.1 = (f32[16,1024]{1,0:T(8,128)S(1)}, f32[16,1024]{1,0:T(8,128)S(1)}) custom-call(f32[3,128,1024]{2,1,0:T(8,128)} %src.2, s32[128,1024]{1,0:T(8,128)} %lab.2), custom_call_target="tpu_custom_call" | custom-call | flops 300000000 | tf_op jit(solution)/shard_map/pack_rows/pallas_call | solution.py:100
  1.8 3.3 %collective-permute-start = (f32[16,1024]{1,0:T(8,128)S(1)}, f32[16,1024]{1,0:T(8,128)S(1)}, u32[]{:S(2)}, u32[]{:S(2)}) collective-permute-start(f32[16,1024]{1,0:T(8,128)S(1)} %get-tuple-element.48), channel_id=1, source_target_pairs={{0,8},{16,24},{32,40},{48,56},{64,72},{80,88},{96,104},{112,120},{... | collective-permute-start | bytes 196616 | tf_op jit(solution)/shard_map/ppermute | solution.py:736
  5.1 1.9 %collective-permute-start.1 = (f32[16,1024]{1,0:T(8,128)S(1)}, f32[16,1024]{1,0:T(8,128)S(1)}, u32[]{:S(2)}, u32[]{:S(2)}) collective-permute-start(f32[16,1024]{1,0:T(8,128)S(1)} %get-tuple-element.49), channel_id=1, source_target_pairs={{8,16},{24,32},{40,48},{56,64},{72,80},{88,96},{104,112},{120,128}... | collective-permute-start | bytes 196616 | tf_op jit(solution)/shard_map/ppermute | solution.py:735
  7.0 0.0 copy-done.1
  7.0 0.0 copy-done
  7.0 2.4 %load_block.1 = (f32[3,8,168,128]{3,2,1,0:T(8,128)S(1)}, s32[8,168,128]{2,1,0:T(8,128)S(1)}, f32[16,128]{1,0:T(8,128)S(1)}, f32[16,128]{1,0:T(8,128)S(1)}, f32[8...) custom-call(f32[3,128,1024]{2,1,0:T(8,128)S(1)} %copy-done, ...), custom_call_target="tpu_custom_call" | custom-call | flops 900000000 | tf_op jit(solution)/shard_map/load_block/pallas_call | solution.py:159
  9.5 0.0 collective-permute-done.refs_6_.got_even
  9.5 1.2 %collective-permute-done.1.refs_7_.got_odd = f32[16,1024]{1,0:T(8,128)S(1)} collective-permute-done((f32[16,1024]{1,0:T(8,128)S(1)}, f32[16,1024]{1,0:T(8,128)S(1)}, u32[]{:S(2)}, u32[]{:S(2)}) %collective-permute-start.1) | collective-permute-done | bytes 65568 | tf_op jit(solution)/shard_map/ppermute | solution.py:735
  10.7 0.1 pack_columns.1
  10.8 0.0 collective-permute-start.2
  10.8 0.7 %collective-permute-start.3 = (f32[24,128]{1,0:T(8,128)S(1)}, f32[24,128]{1,0:T(8,128)S(1)}, u32[]{:S(2)}, u32[]{:S(2)}) collective-permute-start(f32[24,128]{1,0:T(8,128)S(1)} %get-tuple-element.60), channel_id=1, source_target_pairs={{1,2},{3,4},{5,6},{2,1},{4,3},{6,5},{9,10},{11,12},{13,14},{10,9},... | collective-permute-start | bytes 36872 | tf_op jit(solution)/shard_map/ppermute | solution.py:735
  11.5 0.9 %inner_fields.1 = (f32[3,8,168,128]{3,2,1,0:T(8,128)S(1)}, s32[8,168,128]{2,1,0:T(8,128)S(1)}, f32[8,168,128]{2,1,0:T(8,128)S(1)}, f32[8,168,128]{2,1,0:T(8,128)...) custom-call(f32[3,8,168,128]{3,2,1,0:T(8,128)S(1)} %get-tuple-elemen, ...), custom_call_target="tpu_custom_call", output_to_operand_aliasing={{0}: (0, {}), {1}: (1, {}), {2}: (2, {}), {3}: (3, {}), {4}... | custom-call | flops 600000000 | tf_op jit(solution)/shard_map/inner_fields/pallas_call | solution.py:352
  12.3 0.5 pool_fields.1.pooled
  12.8 0.5 collective-permute-done.2.c_even
  13.3 0.0 collective-permute-done.3.c_odd
  13.3 0.8 %seam_fields.1 = (f32[3,168,128]{2,1,0:T(8,128)S(1)}, f32[256,1,128]{2,1,0:T(1,128)S(1)}) custom-call(f32[4,168,128]{2,1,0:T(8,128)S(1)} %get-tuple-element.51.base, f32[6,8,128]{2,1,0:T(8,128)S(1)} %get-tuple-element.56.totals_in, f32[24,128]{1,0:T(8,128)S(1)} %collective-permute-done.2.c_even, f32[24,128]{1,0:T(8,128)S(1)} %collective-permute-done.3.c_odd), custom_call_target="tpu_custom_call" | custom-call | flops 300000000 | tf_op jit(solution)/shard_map/seam_fields/pallas_call | solution.py:447
  14.2 31.1 %all_to_all.10 = f32[256,1,128]{2,1,0:T(1,128)S(1)} all-to-all(f32[256,1,128]{2,1,0:T(1,128)S(1)} %get-tuple-element.61), channel_id=1, replica_groups=mesh['row_0'=4,'row_1'=4,'row_2'=2,'col'=8] {'row_0','row_1','row_2','col'}, dimensions={0} | all-to-all | bytes 262144 | tf_op jit(solution)/shard_map/all_to_all | solution.py:749
  45.3 0.3 coefficients.1
  45.6 13.2 %all_to_all.11.x = f32[16,2,32,128]{3,2,1,0:T(8,128)S(1)} all-to-all(f32[16,2,32,128]{3,2,1,0:T(8,128)S(1)} %get-tuple-element.64), channel_id=1, replica_groups=mesh['row_0'=4,'row_1'=4,'row_2'=2,'col'=8] {'row_0','row_1'}, dimensions={0} | all-to-all | bytes 1048576 | tf_op jit(solution)/shard_map/all_to_all | solution.py:751
  58.8 2.1 %collective-permute-start.4 = (f32[16,2,32,128]{3,2,1,0:T(8,128)S(1)}, f32[16,2,32,128]{3,2,1,0:T(8,128)S(1)}, u32[]{:S(2)}, u32[]{:S(2)}) collective-permute-start(f32[16,2,32,128]{3,2,1,0:T(8,128)S(1)} %all_to_all.11.x), channel_id=1, source_target_pairs={{0,8},{8,0},{1,9},{9,1},{2,10},{10,2},{3,11},{11,3},{4,12},{12,4},... | collective-permute-start | bytes 1572872 | tf_op jit(solution)/shard_map/ppermute | solution.py:752
  60.9 1.2 %own_levels.1 = (f32[128,1024]{1,0:T(8,128)}, f32[64,512]{1,0:T(8,128)}, f32[16,2,32,256]{3,2,1,0:T(8,128)}, f32[16,2,16,128]{3,2,1,0:T(8,128)}) custom-call(f32[16,2,32,128]{3,2,1,0:T(8,128)S(1)} %all_to_all.11.x, f32[3,8,128]{2,1,0:T(8,128)S(1)} %get-tuple-element.65.coef, f32[8,168,128]{2,1,0:T(8,128)S(1)} %get-tuple-element.52.v0, ...), custom_call_target="tpu_custom_call" | custom-call | flops 600000000 | tf_op jit(solution)/shard_map/own_levels/pallas_call | solution.py:680
  62.1 0.3 collective-permute-done.4.x
  62.4 0.9 %other_levels.1 = (f32[16,2,32,256]{3,2,1,0:T(8,128)}, f32[16,2,16,128]{3,2,1,0:T(8,128)}) custom-call(f32[16,2,32,128]{3,2,1,0:T(8,128)S(1)} %collective-permute-done.4.x, f32[16,2,32,256]{3,2,1,0:T(8,128)} %get-tuple-element.68.mid_in, f32[16,2,16,128]{3,2,1,0:T(8,128)} %get-tuple-element.69.coarse_in), custom_call_target="tpu_custom_call", output_to_operand_aliasing={{0}: (1, {}), {1}: (2, {})} | custom-call | flops 300000000 | tf_op jit(solution)/shard_map/other_levels/pallas_call | solution.py:712
Async XLA Ops:
  0.6 6.4 %copy-start.1 = (s32[128,1024]{1,0:T(8,128)S(1)}, s32[128,1024]{1,0:T(8,128)}, u32[]{:S(2)}) copy-start(s32[128,1024]{1,0:T(8,128)} %lab.2) | copy-start | bytes 1572868
  0.6 6.4 %copy-start = (f32[3,128,1024]{2,1,0:T(8,128)S(1)}, f32[3,128,1024]{2,1,0:T(8,128)}, u32[]{:S(2)}) copy-start(f32[3,128,1024]{2,1,0:T(8,128)} %src.2) | copy-start | bytes 4718596
  1.8 7.6 %collective-permute-start = (f32[16,1024]{1,0:T(8,128)S(1)}, f32[16,1024]{1,0:T(8,128)S(1)}, u32[]{:S(2)}, u32[]{:S(2)}) collective-permute-start(f32[16,1024]{1,0:T(8,128)S(1)} %get-tuple-element.48), channel_id=1, source_target_pairs={{0,8},{16,24},{32,40},{48,56},{64,72},{80,88},{96,104},{112,120},{... | collective-permute-start | bytes 196616 | tf_op jit(solution)/shard_map/ppermute | solution.py:736
  5.1 5.6 %collective-permute-start.1 = (f32[16,1024]{1,0:T(8,128)S(1)}, f32[16,1024]{1,0:T(8,128)S(1)}, u32[]{:S(2)}, u32[]{:S(2)}) collective-permute-start(f32[16,1024]{1,0:T(8,128)S(1)} %get-tuple-element.49), channel_id=1, source_target_pairs={{8,16},{24,32},{40,48},{56,64},{72,80},{88,96},{104,112},{120,128}... | collective-permute-start | bytes 196616 | tf_op jit(solution)/shard_map/ppermute | solution.py:735
  10.8 2.6 %collective-permute-start.2 = (f32[24,128]{1,0:T(8,128)S(1)}, f32[24,128]{1,0:T(8,128)S(1)}, u32[]{:S(2)}, u32[]{:S(2)}) collective-permute-start(f32[24,128]{1,0:T(8,128)S(1)} %get-tuple-element.59), channel_id=1, source_target_pairs={{0,1},{2,3},{4,5},{6,7},{1,0},{3,2},{5,4},{7,6},{8,9},{10,11},{12,... | collective-permute-start | bytes 36872 | tf_op jit(solution)/shard_map/ppermute | solution.py:736
  10.8 2.5 %collective-permute-start.3 = (f32[24,128]{1,0:T(8,128)S(1)}, f32[24,128]{1,0:T(8,128)S(1)}, u32[]{:S(2)}, u32[]{:S(2)}) collective-permute-start(f32[24,128]{1,0:T(8,128)S(1)} %get-tuple-element.60), channel_id=1, source_target_pairs={{1,2},{3,4},{5,6},{2,1},{4,3},{6,5},{9,10},{11,12},{13,14},{10,9},... | collective-permute-start | bytes 36872 | tf_op jit(solution)/shard_map/ppermute | solution.py:735
  58.8 3.6 %collective-permute-start.4 = (f32[16,2,32,128]{3,2,1,0:T(8,128)S(1)}, f32[16,2,32,128]{3,2,1,0:T(8,128)S(1)}, u32[]{:S(2)}, u32[]{:S(2)}) collective-permute-start(f32[16,2,32,128]{3,2,1,0:T(8,128)S(1)} %all_to_all.11.x), channel_id=1, source_target_pairs={{0,8},{8,0},{1,9},{9,1},{2,10},{10,2},{3,11},{11,3},{4,12},{12,4},... | collective-permute-start | bytes 1572872 | tf_op jit(solution)/shard_map/ppermute | solution.py:752

commit v8 on v7

--- a/solution.py
+++ b/solution.py
@@ -439,14 +439,15 @@
     for shift in (4, 2, 1):
         s, more = two_sum(s, pltpu.roll(s, shift, 0))
         e = e + pltpu.roll(e, shift, 0) + more
-    line = jnp.where(lane < 16, s, e)[:1].reshape(1, 1, LANES)
-    sums_out[...] = jnp.broadcast_to(line, (256, 1, LANES))
+    line = jnp.where(lane < 16, s, e)
+    for i in range(32):
+        sums_out[pl.ds(8 * i, 8), :] = line
 
 
 def seam(base, totals, c_even, c_odd):
     return pl.pallas_call(
         seam_kernel,
-        out_shape=(near((3, ROWS, LANES)), near((256, 1, LANES))),
+        out_shape=(near((3, ROWS, LANES)), near((256, LANES))),
         in_specs=[WHOLE] * 4,
         out_specs=(WHOLE,) * 2,
         scratch_shapes=[pltpu.VMEM((K + 1, ROWS, LANES), f32)],
@@ -746,6 +747,7 @@
     v0, v1, v2, base, totals = inner(ext, lext, v0, v1, v2, base, r_even, r_odd, totals)
     pooled, totals = lax.optimization_barrier((pool(v0, v1, v2), totals))
     w, sums = seam(base, totals, c_even, c_odd)
+    sums = sums.reshape(256, 1, LANES)
     sums = lax.all_to_all(sums, ALL, split_axis=0, concat_axis=0, tiled=True)
     coef, mid = solve(sums.reshape(256, LANES), pooled, w)
     mid = lax.all_to_all(mid, CHIP, split_axis=0, concat_axis=0, tiled=True)

time: 63.6 us -> 63.5 us (level)
  no operation moved by 1% of the time
where the time goes in v8:
time: 63.5 us; the launch traced here: 63.3 us
  blocking collectives  44.3 us (70%)
  Pallas kernels  8.23 us (13%)
  starting transfers between devices  7.95 us (13%)
  waiting for transfers between devices  2.04 us (3%)
  between operations  0.75 us (1%)
    all_to_all x1, blocking collectives, per_device(): sums = lax.all_to_all(sums, ALL, split_axis=0, concat_axis=0, tiled=True)  31.1 us
    all_to_all x1, blocking collectives, per_device(): mid = lax.all_to_all(mid, CHIP, split_axis=0, concat_axis=0, tiled=True)  13.2 us
    ppermute x2, starting transfers between devices, exchange(): even = lax.ppermute(even, axis, swaps(devices, 0))  3.32 us
    ppermute x2, starting transfers between devices, exchange(): odd = lax.ppermute(odd, axis, swaps(devices, 1))  2.57 us
    pallas_call x1, Pallas kernels, load(): pl.pallas_call(load_kernel, out_shape=(near((K, BLOCKS, ROWS, LANES)), ne...  2.4 us
    ppermute x1, starting transfers between devices, per_device(): other = lax.ppermute(mid, 'row_2', [(0, 1), (1, 0)])  2.06 us
  transfers between devices with their start and end apart: 5, of which 3 were waited for; matrix products, arithmetic and copies ran while one was open for 0% of the time, Pallas kernels for 8%

profile of v8, /device:TPU:1, one launch (start us, length us, event | category | flops | bytes accessed | tf_op | source)
XLA Modules:
  0.0 63.3 jit_solution(5550385170679369308)
XLA Ops:
  0.6 0.0 copy-start.1
  0.6 0.0 copy-start
  0.7 1.2 %pack_rows.1 = (f32[16,1024]{1,0:T(8,128)S(1)}, f32[16,1024]{1,0:T(8,128)S(1)}) custom-call(f32[3,128,1024]{2,1,0:T(8,128)} %src.2, s32[128,1024]{1,0:T(8,128)} %lab.2), custom_call_target="tpu_custom_call" | custom-call | flops 300000000 | tf_op jit(solution)/shard_map/pack_rows/pallas_call | solution.py:100
  1.8 3.3 %collective-permute-start = (f32[16,1024]{1,0:T(8,128)S(1)}, f32[16,1024]{1,0:T(8,128)S(1)}, u32[]{:S(2)}, u32[]{:S(2)}) collective-permute-start(f32[16,1024]{1,0:T(8,128)S(1)} %get-tuple-element.48), channel_id=1, source_target_pairs={{0,8},{16,24},{32,40},{48,56},{64,72},{80,88},{96,104},{112,120},{... | collective-permute-start | bytes 196616 | tf_op jit(solution)/shard_map/ppermute | solution.py:737
  5.1 1.9 %collective-permute-start.1 = (f32[16,1024]{1,0:T(8,128)S(1)}, f32[16,1024]{1,0:T(8,128)S(1)}, u32[]{:S(2)}, u32[]{:S(2)}) collective-permute-start(f32[16,1024]{1,0:T(8,128)S(1)} %get-tuple-element.49), channel_id=1, source_target_pairs={{8,16},{24,32},{40,48},{56,64},{72,80},{88,96},{104,112},{120,128}... | collective-permute-start | bytes 196616 | tf_op jit(solution)/shard_map/ppermute | solution.py:736
  7.0 0.0 copy-done.1
  7.0 0.0 copy-done
  7.0 2.4 %load_block.1 = (f32[3,8,168,128]{3,2,1,0:T(8,128)S(1)}, s32[8,168,128]{2,1,0:T(8,128)S(1)}, f32[16,128]{1,0:T(8,128)S(1)}, f32[16,128]{1,0:T(8,128)S(1)}, f32[8...) custom-call(f32[3,128,1024]{2,1,0:T(8,128)S(1)} %copy-done, ...), custom_call_target="tpu_custom_call" | custom-call | flops 900000000 | tf_op jit(solution)/shard_map/load_block/pallas_call | solution.py:159
  9.5 0.0 collective-permute-done.refs_6_.got_even
  9.5 1.2 %collective-permute-done.1.refs_7_.got_odd = f32[16,1024]{1,0:T(8,128)S(1)} collective-permute-done((f32[16,1024]{1,0:T(8,128)S(1)}, f32[16,1024]{1,0:T(8,128)S(1)}, u32[]{:S(2)}, u32[]{:S(2)}) %collective-permute-start.1) | collective-permute-done | bytes 65568 | tf_op jit(solution)/shard_map/ppermute | solution.py:736
  10.7 0.1 pack_columns.1
  10.8 0.0 collective-permute-start.2
  10.8 0.7 %collective-permute-start.3 = (f32[24,128]{1,0:T(8,128)S(1)}, f32[24,128]{1,0:T(8,128)S(1)}, u32[]{:S(2)}, u32[]{:S(2)}) collective-permute-start(f32[24,128]{1,0:T(8,128)S(1)} %get-tuple-element.60), channel_id=1, source_target_pairs={{1,2},{3,4},{5,6},{2,1},{4,3},{6,5},{9,10},{11,12},{13,14},{10,9},... | collective-permute-start | bytes 36872 | tf_op jit(solution)/shard_map/ppermute | solution.py:736
  11.5 0.9 %inner_fields.1 = (f32[3,8,168,128]{3,2,1,0:T(8,128)S(1)}, s32[8,168,128]{2,1,0:T(8,128)S(1)}, f32[8,168,128]{2,1,0:T(8,128)S(1)}, f32[8,168,128]{2,1,0:T(8,128)...) custom-call(f32[3,8,168,128]{3,2,1,0:T(8,128)S(1)} %get-tuple-elemen, ...), custom_call_target="tpu_custom_call", output_to_operand_aliasing={{0}: (0, {}), {1}: (1, {}), {2}: (2, {}), {3}: (3, {}), {4}... | custom-call | flops 600000000 | tf_op jit(solution)/shard_map/inner_fields/pallas_call | solution.py:352
  12.3 0.5 pool_fields.1.pooled
  12.8 0.5 collective-permute-done.2.c_even
  13.3 0.0 collective-permute-done.3.c_odd
  13.3 0.8 %seam_fields.1 = (f32[3,168,128]{2,1,0:T(8,128)S(1)}, f32[256,128]{1,0:T(8,128)S(1)}) custom-call(f32[4,168,128]{2,1,0:T(8,128)S(1)} %get-tuple-element.51.base, f32[6,8,128]{2,1,0:T(8,128)S(1)} %get-tuple-element.56.totals_in, f32[24,128]{1,0:T(8,128)S(1)} %collective-permute-done.2.c_even, f32[24,128]{1,0:T(8,128)S(1)} %collective-permute-done.3.c_odd), custom_call_target="tpu_custom_call" | custom-call | flops 300000000 | tf_op jit(solution)/shard_map/seam_fields/pallas_call | solution.py:448
  14.1 31.1 %all_to_all.10 = f32[256,1,128]{2,1,0:T(1,128)S(1)} all-to-all(f32[256,1,128]{2,1,0:T(1,128)S(1)} %bitcast.6), channel_id=1, replica_groups=mesh['row_0'=4,'row_1'=4,'row_2'=2,'col'=8] {'row_0','row_1','row_2','col'}, dimensions={0} | all-to-all | bytes 262144 | tf_op jit(solution)/shard_map/all_to_all | solution.py:751
  45.2 0.3 coefficients.1
  45.5 13.2 %all_to_all.11.x = f32[16,2,32,128]{3,2,1,0:T(8,128)S(1)} all-to-all(f32[16,2,32,128]{3,2,1,0:T(8,128)S(1)} %get-tuple-element.64), channel_id=1, replica_groups=mesh['row_0'=4,'row_1'=4,'row_2'=2,'col'=8] {'row_0','row_1'}, dimensions={0} | all-to-all | bytes 1048576 | tf_op jit(solution)/shard_map/all_to_all | solution.py:753
  58.7 2.1 %collective-permute-start.4 = (f32[16,2,32,128]{3,2,1,0:T(8,128)S(1)}, f32[16,2,32,128]{3,2,1,0:T(8,128)S(1)}, u32[]{:S(2)}, u32[]{:S(2)}) collective-permute-start(f32[16,2,32,128]{3,2,1,0:T(8,128)S(1)} %all_to_all.11.x), channel_id=1, source_target_pairs={{0,8},{8,0},{1,9},{9,1},{2,10},{10,2},{3,11},{11,3},{4,12},{12,4},... | collective-permute-start | bytes 1572872 | tf_op jit(solution)/shard_map/ppermute | solution.py:754
  60.8 1.2 %own_levels.1 = (f32[128,1024]{1,0:T(8,128)}, f32[64,512]{1,0:T(8,128)}, f32[16,2,32,256]{3,2,1,0:T(8,128)}, f32[16,2,16,128]{3,2,1,0:T(8,128)}) custom-call(f32[16,2,32,128]{3,2,1,0:T(8,128)S(1)} %all_to_all.11.x, f32[3,8,128]{2,1,0:T(8,128)S(1)} %get-tuple-element.65.coef, f32[8,168,128]{2,1,0:T(8,128)S(1)} %get-tuple-element.52.v0, ...), custom_call_target="tpu_custom_call" | custom-call | flops 600000000 | tf_op jit(solution)/shard_map/own_levels/pallas_call | solution.py:681
  62.1 0.3 collective-permute-done.4.x
  62.3 0.9 %other_levels.1 = (f32[16,2,32,256]{3,2,1,0:T(8,128)}, f32[16,2,16,128]{3,2,1,0:T(8,128)}) custom-call(f32[16,2,32,128]{3,2,1,0:T(8,128)S(1)} %collective-permute-done.4.x, f32[16,2,32,256]{3,2,1,0:T(8,128)} %get-tuple-element.68.mid_in, f32[16,2,16,128]{3,2,1,0:T(8,128)} %get-tuple-element.69.coarse_in), custom_call_target="tpu_custom_call", output_to_operand_aliasing={{0}: (1, {}), {1}: (2, {})} | custom-call | flops 300000000 | tf_op jit(solution)/shard_map/other_levels/pallas_call | solution.py:713
Async XLA Ops:
  0.6 6.4 %copy-start.1 = (s32[128,1024]{1,0:T(8,128)S(1)}, s32[128,1024]{1,0:T(8,128)}, u32[]{:S(2)}) copy-start(s32[128,1024]{1,0:T(8,128)} %lab.2) | copy-start | bytes 1572868
  0.6 6.4 %copy-start = (f32[3,128,1024]{2,1,0:T(8,128)S(1)}, f32[3,128,1024]{2,1,0:T(8,128)}, u32[]{:S(2)}) copy-start(f32[3,128,1024]{2,1,0:T(8,128)} %src.2) | copy-start | bytes 4718596
  1.8 7.6 %collective-permute-start = (f32[16,1024]{1,0:T(8,128)S(1)}, f32[16,1024]{1,0:T(8,128)S(1)}, u32[]{:S(2)}, u32[]{:S(2)}) collective-permute-start(f32[16,1024]{1,0:T(8,128)S(1)} %get-tuple-element.48), channel_id=1, source_target_pairs={{0,8},{16,24},{32,40},{48,56},{64,72},{80,88},{96,104},{112,120},{... | collective-permute-start | bytes 196616 | tf_op jit(solution)/shard_map/ppermute | solution.py:737
  5.1 5.6 %collective-permute-start.1 = (f32[16,1024]{1,0:T(8,128)S(1)}, f32[16,1024]{1,0:T(8,128)S(1)}, u32[]{:S(2)}, u32[]{:S(2)}) collective-permute-start(f32[16,1024]{1,0:T(8,128)S(1)} %get-tuple-element.49), channel_id=1, source_target_pairs={{8,16},{24,32},{40,48},{56,64},{72,80},{88,96},{104,112},{120,128}... | collective-permute-start | bytes 196616 | tf_op jit(solution)/shard_map/ppermute | solution.py:736
  10.8 2.6 %collective-permute-start.2 = (f32[24,128]{1,0:T(8,128)S(1)}, f32[24,128]{1,0:T(8,128)S(1)}, u32[]{:S(2)}, u32[]{:S(2)}) collective-permute-start(f32[24,128]{1,0:T(8,128)S(1)} %get-tuple-element.59), channel_id=1, source_target_pairs={{0,1},{2,3},{4,5},{6,7},{1,0},{3,2},{5,4},{7,6},{8,9},{10,11},{12,... | collective-permute-start | bytes 36872 | tf_op jit(solution)/shard_map/ppermute | solution.py:737
  10.8 2.5 %collective-permute-start.3 = (f32[24,128]{1,0:T(8,128)S(1)}, f32[24,128]{1,0:T(8,128)S(1)}, u32[]{:S(2)}, u32[]{:S(2)}) collective-permute-start(f32[24,128]{1,0:T(8,128)S(1)} %get-tuple-element.60), channel_id=1, source_target_pairs={{1,2},{3,4},{5,6},{2,1},{4,3},{6,5},{9,10},{11,12},{13,14},{10,9},... | collective-permute-start | bytes 36872 | tf_op jit(solution)/shard_map/ppermute | solution.py:736
  58.7 3.6 %collective-permute-start.4 = (f32[16,2,32,128]{3,2,1,0:T(8,128)S(1)}, f32[16,2,32,128]{3,2,1,0:T(8,128)S(1)}, u32[]{:S(2)}, u32[]{:S(2)}) collective-permute-start(f32[16,2,32,128]{3,2,1,0:T(8,128)S(1)} %all_to_all.11.x), channel_id=1, source_target_pairs={{0,8},{8,0},{1,9},{9,1},{2,10},{10,2},{3,11},{11,3},{4,12},{12,4},... | collective-permute-start | bytes 1572872 | tf_op jit(solution)/shard_map/ppermute | solution.py:754

commit v9 on v7

--- a/solution.py
+++ b/solution.py
@@ -16,7 +16,6 @@
 HALO = 4
 ROW = ("row_0", "row_1", "row_2")
 CHIP = ("row_0", "row_1")
-ALL = ("row_0", "row_1", "row_2", "col")
 VMEM = pltpu.MemorySpace.VMEM
 WHOLE = pl.BlockSpec(memory_space=VMEM)
 FAR = pl.BlockSpec(memory_space=pltpu.MemorySpace.HBM)
@@ -431,7 +430,7 @@
         big = 512.0 * jnp.max(jnp.abs(x), axis=1, keepdims=True)
         high = (x + big) - big
         line = jnp.where(
-            (lane == i) | (lane == i + 16),
+            (lane == i) | (lane == i + 16) | (lane == i + 24),
             jnp.sum(high, axis=1, keepdims=True),
             jnp.where(lane == i + 8, jnp.sum(x - high, axis=1, keepdims=True), line),
         )
@@ -439,14 +438,13 @@
     for shift in (4, 2, 1):
         s, more = two_sum(s, pltpu.roll(s, shift, 0))
         e = e + pltpu.roll(e, shift, 0) + more
-    line = jnp.where(lane < 16, s, e)[:1].reshape(1, 1, LANES)
-    sums_out[...] = jnp.broadcast_to(line, (256, 1, LANES))
+    sums_out[...] = jnp.where(lane < 24, s, e)
 
 
 def seam(base, totals, c_even, c_odd):
     return pl.pallas_call(
         seam_kernel,
-        out_shape=(near((3, ROWS, LANES)), near((256, 1, LANES))),
+        out_shape=(near((3, ROWS, LANES)), near((8, LANES))),
         in_specs=[WHOLE] * 4,
         out_specs=(WHOLE,) * 2,
         scratch_shapes=[pltpu.VMEM((K + 1, ROWS, LANES), f32)],
@@ -454,6 +452,24 @@
         cost_estimate=cost(1),
         name="seam_fields",
     )(*held(base, totals, c_even, c_odd))
+
+
+def merge_kernel(own, other, out):
+    s, e = two_sum(own[...], other[...])
+    line = jnp.where(window(iota((8, LANES), 1), 16, 8), e, s)
+    out[...] = jnp.broadcast_to(line[:1].reshape(1, 1, LANES), (128, 1, LANES))
+
+
+def merge(own, other):
+    return pl.pallas_call(
+        merge_kernel,
+        out_shape=near((128, 1, LANES)),
+        in_specs=[WHOLE] * 2,
+        out_specs=WHOLE,
+        compiler_params=LIMIT,
+        cost_estimate=cost(0.2),
+        name="merge_cores",
+    )(*held(own, other))
 
 
 def pool_kernel(v0, v1, v2, out):
@@ -550,7 +566,7 @@
         rows.append((at[0] + at[1]) + (at[2] + at[3]))
     weights = jnp.where(first | final, f32(0.0625), f32(0.0)).astype(jnp.bfloat16)
     edges = sums_of(jnp.concatenate(rows, 0), weights)
-    tiles = [(all_sums[pl.ds(8 * i, 8), :], jnp.zeros((8, LANES), f32)) for i in range(32)]
+    tiles = [(all_sums[pl.ds(8 * i, 8), :], jnp.zeros((8, LANES), f32)) for i in range(16)]
     while len(tiles) > 1:
         merged = []
         for a, b in zip(tiles[0::2], tiles[1::2]):
@@ -570,7 +586,9 @@
     n = []
     for i in range(6):
         high = over_lanes(jnp.where(lane == i, s, zero))
-        low = over_lanes(jnp.where((lane == i + 8) | (lane == i + 16), s, jnp.where(lane == i, e, zero)))
+        low = over_lanes(
+            jnp.where((lane == i + 8) | (lane == i + 16) | (lane == i + 24), s, jnp.where(lane == i, e, zero))
+        )
         n.append(two_sum(high, low))
     c = coefficients(n)
     for i in range(3):
@@ -746,8 +764,9 @@
     v0, v1, v2, base, totals = inner(ext, lext, v0, v1, v2, base, r_even, r_odd, totals)
     pooled, totals = lax.optimization_barrier((pool(v0, v1, v2), totals))
     w, sums = seam(base, totals, c_even, c_odd)
-    sums = lax.all_to_all(sums, ALL, split_axis=0, concat_axis=0, tiled=True)
-    coef, mid = solve(sums.reshape(256, LANES), pooled, w)
+    sums = merge(sums, lax.ppermute(sums, "row_2", [(0, 1), (1, 0)]))
+    sums = lax.all_to_all(sums, (*CHIP, "col"), split_axis=0, concat_axis=0, tiled=True)
+    coef, mid = solve(sums.reshape(128, LANES), pooled, w)
     mid = lax.all_to_all(mid, CHIP, split_axis=0, concat_axis=0, tiled=True)
     other = lax.ppermute(mid, "row_2", [(0, 1), (1, 0)])
     blended, fine, overview_mid, overview_coarse = own_levels(mid, coef, v0, v1, v2, w)

time: 63.6 us -> 63.4 us (level)
  blocking collectives: 44.3 us -> 42.4 us
  waiting for transfers between devices: 2.04 us -> 3.2 us
    all_to_all x1, blocking collectives: 31.1 us -> 29.9 us  [per_device(): lax.all_to_all(sums, (*CHIP, 'col'), split_axis=0, concat_axis=0, tiled=T...]
    ppermute x0 -> x1, waiting for transfers between devices: none -> 1.15 us  [per_device(): sums = merge(sums, lax.ppermute(sums, 'row_2', [(0, 1), (1, 0)]))]
    all_to_all x1, blocking collectives: 13.2 us -> 12.6 us  [per_device(): mid = lax.all_to_all(mid, CHIP, split_axis=0, concat_axis=0, tiled=True)]
  transfers between devices with their start and end apart: 5 -> 6, of which waited for: 3 -> 4; matrix products, arithmetic and copies ran while one was open for 0% -> 0% of each run, Pallas kernels for 8% -> 8%
where the time goes in v9:
time: 63.4 us; the launch traced here: 63.2 us
  blocking collectives  42.4 us (67%)
  starting transfers between devices  8.55 us (13%)
  Pallas kernels  8.24 us (13%)
  waiting for transfers between devices  3.2 us (5%)
  between operations  0.76 us (1%)
    all_to_all x1, blocking collectives, per_device(): lax.all_to_all(sums, (*CHIP, 'col'), split_axis=0, concat_axis=0, tiled=T...  29.9 us
    all_to_all x1, blocking collectives, per_device(): mid = lax.all_to_all(mid, CHIP, split_axis=0, concat_axis=0, tiled=True)  12.6 us
    ppermute x2, starting transfers between devices, exchange(): even = lax.ppermute(even, axis, swaps(devices, 0))  3.32 us
    ppermute x2, starting transfers between devices, exchange(): odd = lax.ppermute(odd, axis, swaps(devices, 1))  2.57 us
    ppermute x1, starting transfers between devices, per_device(): other = lax.ppermute(mid, 'row_2', [(0, 1), (1, 0)])  2.57 us
    pallas_call x1, Pallas kernels, load(): pl.pallas_call(load_kernel, out_shape=(near((K, BLOCKS, ROWS, LANES)), ne...  2.4 us
  transfers between devices with their start and end apart: 6, of which 4 were waited for; matrix products, arithmetic and copies ran while one was open for 0% of the time, Pallas kernels for 8%

profile of v9, /device:TPU:1, one launch (start us, length us, event | category | flops | bytes accessed | tf_op | source)
XLA Modules:
  0.0 63.2 jit_solution(9033899663978574962)
XLA Ops:
  0.6 0.0 copy-start.1
  0.6 0.0 copy-start
  0.7 1.2 %pack_rows.1 = (f32[16,1024]{1,0:T(8,128)S(1)}, f32[16,1024]{1,0:T(8,128)S(1)}) custom-call(f32[3,128,1024]{2,1,0:T(8,128)} %src.2, s32[128,1024]{1,0:T(8,128)} %lab.2), custom_call_target="tpu_custom_call" | custom-call | flops 300000000 | tf_op jit(solution)/shard_map/pack_rows/pallas_call | solution.py:99
  1.8 3.3 %collective-permute-start = (f32[16,1024]{1,0:T(8,128)S(1)}, f32[16,1024]{1,0:T(8,128)S(1)}, u32[]{:S(2)}, u32[]{:S(2)}) collective-permute-start(f32[16,1024]{1,0:T(8,128)S(1)} %get-tuple-element.48), channel_id=1, source_target_pairs={{0,8},{16,24},{32,40},{48,56},{64,72},{80,88},{96,104},{112,120},{... | collective-permute-start | bytes 196616 | tf_op jit(solution)/shard_map/ppermute | solution.py:754
  5.1 1.9 %collective-permute-start.1 = (f32[16,1024]{1,0:T(8,128)S(1)}, f32[16,1024]{1,0:T(8,128)S(1)}, u32[]{:S(2)}, u32[]{:S(2)}) collective-permute-start(f32[16,1024]{1,0:T(8,128)S(1)} %get-tuple-element.49), channel_id=1, source_target_pairs={{8,16},{24,32},{40,48},{56,64},{72,80},{88,96},{104,112},{120,128}... | collective-permute-start | bytes 196616 | tf_op jit(solution)/shard_map/ppermute | solution.py:753
  7.0 0.0 copy-done.1
  7.0 0.0 copy-done
  7.0 2.4 %load_block.1 = (f32[3,8,168,128]{3,2,1,0:T(8,128)S(1)}, s32[8,168,128]{2,1,0:T(8,128)S(1)}, f32[16,128]{1,0:T(8,128)S(1)}, f32[16,128]{1,0:T(8,128)S(1)}, f32[8...) custom-call(f32[3,128,1024]{2,1,0:T(8,128)S(1)} %copy-done, ...), custom_call_target="tpu_custom_call" | custom-call | flops 900000000 | tf_op jit(solution)/shard_map/load_block/pallas_call | solution.py:158
  9.5 0.0 collective-permute-done.refs_6_.got_even
  9.5 1.2 %collective-permute-done.1.refs_7_.got_odd = f32[16,1024]{1,0:T(8,128)S(1)} collective-permute-done((f32[16,1024]{1,0:T(8,128)S(1)}, f32[16,1024]{1,0:T(8,128)S(1)}, u32[]{:S(2)}, u32[]{:S(2)}) %collective-permute-start.1) | collective-permute-done | bytes 65568 | tf_op jit(solution)/shard_map/ppermute | solution.py:753
  10.7 0.1 pack_columns.1
  10.8 0.0 collective-permute-start.2
  10.8 0.7 %collective-permute-start.3 = (f32[24,128]{1,0:T(8,128)S(1)}, f32[24,128]{1,0:T(8,128)S(1)}, u32[]{:S(2)}, u32[]{:S(2)}) collective-permute-start(f32[24,128]{1,0:T(8,128)S(1)} %get-tuple-element.60), channel_id=1, source_target_pairs={{1,2},{3,4},{5,6},{2,1},{4,3},{6,5},{9,10},{11,12},{13,14},{10,9},... | collective-permute-start | bytes 36872 | tf_op jit(solution)/shard_map/ppermute | solution.py:753
  11.5 0.9 %inner_fields.1 = (f32[3,8,168,128]{3,2,1,0:T(8,128)S(1)}, s32[8,168,128]{2,1,0:T(8,128)S(1)}, f32[8,168,128]{2,1,0:T(8,128)S(1)}, f32[8,168,128]{2,1,0:T(8,128)...) custom-call(f32[3,8,168,128]{3,2,1,0:T(8,128)S(1)} %get-tuple-elemen, ...), custom_call_target="tpu_custom_call", output_to_operand_aliasing={{0}: (0, {}), {1}: (1, {}), {2}: (2, {}), {3}: (3, {}), {4}... | custom-call | flops 600000000 | tf_op jit(solution)/shard_map/inner_fields/pallas_call | solution.py:351
  12.3 0.5 pool_fields.1.pooled
  12.8 0.5 collective-permute-done.2.c_even
  13.3 0.0 collective-permute-done.3.c_odd
  13.3 0.8 %seam_fields.1 = (f32[3,168,128]{2,1,0:T(8,128)S(1)}, f32[8,128]{1,0:T(8,128)S(1)}) custom-call(f32[4,168,128]{2,1,0:T(8,128)S(1)} %get-tuple-element.51.base, f32[6,8,128]{2,1,0:T(8,128)S(1)} %get-tuple-element.56.totals_in, f32[24,128]{1,0:T(8,128)S(1)} %collective-permute-done.2.c_even, f32[24,128]{1,0:T(8,128)S(1)} %collective-permute-done.3.c_odd), custom_call_target="tpu_custom_call" | custom-call | flops 300000000 | tf_op jit(solution)/shard_map/seam_fields/pallas_call | solution.py:445
  14.1 0.1 collective-permute-start.4
  14.2 1.2 %collective-permute-done.4.other = f32[8,128]{1,0:T(8,128)S(1)} collective-permute-done((f32[8,128]{1,0:T(8,128)S(1)}, f32[8,128]{1,0:T(8,128)S(1)}, u32[]{:S(2)}, u32[]{:S(2)}) %collective-permute-start.4) | collective-permute-done | bytes 4128 | tf_op jit(solution)/shard_map/ppermute | solution.py:767
  15.4 29.9 %all_to_all.10 = f32[128,1,128]{2,1,0:T(1,128)S(1)} all-to-all(f32[128,1,128]{2,1,0:T(1,128)S(1)} %merge_cores.1), channel_id=1, replica_groups=mesh['row_0'=4,'row_1'=4,'row_2'=2,'col'=8] {'row_0','row_1','col'}, dimensions={0} | all-to-all | bytes 131072 | tf_op jit(solution)/shard_map/all_to_all | solution.py:768
  45.3 0.3 coefficients.1
  45.6 12.6 %all_to_all.11.x = f32[16,2,32,128]{3,2,1,0:T(8,128)S(1)} all-to-all(f32[16,2,32,128]{3,2,1,0:T(8,128)S(1)} %get-tuple-element.64), channel_id=1, replica_groups=mesh['row_0'=4,'row_1'=4,'row_2'=2,'col'=8] {'row_0','row_1'}, dimensions={0} | all-to-all | bytes 1048576 | tf_op jit(solution)/shard_map/all_to_all | solution.py:770
  58.1 2.6 %collective-permute-start.5 = (f32[16,2,32,128]{3,2,1,0:T(8,128)S(1)}, f32[16,2,32,128]{3,2,1,0:T(8,128)S(1)}, u32[]{:S(2)}, u32[]{:S(2)}) collective-permute-start(f32[16,2,32,128]{3,2,1,0:T(8,128)S(1)} %all_to_all.11.x), channel_id=1, source_target_pairs={{0,8},{8,0},{1,9},{9,1},{2,10},{10,2},{3,11},{11,3},{4,12},{12,4},... | collective-permute-start | bytes 1572872 | tf_op jit(solution)/shard_map/ppermute | solution.py:771
  60.7 1.2 %own_levels.1 = (f32[128,1024]{1,0:T(8,128)}, f32[64,512]{1,0:T(8,128)}, f32[16,2,32,256]{3,2,1,0:T(8,128)}, f32[16,2,16,128]{3,2,1,0:T(8,128)}) custom-call(f32[16,2,32,128]{3,2,1,0:T(8,128)S(1)} %all_to_all.11.x, f32[3,8,128]{2,1,0:T(8,128)S(1)} %get-tuple-element.65.coef, f32[8,168,128]{2,1,0:T(8,128)S(1)} %get-tuple-element.52.v0, ...), custom_call_target="tpu_custom_call" | custom-call | flops 600000000 | tf_op jit(solution)/shard_map/own_levels/pallas_call | solution.py:698
  62.0 0.3 collective-permute-done.5.x
  62.3 0.9 %other_levels.1 = (f32[16,2,32,256]{3,2,1,0:T(8,128)}, f32[16,2,16,128]{3,2,1,0:T(8,128)}) custom-call(f32[16,2,32,128]{3,2,1,0:T(8,128)S(1)} %collective-permute-done.5.x, f32[16,2,32,256]{3,2,1,0:T(8,128)} %get-tuple-element.68.mid_in, f32[16,2,16,128]{3,2,1,0:T(8,128)} %get-tuple-element.69.coarse_in), custom_call_target="tpu_custom_call", output_to_operand_aliasing={{0}: (1, {}), {1}: (2, {})} | custom-call | flops 300000000 | tf_op jit(solution)/shard_map/other_levels/pallas_call | solution.py:730
  (1 shorter events, 0.0 us)
Async XLA Ops:
  0.6 6.4 %copy-start.1 = (s32[128,1024]{1,0:T(8,128)S(1)}, s32[128,1024]{1,0:T(8,128)}, u32[]{:S(2)}) copy-start(s32[128,1024]{1,0:T(8,128)} %lab.2) | copy-start | bytes 1572868
  0.6 6.4 %copy-start = (f32[3,128,1024]{2,1,0:T(8,128)S(1)}, f32[3,128,1024]{2,1,0:T(8,128)}, u32[]{:S(2)}) copy-start(f32[3,128,1024]{2,1,0:T(8,128)} %src.2) | copy-start | bytes 4718596
  1.8 7.6 %collective-permute-start = (f32[16,1024]{1,0:T(8,128)S(1)}, f32[16,1024]{1,0:T(8,128)S(1)}, u32[]{:S(2)}, u32[]{:S(2)}) collective-permute-start(f32[16,1024]{1,0:T(8,128)S(1)} %get-tuple-element.48), channel_id=1, source_target_pairs={{0,8},{16,24},{32,40},{48,56},{64,72},{80,88},{96,104},{112,120},{... | collective-permute-start | bytes 196616 | tf_op jit(solution)/shard_map/ppermute | solution.py:754
  5.1 5.6 %collective-permute-start.1 = (f32[16,1024]{1,0:T(8,128)S(1)}, f32[16,1024]{1,0:T(8,128)S(1)}, u32[]{:S(2)}, u32[]{:S(2)}) collective-permute-start(f32[16,1024]{1,0:T(8,128)S(1)} %get-tuple-element.49), channel_id=1, source_target_pairs={{8,16},{24,32},{40,48},{56,64},{72,80},{88,96},{104,112},{120,128}... | collective-permute-start | bytes 196616 | tf_op jit(solution)/shard_map/ppermute | solution.py:753
  10.8 2.6 %collective-permute-start.2 = (f32[24,128]{1,0:T(8,128)S(1)}, f32[24,128]{1,0:T(8,128)S(1)}, u32[]{:S(2)}, u32[]{:S(2)}) collective-permute-start(f32[24,128]{1,0:T(8,128)S(1)} %get-tuple-element.59), channel_id=1, source_target_pairs={{0,1},{2,3},{4,5},{6,7},{1,0},{3,2},{5,4},{7,6},{8,9},{10,11},{12,... | collective-permute-start | bytes 36872 | tf_op jit(solution)/shard_map/ppermute | solution.py:754
  10.8 2.5 %collective-permute-start.3 = (f32[24,128]{1,0:T(8,128)S(1)}, f32[24,128]{1,0:T(8,128)S(1)}, u32[]{:S(2)}, u32[]{:S(2)}) collective-permute-start(f32[24,128]{1,0:T(8,128)S(1)} %get-tuple-element.60), channel_id=1, source_target_pairs={{1,2},{3,4},{5,6},{2,1},{4,3},{6,5},{9,10},{11,12},{13,14},{10,9},... | collective-permute-start | bytes 36872 | tf_op jit(solution)/shard_map/ppermute | solution.py:753
  14.1 1.3 %collective-permute-start.4 = (f32[8,128]{1,0:T(8,128)S(1)}, f32[8,128]{1,0:T(8,128)S(1)}, u32[]{:S(2)}, u32[]{:S(2)}) collective-permute-start(f32[8,128]{1,0:T(8,128)S(1)} %get-tuple-element.61.own), channel_id=1, source_target_pairs={{0,8},{8,0},{1,9},{9,1},{2,10},{10,2},{3,11},{11,3},{4,12},{12,4},... | collective-permute-start | bytes 12296 | tf_op jit(solution)/shard_map/ppermute | solution.py:767
  58.1 4.1 %collective-permute-start.5 = (f32[16,2,32,128]{3,2,1,0:T(8,128)S(1)}, f32[16,2,32,128]{3,2,1,0:T(8,128)S(1)}, u32[]{:S(2)}, u32[]{:S(2)}) collective-permute-start(f32[16,2,32,128]{3,2,1,0:T(8,128)S(1)} %all_to_all.11.x), channel_id=1, source_target_pairs={{0,8},{8,0},{1,9},{9,1},{2,10},{10,2},{3,11},{11,3},{4,12},{12,4},... | collective-permute-start | bytes 1572872 | tf_op jit(solution)/shard_map/ppermute | solution.py:771

commit v10 on v9

--- a/solution.py
+++ b/solution.py
@@ -762,9 +762,10 @@
     ext, lext, left, right, v0, v1, v2, totals, base = load(planes, marks)
     c_even, c_odd = exchange(*pack_columns(r_even, r_odd, left, right), "col")
     v0, v1, v2, base, totals = inner(ext, lext, v0, v1, v2, base, r_even, r_odd, totals)
-    pooled, totals = lax.optimization_barrier((pool(v0, v1, v2), totals))
     w, sums = seam(base, totals, c_even, c_odd)
-    sums = merge(sums, lax.ppermute(sums, "row_2", [(0, 1), (1, 0)]))
+    swapped = lax.ppermute(sums, "row_2", [(0, 1), (1, 0)])
+    pooled, sums = lax.optimization_barrier((pool(v0, v1, v2), sums))
+    sums = merge(sums, swapped)
     sums = lax.all_to_all(sums, (*CHIP, "col"), split_axis=0, concat_axis=0, tiled=True)
     coef, mid = solve(sums.reshape(128, LANES), pooled, w)
     mid = lax.all_to_all(mid, CHIP, split_axis=0, concat_axis=0, tiled=True)

time: 63.4 us -> 63.4 us (level)
  no operation moved by 1% of the time
where the time goes in v10:
time: 63.4 us; the launch traced here: 63.2 us
  blocking collectives  42.4 us (67%)
  starting transfers between devices  8.55 us (13%)
  Pallas kernels  8.24 us (13%)
  waiting for transfers between devices  3.2 us (5%)
  between operations  0.76 us (1%)
    all_to_all x1, blocking collectives, per_device(): lax.all_to_all(sums, (*CHIP, 'col'), split_axis=0, concat_axis=0, tiled=T...  29.9 us
    all_to_all x1, blocking collectives, per_device(): mid = lax.all_to_all(mid, CHIP, split_axis=0, concat_axis=0, tiled=True)  12.6 us
    ppermute x2, starting transfers between devices, exchange(): even = lax.ppermute(even, axis, swaps(devices, 0))  3.32 us
    ppermute x2, starting transfers between devices, exchange(): odd = lax.ppermute(odd, axis, swaps(devices, 1))  2.57 us
    ppermute x1, starting transfers between devices, per_device(): other = lax.ppermute(mid, 'row_2', [(0, 1), (1, 0)])  2.57 us
    pallas_call x1, Pallas kernels, load(): pl.pallas_call(load_kernel, out_shape=(near((K, BLOCKS, ROWS, LANES)), ne...  2.4 us
  transfers between devices with their start and end apart: 6, of which 4 were waited for; matrix products, arithmetic and copies ran while one was open for 0% of the time, Pallas kernels for 8%

profile of v10, /device:TPU:1, one launch (start us, length us, event | category | flops | bytes accessed | tf_op | source)
XLA Modules:
  0.0 63.2 jit_solution(5218445696449065603)
XLA Ops:
  0.6 0.0 copy-start.1
  0.6 0.0 copy-start
  0.7 1.2 %pack_rows.1 = (f32[16,1024]{1,0:T(8,128)S(1)}, f32[16,1024]{1,0:T(8,128)S(1)}) custom-call(f32[3,128,1024]{2,1,0:T(8,128)} %src.2, s32[128,1024]{1,0:T(8,128)} %lab.2), custom_call_target="tpu_custom_call" | custom-call | flops 300000000 | tf_op jit(solution)/shard_map/pack_rows/pallas_call | solution.py:99
  1.8 3.3 %collective-permute-start = (f32[16,1024]{1,0:T(8,128)S(1)}, f32[16,1024]{1,0:T(8,128)S(1)}, u32[]{:S(2)}, u32[]{:S(2)}) collective-permute-start(f32[16,1024]{1,0:T(8,128)S(1)} %get-tuple-element.48), channel_id=1, source_target_pairs={{0,8},{16,24},{32,40},{48,56},{64,72},{80,88},{96,104},{112,120},{... | collective-permute-start | bytes 196616 | tf_op jit(solution)/shard_map/ppermute | solution.py:754
  5.1 1.9 %collective-permute-start.1 = (f32[16,1024]{1,0:T(8,128)S(1)}, f32[16,1024]{1,0:T(8,128)S(1)}, u32[]{:S(2)}, u32[]{:S(2)}) collective-permute-start(f32[16,1024]{1,0:T(8,128)S(1)} %get-tuple-element.49), channel_id=1, source_target_pairs={{8,16},{24,32},{40,48},{56,64},{72,80},{88,96},{104,112},{120,128}... | collective-permute-start | bytes 196616 | tf_op jit(solution)/shard_map/ppermute | solution.py:753
  7.0 0.0 copy-done.1
  7.0 0.0 copy-done
  7.0 2.4 %load_block.1 = (f32[3,8,168,128]{3,2,1,0:T(8,128)S(1)}, s32[8,168,128]{2,1,0:T(8,128)S(1)}, f32[16,128]{1,0:T(8,128)S(1)}, f32[16,128]{1,0:T(8,128)S(1)}, f32[8...) custom-call(f32[3,128,1024]{2,1,0:T(8,128)S(1)} %copy-done, ...), custom_call_target="tpu_custom_call" | custom-call | flops 900000000 | tf_op jit(solution)/shard_map/load_block/pallas_call | solution.py:158
  9.5 0.0 collective-permute-done.refs_6_.got_even
  9.5 1.2 %collective-permute-done.1.refs_7_.got_odd = f32[16,1024]{1,0:T(8,128)S(1)} collective-permute-done((f32[16,1024]{1,0:T(8,128)S(1)}, f32[16,1024]{1,0:T(8,128)S(1)}, u32[]{:S(2)}, u32[]{:S(2)}) %collective-permute-start.1) | collective-permute-done | bytes 65568 | tf_op jit(solution)/shard_map/ppermute | solution.py:753
  10.7 0.1 pack_columns.1
  10.8 0.0 collective-permute-start.2
  10.8 0.7 %collective-permute-start.3 = (f32[24,128]{1,0:T(8,128)S(1)}, f32[24,128]{1,0:T(8,128)S(1)}, u32[]{:S(2)}, u32[]{:S(2)}) collective-permute-start(f32[24,128]{1,0:T(8,128)S(1)} %get-tuple-element.59), channel_id=1, source_target_pairs={{1,2},{3,4},{5,6},{2,1},{4,3},{6,5},{9,10},{11,12},{13,14},{10,9},... | collective-permute-start | bytes 36872 | tf_op jit(solution)/shard_map/ppermute | solution.py:753
  11.5 0.9 %inner_fields.1 = (f32[3,8,168,128]{3,2,1,0:T(8,128)S(1)}, s32[8,168,128]{2,1,0:T(8,128)S(1)}, f32[8,168,128]{2,1,0:T(8,128)S(1)}, f32[8,168,128]{2,1,0:T(8,128)...) custom-call(f32[3,8,168,128]{3,2,1,0:T(8,128)S(1)} %get-tuple-elemen, ...), custom_call_target="tpu_custom_call", output_to_operand_aliasing={{0}: (0, {}), {1}: (1, {}), {2}: (2, {}), {3}: (3, {}), {4}... | custom-call | flops 600000000 | tf_op jit(solution)/shard_map/inner_fields/pallas_call | solution.py:351
  12.3 1.0 %collective-permute-done.2.c_even = f32[24,128]{1,0:T(8,128)S(1)} collective-permute-done((f32[24,128]{1,0:T(8,128)S(1)}, f32[24,128]{1,0:T(8,128)S(1)}, u32[]{:S(2)}, u32[]{:S(2)}) %collective-permute-start.2) | collective-permute-done | bytes 12320 | tf_op jit(solution)/shard_map/ppermute | solution.py:754
  13.3 0.0 collective-permute-done.3.c_odd
  13.3 0.8 %seam_fields.1 = (f32[3,168,128]{2,1,0:T(8,128)S(1)}, f32[8,128]{1,0:T(8,128)S(1)}) custom-call(f32[4,168,128]{2,1,0:T(8,128)S(1)} %get-tuple-element.54.base, f32[6,8,128]{2,1,0:T(8,128)S(1)} %get-tuple-element.55.totals_in, f32[24,128]{1,0:T(8,128)S(1)} %collective-permute-done.2.c_even, f32[24,128]{1,0:T(8,128)S(1)} %collective-permute-done.3.c_odd), custom_call_target="tpu_custom_call" | custom-call | flops 300000000 | tf_op jit(solution)/shard_map/seam_fields/pallas_call | solution.py:445
  14.1 0.1 collective-permute-start.4
  14.2 0.5 pool_fields.1.pooled
  14.7 0.7 %collective-permute-done.4.other = f32[8,128]{1,0:T(8,128)S(1)} collective-permute-done((f32[8,128]{1,0:T(8,128)S(1)}, f32[8,128]{1,0:T(8,128)S(1)}, u32[]{:S(2)}, u32[]{:S(2)}) %collective-permute-start.4) | collective-permute-done | bytes 4128 | tf_op jit(solution)/shard_map/ppermute | solution.py:766
  15.4 29.9 %all_to_all.10 = f32[128,1,128]{2,1,0:T(1,128)S(1)} all-to-all(f32[128,1,128]{2,1,0:T(1,128)S(1)} %merge_cores.1), channel_id=1, replica_groups=mesh['row_0'=4,'row_1'=4,'row_2'=2,'col'=8] {'row_0','row_1','col'}, dimensions={0} | all-to-all | bytes 131072 | tf_op jit(solution)/shard_map/all_to_all | solution.py:769
  45.3 0.3 coefficients.1
  45.6 12.6 %all_to_all.11.x = f32[16,2,32,128]{3,2,1,0:T(8,128)S(1)} all-to-all(f32[16,2,32,128]{3,2,1,0:T(8,128)S(1)} %get-tuple-element.64), channel_id=1, replica_groups=mesh['row_0'=4,'row_1'=4,'row_2'=2,'col'=8] {'row_0','row_1'}, dimensions={0} | all-to-all | bytes 1048576 | tf_op jit(solution)/shard_map/all_to_all | solution.py:771
  58.1 2.6 %collective-permute-start.5 = (f32[16,2,32,128]{3,2,1,0:T(8,128)S(1)}, f32[16,2,32,128]{3,2,1,0:T(8,128)S(1)}, u32[]{:S(2)}, u32[]{:S(2)}) collective-permute-start(f32[16,2,32,128]{3,2,1,0:T(8,128)S(1)} %all_to_all.11.x), channel_id=1, source_target_pairs={{0,8},{8,0},{1,9},{9,1},{2,10},{10,2},{3,11},{11,3},{4,12},{12,4},... | collective-permute-start | bytes 1572872 | tf_op jit(solution)/shard_map/ppermute | solution.py:772
  60.7 1.2 %own_levels.1 = (f32[128,1024]{1,0:T(8,128)}, f32[64,512]{1,0:T(8,128)}, f32[16,2,32,256]{3,2,1,0:T(8,128)}, f32[16,2,16,128]{3,2,1,0:T(8,128)}) custom-call(f32[16,2,32,128]{3,2,1,0:T(8,128)S(1)} %all_to_all.11.x, f32[3,8,128]{2,1,0:T(8,128)S(1)} %get-tuple-element.65.coef, f32[8,168,128]{2,1,0:T(8,128)S(1)} %get-tuple-element.51.v0, ...), custom_call_target="tpu_custom_call" | custom-call | flops 600000000 | tf_op jit(solution)/shard_map/own_levels/pallas_call | solution.py:698
  62.0 0.3 collective-permute-done.5.x
  62.3 0.9 %other_levels.1 = (f32[16,2,32,256]{3,2,1,0:T(8,128)}, f32[16,2,16,128]{3,2,1,0:T(8,128)}) custom-call(f32[16,2,32,128]{3,2,1,0:T(8,128)S(1)} %collective-permute-done.5.x, f32[16,2,32,256]{3,2,1,0:T(8,128)} %get-tuple-element.68.mid_in, f32[16,2,16,128]{3,2,1,0:T(8,128)} %get-tuple-element.69.coarse_in), custom_call_target="tpu_custom_call", output_to_operand_aliasing={{0}: (1, {}), {1}: (2, {})} | custom-call | flops 300000000 | tf_op jit(solution)/shard_map/other_levels/pallas_call | solution.py:730
  (1 shorter events, 0.0 us)
Async XLA Ops:
  0.6 6.4 %copy-start.1 = (s32[128,1024]{1,0:T(8,128)S(1)}, s32[128,1024]{1,0:T(8,128)}, u32[]{:S(2)}) copy-start(s32[128,1024]{1,0:T(8,128)} %lab.2) | copy-start | bytes 1572868
  0.6 6.4 %copy-start = (f32[3,128,1024]{2,1,0:T(8,128)S(1)}, f32[3,128,1024]{2,1,0:T(8,128)}, u32[]{:S(2)}) copy-start(f32[3,128,1024]{2,1,0:T(8,128)} %src.2) | copy-start | bytes 4718596
  1.8 7.6 %collective-permute-start = (f32[16,1024]{1,0:T(8,128)S(1)}, f32[16,1024]{1,0:T(8,128)S(1)}, u32[]{:S(2)}, u32[]{:S(2)}) collective-permute-start(f32[16,1024]{1,0:T(8,128)S(1)} %get-tuple-element.48), channel_id=1, source_target_pairs={{0,8},{16,24},{32,40},{48,56},{64,72},{80,88},{96,104},{112,120},{... | collective-permute-start | bytes 196616 | tf_op jit(solution)/shard_map/ppermute | solution.py:754
  5.1 5.6 %collective-permute-start.1 = (f32[16,1024]{1,0:T(8,128)S(1)}, f32[16,1024]{1,0:T(8,128)S(1)}, u32[]{:S(2)}, u32[]{:S(2)}) collective-permute-start(f32[16,1024]{1,0:T(8,128)S(1)} %get-tuple-element.49), channel_id=1, source_target_pairs={{8,16},{24,32},{40,48},{56,64},{72,80},{88,96},{104,112},{120,128}... | collective-permute-start | bytes 196616 | tf_op jit(solution)/shard_map/ppermute | solution.py:753
  10.8 2.6 %collective-permute-start.2 = (f32[24,128]{1,0:T(8,128)S(1)}, f32[24,128]{1,0:T(8,128)S(1)}, u32[]{:S(2)}, u32[]{:S(2)}) collective-permute-start(f32[24,128]{1,0:T(8,128)S(1)} %get-tuple-element.58), channel_id=1, source_target_pairs={{0,1},{2,3},{4,5},{6,7},{1,0},{3,2},{5,4},{7,6},{8,9},{10,11},{12,... | collective-permute-start | bytes 36872 | tf_op jit(solution)/shard_map/ppermute | solution.py:754
  10.8 2.5 %collective-permute-start.3 = (f32[24,128]{1,0:T(8,128)S(1)}, f32[24,128]{1,0:T(8,128)S(1)}, u32[]{:S(2)}, u32[]{:S(2)}) collective-permute-start(f32[24,128]{1,0:T(8,128)S(1)} %get-tuple-element.59), channel_id=1, source_target_pairs={{1,2},{3,4},{5,6},{2,1},{4,3},{6,5},{9,10},{11,12},{13,14},{10,9},... | collective-permute-start | bytes 36872 | tf_op jit(solution)/shard_map/ppermute | solution.py:753
  14.1 1.3 %collective-permute-start.4 = (f32[8,128]{1,0:T(8,128)S(1)}, f32[8,128]{1,0:T(8,128)S(1)}, u32[]{:S(2)}, u32[]{:S(2)}) collective-permute-start(f32[8,128]{1,0:T(8,128)S(1)} %get-tuple-element.61.own), channel_id=1, source_target_pairs={{0,8},{8,0},{1,9},{9,1},{2,10},{10,2},{3,11},{11,3},{4,12},{12,4},... | collective-permute-start | bytes 12296 | tf_op jit(solution)/shard_map/ppermute | solution.py:766
  58.1 4.1 %collective-permute-start.5 = (f32[16,2,32,128]{3,2,1,0:T(8,128)S(1)}, f32[16,2,32,128]{3,2,1,0:T(8,128)S(1)}, u32[]{:S(2)}, u32[]{:S(2)}) collective-permute-start(f32[16,2,32,128]{3,2,1,0:T(8,128)S(1)} %all_to_all.11.x), channel_id=1, source_target_pairs={{0,8},{8,0},{1,9},{9,1},{2,10},{10,2},{3,11},{11,3},{4,12},{12,4},... | collective-permute-start | bytes 1572872 | tf_op jit(solution)/shard_map/ppermute | solution.py:772
